TPU v7x, 256 devices: a whole 4x4x8 slice. The times are simulated.
256 devices in a mesh: row: 32 (over x, z_lo, core), chan: 8 (over y, z_hi).
Axes of the slice: x: 4, y: 4, z: 8 (z_hi: 2, z_lo: 4; z = z_hi * 4 + z_lo), core: 2. Of those that a mesh axis runs over, the one named last changes fastest.
Arguments:
- pair: bfloat16 [128, 768, 768], P('chan', 'row'), may hold values from -24 to 24
- single: bfloat16 [768, 384], P('row'), may hold values from -6 to 6
- token_mask: int32 [768], replicated, may hold values from 0 to 1, as said below
- pair_gain: float32 [128], replicated, may hold values from 0.5 to 1.5
- w_ab: bfloat16 [128, 4, 128], replicated, may hold values from -0.5 to 0.5
- w_out_gate: bfloat16 [128, 128], replicated, may hold values from -0.5 to 0.5
- x_gain: float32 [128], replicated, may hold values from 0.5 to 1.5
- w_tri_out: bfloat16 [128, 128], replicated, may hold values from -0.5 to 0.5
- bias_gain: float32 [128], replicated, may hold values from 0.5 to 1.5
- w_bias: bfloat16 [128, 16], replicated, may hold values from -0.5 to 0.5
- single_gain: float32 [384], replicated, may hold values from 0.5 to 1.5
- w_query: bfloat16 [384, 384], P(None, 'chan'), may hold values from -1 to 1
- w_key: bfloat16 [384, 384], P(None, 'chan'), may hold values from -16 to 16
- w_value_gate: bfloat16 [384, 2, 384], P(None, None, 'chan'), may hold values from -0.3125 to 0.3125
- w_mix: bfloat16 [384, 384], P('chan'), may hold values from -0.3125 to 0.3125
Outputs:
- pair_out: bfloat16 [128, 768, 768], P('chan', 'row')
- attended: bfloat16 [768, 384], P('row', 'chan')
Inputs may be any that keep to these rules, and one draw needn't show every extreme that they name: token_mask is 1 on the first tokens and 0 on the rest; at least 672 tokens are real.
All inputs are finite; a program needn't handle non-finite values.
Results may differ from a plain program's by a relative error of at most 0.015.
The roundings to bfloat16 on the way count: a program that leaves them out, or rounds other values in their place, can miss the bound.
Values may be sent and summed in bfloat16 or wider, within the bound.
No kernel may reach another device: no remote copies, remote signals or barrier semaphores. Data moves between devices by JAX's collectives and lax.ppermute only.
A program may use at most 64 MiB of HBM per device.

v0:
```python
import jax
import jax.numpy as jnp
from jax import lax
from jax.sharding import Mesh
from jax.sharding import PartitionSpec as P

D = 384
H = 16
CHAN = ("chan_0", "chan_1")


EPS = 1e-05


def gathered_by_axis(shard, axes, dim):
    for axis in reversed(axes):
        shard = lax.all_gather(shard, axis, axis=dim, tiled=True)
    return shard


def sent_together(arrays, axis, dim, along):
    widths = [a.shape[along] for a in arrays]
    both = jnp.concatenate(arrays, axis=along)
    whole = lax.all_gather(both, axis, axis=dim, tiled=True)
    return tuple(jnp.split(whole, [sum(widths[:k]) for k in range(1, len(widths))], axis=along))


def cut_along(shard, dim, peers):
    before, after = (shard.shape[:dim], shard.shape[dim + 1 :])
    return jnp.moveaxis(shard.reshape(*before, peers, -1, *after), dim, 0)


def sent_and_summed(shard, axis, dim):
    peers = lax.axis_size(axis)
    blocks = lax.all_to_all(cut_along(shard, dim, peers), axis, 0, 0, tiled=True)
    return jnp.sum(blocks.astype(jnp.float32), axis=0)


def layer_norm(values, gain, axis):
    middle = jnp.mean(values, axis=axis, keepdims=True)
    centred = values - middle
    spread = jnp.mean(centred * centred, axis=axis, keepdims=True)
    return centred * lax.rsqrt(spread + EPS) * gain


def body(
    pair,
    single,
    token_mask,
    pair_gain,
    w_ab,
    w_out_gate,
    x_gain,
    w_tri_out,
    bias_gain,
    w_bias,
    single_gain,
    w_query,
    w_key,
    w_value_gate,
    w_mix,
):
    chans = pair.shape[0]
    rows = pair.shape[1]
    width = pair.shape[2]
    ranks = lax.axis_size("row")
    chan_start = lax.axis_index(CHAN) * chans
    row_start = lax.axis_index("row") * rows
    live = token_mask.astype(jnp.float32)
    live_rows = lax.dynamic_slice_in_dim(live, row_start, rows, 0)
    pair_mask = live_rows[:, None] * live[None, :]
    full = gathered_by_axis(pair, CHAN, 0)
    normed = layer_norm(full.astype(jnp.float32), pair_gain[:, None, None], 0).astype(jnp.bfloat16)
    w_own = lax.dynamic_slice_in_dim(w_ab, chan_start, chans, 2)
    share = max(1, ranks // chans)
    per_owner = max(1, chans // ranks)
    groups = chans // per_owner
    part_rows = rows // share
    projected = jnp.einsum("cik,cpd->pdik", normed, w_own, preferred_element_type=jnp.float32)
    left = (jax.nn.sigmoid(projected[0]) * projected[1] * pair_mask[None]).astype(jnp.bfloat16)
    right = (jax.nn.sigmoid(projected[2]) * projected[3] * pair_mask[None]).astype(jnp.bfloat16)
    left_send = left.reshape(groups, per_owner, share, part_rows, width).transpose(0, 2, 1, 3, 4)
    left_send = left_send.reshape(ranks * per_owner, part_rows, width)
    right_send = jnp.broadcast_to(
        right.reshape(groups, 1, per_owner, rows, width), (groups, share, per_owner, rows, width)
    )
    right_send = right_send.reshape(ranks * per_owner, rows, width)
    left_owned, right_owned = (
        lax.all_to_all(left_send, "row", split_axis=0, concat_axis=1, tiled=True),
        lax.all_to_all(right_send, "row", split_axis=0, concat_axis=1, tiled=True),
    )
    owned = jnp.einsum(
        "uik,ujk->uij", left_owned, right_owned, preferred_element_type=jnp.float32
    ).astype(jnp.bfloat16)
    returned = lax.all_to_all(owned, "row", split_axis=1, concat_axis=0, tiled=True)
    summed = (
        returned.reshape(groups, share, per_owner, part_rows, width)
        .transpose(0, 2, 1, 3, 4)
        .reshape(chans, rows, width)
    )
    crossed = lax.all_gather(summed, CHAN, axis=0, tiled=True)
    product_normed = layer_norm(crossed.astype(jnp.float32), x_gain[:, None, None], 0).astype(
        jnp.bfloat16
    )
    out_gate = jax.nn.sigmoid(
        jnp.einsum("cij,cd->dij", normed, w_out_gate, preferred_element_type=jnp.float32)
    )
    update = jnp.einsum(
        "cij,cd->dij", product_normed, w_tri_out, preferred_element_type=jnp.float32
    )
    renewed = (full.astype(jnp.float32) + out_gate * update).astype(jnp.bfloat16)
    pair_out = lax.dynamic_slice_in_dim(renewed, chan_start, chans, 0)
    head_size = D // H
    local_width = w_query.shape[1]
    heads = local_width // head_size
    head_start = lax.axis_index(CHAN) * heads
    bias_input = layer_norm(renewed.astype(jnp.float32), bias_gain[:, None, None], 0).astype(
        jnp.bfloat16
    )
    w_bias_own = lax.dynamic_slice_in_dim(w_bias, head_start, heads, 1)
    bias = jnp.einsum("cij,ch->hij", bias_input, w_bias_own, preferred_element_type=jnp.float32)
    single_normed = layer_norm(single.astype(jnp.float32), single_gain[None, :], 1).astype(
        jnp.bfloat16
    )
    queries = jnp.dot(single_normed, w_query, preferred_element_type=jnp.float32).astype(
        jnp.bfloat16
    )
    head_gate = jax.nn.sigmoid(
        jnp.dot(single_normed, w_value_gate[:, 1, :], preferred_element_type=jnp.float32)
    )
    own_keys = jnp.dot(single_normed, w_key, preferred_element_type=jnp.float32).astype(
        jnp.bfloat16
    )
    own_values = jnp.dot(
        single_normed, w_value_gate[:, 0, :], preferred_element_type=jnp.float32
    ).astype(jnp.bfloat16)
    keys, values = sent_together((own_keys, own_values), "row", 0, 1)
    tokens = keys.shape[0]
    query_heads = queries.reshape(rows, heads, head_size)
    key_heads = keys.reshape(tokens, heads, head_size)
    value_heads = values.reshape(tokens, heads, head_size)
    scores = jnp.einsum("ihe,jhe->hij", query_heads, key_heads, preferred_element_type=jnp.float32)
    scores = scores / jnp.sqrt(jnp.float32(head_size)) + bias
    scores = jnp.where(live[None, None, :] > 0, scores, -jnp.inf)
    top = jnp.max(scores, axis=2, keepdims=True)
    raised = jnp.exp(scores - top)
    weights = (raised / jnp.sum(raised, axis=2, keepdims=True)).astype(jnp.bfloat16)
    mixed = jnp.einsum("hij,jhe->ihe", weights, value_heads, preferred_element_type=jnp.float32)
    heads_out = (mixed.reshape(rows, local_width) * head_gate).astype(jnp.bfloat16)
    terms = jnp.dot(heads_out, w_mix, preferred_element_type=jnp.float32)
    attended = sent_and_summed(terms.astype(jnp.bfloat16), CHAN, 1).astype(jnp.bfloat16)
    return (pair_out, attended)


def solution(mesh):
    split = Mesh(mesh.devices.reshape(mesh.shape["row"], 4, 2), ("row", "chan_0", "chan_1"))
    return jax.shard_map(
        body,
        mesh=split,
        in_specs=(
            P(CHAN, "row", None),
            P("row", None),
            P(),
            P(),
            P(),
            P(),
            P(),
            P(),
            P(),
            P(),
            P(),
            P(None, CHAN),
            P(None, CHAN),
            P(None, None, CHAN),
            P(CHAN, None),
        ),
        out_specs=(P(CHAN, "row", None), P("row", CHAN)),
        check_vma=False,
    )
```

profile of v0, /device:TPU:32, one launch (start us, length us, event | category | flops | bytes accessed | tf_op | source)
XLA Modules:
  0.0 370.3 jit_solution(35078988886564830)
XLA Ops:
  7.2 2.0 copy.73
  9.3 47.5 %all-gather.4.cloned.1.call-done = bf16[32,24,768]{2,0,1:T(8,128)(2,1)} async-done(((bf16[16,24,768]{2,0,1:T(8,128)(2,1)}), bf16[32,24,768]{2,0,1:T(8,128)(2,1)}) %all-gather.4.cloned.1.call-update) | async-done | bytes 1179664 | tf_op jit(solution)/shard_map/all_gather | solution.py:17
  56.9 0.1 constant_dynamic-slice_fusion.2
  57.0 0.1 copy.95
  57.1 0.7 convert_element_type.70
  58.0 0.1 mul.157
  58.2 52.7 %all-gather.6.cloned.1.call-done = bf16[128,24,768]{2,0,1:T(8,128)(2,1)} async-done(((bf16[32,24,768]{2,0,1:T(8,128)(2,1)}), bf16[128,24,768]{2,0,1:T(8,128)(2,1)}) %all-gather.6.cloned.1.call-update) | async-done | bytes 4718608 | tf_op jit(solution)/shard_map/all_gather | solution.py:17
  110.9 3.2 convert_reduce_fusion
  114.2 0.5 copy-done.1
  114.7 1.4 fusion.7
  116.1 1.9 fusion.17
  118.0 2.2 copy-done.3
  120.2 0.3 slice_multiply_fusion.1
  120.5 1.7 copy.76
  122.2 1.4 reshape.164
  123.6 1.1 multiply_convert_fusion
  124.7 7.8 %all-to-all-start = ((bf16[32,12,768]{2,1,0:T(8,128)(2,1)}), bf16[32,12,768]{2,1,0:T(8,128)(2,1)S(1)}, u32[]{:S(2)}, u32[]{:S(2)}) async-start(bf16[32,12,768]{2,1,0:T(8,128)(2,1)} %multiply_convert_fusion), calls=%async_computation | async-start | bytes 1572864 | tf_op jit(solution)/shard_map/all_to_all | solution.py:89
  132.5 2.0 fusion.26
  134.5 0.2 copy.78
  134.7 18.0 %all-to-all-done = bf16[32,12,768]{2,1,0:T(8,128)(2,1)S(1)} async-done(((bf16[32,12,768]{2,1,0:T(8,128)(2,1)}), bf16[32,12,768]{2,1,0:T(8,128)(2,1)S(1)}, u32[]{:S(2)}, u32[]{:S(2)}) %all-to-all-start) | async-done | bytes 589856 | tf_op jit(solution)/shard_map/all_to_all | solution.py:89
  152.7 1.1 broadcast_in_dim.12
  153.8 5.9 %all-to-all-start.1 = ((bf16[32,24,768]{2,1,0:T(8,128)(2,1)}), bf16[32,24,768]{2,1,0:T(8,128)(2,1)S(1)}, u32[]{:S(2)}, u32[]{:S(2)}) async-start(bf16[32,24,768]{2,1,0:T(8,128)(2,1)} %bitcast.5), calls=%async_computation.1 | async-start | bytes 2359296 | tf_op jit(solution)/shard_map/all_to_all | solution.py:90
  159.7 0.2 all-gather.8.cloned.1.call-start
  160.0 0.1 reshape.157
  160.1 27.8 %all-to-all-done.1 = bf16[32,24,768]{2,1,0:T(8,128)(2,1)S(1)} async-done(((bf16[32,24,768]{2,1,0:T(8,128)(2,1)}), bf16[32,24,768]{2,1,0:T(8,128)(2,1)S(1)}, u32[]{:S(2)}, u32[]{:S(2)}) %all-to-all-start.1) | async-done | bytes 1179680 | tf_op jit(solution)/shard_map/all_to_all | solution.py:90
  187.9 0.7 fusion.23
  188.6 0.9 copy.105
  189.5 0.5 broadcast.172
  190.0 4.2 %reduce.1 = bf16[384,768]{1,0:T(8,128)(2,1)S(1)} reduce(bf16[384,1,768]{2,1,0:T(2,128)(2,1)S(1)} %bitcast.64, bf16[]{:T(256)} %broadcast.172), dimensions={1}, to_apply=%bitcast.61.reduce_sub_computation | reduce | bytes 1179650
  194.3 0.2 reshape.171
  194.5 22.5 %all_to_all.32 = bf16[32,2,4608]{2,1,0:T(2,128)(2,1)S(1)} all-to-all(bf16[32,2,4608]{2,1,0:T(2,128)(2,1)S(1)} %reshape.171), channel_id=1, replica_groups=mesh['row'=32,'chan_0'=4,'chan_1'=2] {'row'}, dimensions={0} | all-to-all | bytes 1179648 | tf_op jit(solution)/shard_map/all_to_all | solution.py:95
  217.0 0.5 reshape.172
  217.4 0.9 copy.94
  218.4 0.1 convert_reduce_fusion.3
  218.5 0.2 fusion.47
  218.7 0.2 convolution_convert_fusion.3
  218.9 0.2 convolution_convert_fusion.4
  219.1 0.1 pad_maximum_fusion
  219.2 41.5 %all_gather.15 = bf16[768,96]{1,0:T(8,128)(2,1)S(1)} all-gather(bf16[24,96]{1,0:T(8,128)(2,1)S(1)} %pad_maximum_fusion), channel_id=1, replica_groups=mesh['row'=32,'chan_0'=4,'chan_1'=2] {'row'}, dimensions={0}, use_global_device_ids=true | all-gather | bytes 152064 | tf_op jit(solution)/shard_map/all_gather | solution.py:24
  260.7 0.1 fusion.70
  260.8 0.1 copy.83
  261.0 0.2 convolution_convert_fusion.2
  261.3 0.1 copy.82
  261.4 69.3 %all-gather.8.cloned.1.call-done = bf16[128,24,768]{2,1,0:T(8,128)(2,1)} async-done(((bf16[16,24,768]{2,1,0:T(8,128)(2,1)}), bf16[128,24,768]{2,1,0:T(8,128)(2,1)}) %all-gather.8.cloned.1.call-update) | async-done | bytes 4718608 | tf_op jit(solution)/shard_map/all_gather | solution.py:101
  330.8 3.2 convert_reduce_fusion.2
  334.0 0.6 copy-done.2
  334.5 1.3 fusion.13
  335.9 1.4 fusion.15
  337.3 1.4 fusion.19
  338.8 5.2 %convert_reduce_fusion.1 = (f32[24,768]{1,0:T(8,128)S(1)}, bf16[128,24,768]{2,0,1:T(8,128)(2,1)S(1)}) fusion(f32[24,768,128]{1,2,0:T(8,128)S(1)} %fusion.19, bf16[128,128]{1,0:T(8,128)(2,1)S(1)} %copy-done.14, bf16[128,24,768]{2,0,1:T(8,128)(2,1)S(1)} %bitcast.63, f32[128]{0:T(128)S(1)} %copy-done.9, f32[24,768]{1,0:T(8,128)S(1)} %add_rsqrt_fusion.2, ...), kind=kOutput, calls=%fused_computation.5 | convolution fusion | flops 636991488 | bytes 19128832 | tf_op jit(solution)/shard_map/cij,cd->dij/dot_general | solution.py:106
  344.1 1.3 fusion.10
  345.5 2.3 fusion.21
  347.8 0.2 fusion.36
  347.9 0.2 fusion.71
  348.1 0.2 fusion.44
  348.4 0.4 convolution_convert_fusion.1
  348.8 0.1 reshape.163
  348.9 0.7 reshape.173
  349.6 3.3 all-to-all-start.3
  352.9 1.1 constant_dynamic-slice_fusion.1
  354.1 1.0 copy.88
  355.1 7.9 %all-to-all-done.3 = bf16[8,2,576]{2,1,0:T(2,128)(2,1)S(1)} async-done(((bf16[8,2,576]{2,1,0:T(2,128)(2,1)}), bf16[8,2,576]{2,1,0:T(2,128)(2,1)S(1)}, u32[]{:S(2)}, u32[]{:S(2)}) %all-to-all-start.3) | async-done | bytes 18464 | tf_op jit(solution)/shard_map/all_to_all | solution.py:35
  363.0 0.1 reshape.174
  363.1 0.6 reduce_sum.102
  (56 shorter events, 0.7 us)
Async XLA Ops:
  7.2 49.7 %copy-start = (bf16[128,4,128]{2,1,0:T(4,128)(2,1)S(1)}, bf16[128,4,128]{2,1,0:T(4,128)(2,1)}, u32[]{:S(2)}) copy-start(bf16[128,4,128]{2,1,0:T(4,128)(2,1)} %param.19) | copy-start | bytes 393220
  7.2 49.7 %all-gather.4.cloned.1.call-start = ((), (), s32[]{:S(2)}) async-start(), calls=%async_computation.4 | async-start | bytes 1769472 | tf_op jit(solution)/shard_map/all_gather | solution.py:17
  9.3 101.7 %all-gather.6.cloned.1.call-start = ((), (), s32[]{:S(2)}) async-start(), calls=%async_computation.5 | async-start | bytes 5898240 | tf_op jit(solution)/shard_map/all_gather | solution.py:17
  58.2 57.9 %copy-start.9 = (f32[128]{0:T(128)S(1)}, f32[128]{0:T(128)}, u32[]{:S(2)}) copy-start(f32[128]{0:T(128)} %param.18) | copy-start | bytes 1540
  110.9 3.8 %copy-start.1 = (bf16[128,24,768]{2,0,1:T(8,128)(2,1)S(1)}, bf16[128,24,768]{2,0,1:T(8,128)(2,1)}, u32[]{:S(2)}) copy-start(bf16[128,24,768]{2,0,1:T(8,128)(2,1)} %all-gather.6.cloned.1.call-done) | copy-start | bytes 14155780
  118.0 2.2 copy-start.3
  124.7 28.0 %all-to-all-start = ((bf16[32,12,768]{2,1,0:T(8,128)(2,1)}), bf16[32,12,768]{2,1,0:T(8,128)(2,1)S(1)}, u32[]{:S(2)}, u32[]{:S(2)}) async-start(bf16[32,12,768]{2,1,0:T(8,128)(2,1)} %multiply_convert_fusion), calls=%async_computation | async-start | bytes 1572864 | tf_op jit(solution)/shard_map/all_to_all | solution.py:89
  153.8 34.1 %all-to-all-start.1 = ((bf16[32,24,768]{2,1,0:T(8,128)(2,1)}), bf16[32,24,768]{2,1,0:T(8,128)(2,1)S(1)}, u32[]{:S(2)}, u32[]{:S(2)}) async-start(bf16[32,24,768]{2,1,0:T(8,128)(2,1)} %bitcast.5), calls=%async_computation.1 | async-start | bytes 2359296 | tf_op jit(solution)/shard_map/all_to_all | solution.py:90
  159.7 171.0 %all-gather.8.cloned.1.call-start = ((), (), s32[]{:S(2)}) async-start(), calls=%async_computation.6 | async-start | bytes 5308416 | tf_op jit(solution)/shard_map/all_gather | solution.py:101
  188.6 29.8 %copy-start.5 = (bf16[24,384]{1,0:T(8,128)(2,1)S(1)}, bf16[24,384]{1,0:T(8,128)(2,1)}, u32[]{:S(2)}) copy-start(bf16[24,384]{1,0:T(8,128)(2,1)} %param.16) | copy-start | bytes 55300
  188.6 30.1 %copy-start.10 = (bf16[384,2,48]{0,2,1:T(8,128)(2,1)S(1)}, bf16[384,2,48]{0,2,1:T(8,128)(2,1)}, u32[]{:S(2)}) copy-start(bf16[384,2,48]{0,2,1:T(8,128)(2,1)} %param.28) | copy-start | bytes 221188
  188.6 30.1 %copy-start.15 = (f32[384]{0:T(512)S(1)}, f32[384]{0:T(512)}, u32[]{:S(2)}) copy-start(f32[384]{0:T(512)} %param.25) | copy-start | bytes 4612
  188.6 30.3 %copy-start.11 = (bf16[384,48]{0,1:T(8,128)(2,1)S(1)}, bf16[384,48]{0,1:T(8,128)(2,1)}, u32[]{:S(2)}) copy-start(bf16[384,48]{0,1:T(8,128)(2,1)} %param.27) | copy-start | bytes 110596
  190.0 70.9 %copy-start.12 = (bf16[384,48]{0,1:T(8,128)(2,1)S(1)}, bf16[384,48]{0,1:T(8,128)(2,1)}, u32[]{:S(2)}) copy-start(bf16[384,48]{0,1:T(8,128)(2,1)} %param.26) | copy-start | bytes 110596
  190.0 71.4 %copy-start.7 = (s32[768]{0:T(1024)S(1)}, s32[768]{0:T(1024)}, u32[]{:S(2)}) copy-start(s32[768]{0:T(1024)} %param.17) | copy-start | bytes 9220
  261.4 74.4 %copy-start.8 = (f32[128]{0:T(128)S(1)}, f32[128]{0:T(128)}, u32[]{:S(2)}) copy-start(f32[128]{0:T(128)} %param.21) | copy-start | bytes 1540
  330.8 3.8 %copy-start.2 = (bf16[128,24,768]{2,1,0:T(8,128)(2,1)S(1)}, bf16[128,24,768]{2,1,0:T(8,128)(2,1)}, u32[]{:S(2)}) copy-start(bf16[128,24,768]{2,1,0:T(8,128)(2,1)} %all-gather.8.cloned.1.call-done) | copy-start | bytes 14155780
  335.8 1.5 copy-start.6
  335.9 2.9 slice-start
  337.3 1.5 slice-start.1
  337.3 1.5 copy-start.14
  344.1 3.7 copy-start.4
  344.1 1.4 copy-start.16
  345.5 2.9 copy-start.13
  349.6 13.4 %all-to-all-start.3 = ((bf16[8,2,576]{2,1,0:T(2,128)(2,1)}), bf16[8,2,576]{2,1,0:T(2,128)(2,1)S(1)}, u32[]{:S(2)}, u32[]{:S(2)}) async-start(bf16[8,2,576]{2,1,0:T(2,128)(2,1)} %reshape.173), calls=%async_computation.3 | async-start | bytes 40960 | tf_op jit(solution)/shard_map/all_to_all | solution.py:35
Sparse Core Ops, SparseCore 0:
  10.4 46.4 all-gather.3
  58.6 52.2 all-gather.5
  218.5 112.2 all-gather.7
where the time goes:
time: 372 us; the launch traced here: 370 us
  waiting for transfers between devices  223 us (60%)
  blocking collectives  64 us (17%)
  other arithmetic  21.5 us (6%)
  starting transfers between devices  17.4 us (5%)
  local copies, waits for them, and re-layouts  17 us (5%)
  between operations  14.2 us (4%)
  matrix products  12.9 us (3%)
    all_gather x2, waiting for transfers between devices, gathered_by_axis(): shard = lax.all_gather(shard, axis, axis=dim, tiled=True)  100 us
    all_gather x1, waiting for transfers between devices, body(): crossed = lax.all_gather(summed, CHAN, axis=0, tiled=True)  69.3 us
    all_gather x1, blocking collectives, sent_together(): whole = lax.all_gather(both, axis, axis=dim, tiled=True)  41.5 us
    all_to_all x1, waiting for transfers between devices, body(): lax.all_to_all(right_send, 'row', split_axis=0, concat_axis=1, tiled=True)  27.8 us
    all_to_all x1, blocking collectives, body(): lax.all_to_all(owned, 'row', split_axis=1, concat_axis=0, tiled=True)  22.5 us
    all_to_all x1, waiting for transfers between devices, body(): lax.all_to_all(left_send, 'row', split_axis=0, concat_axis=1, tiled=True)  18 us
    unnamed x47, local copies, waits for them, and re-layouts  9.37 us
    all_to_all x1, waiting for transfers between devices, sent_and_summed(): lax.all_to_all(cut_along(shard, dim, peers), axis, 0, 0, tiled=True)  7.95 us
  transfers between devices with their start and end apart: 6, of which 6 were waited for; matrix products, arithmetic and copies ran while one was open for 2% of the time, Pallas kernels for 0%

commit v1 on v0

v1 whole, which is shorter than its diff:
```python
import jax
import jax.numpy as jnp
from jax import lax
from jax.sharding import Mesh
from jax.sharding import PartitionSpec as P

D = 384
H = 16
C = 128
EPS = 1e-05
ROW = ("x", "zl", "core")
CHAN = ("y", "zh")
OWN = ("x", "zl", "y", "zh")
BF = jnp.bfloat16
F32 = jnp.float32


def layer_norm(values, gain, axis):
    middle = jnp.mean(values, axis=axis, keepdims=True)
    centred = values - middle
    spread = jnp.mean(centred * centred, axis=axis, keepdims=True)
    return centred * lax.rsqrt(spread + EPS) * gain


def swap(shard, axes):
    return lax.all_to_all(shard, axes, 0, 0, tiled=True)


def body(
    pair,
    single,
    token_mask,
    pair_gain,
    w_ab,
    w_out_gate,
    x_gain,
    w_tri_out,
    bias_gain,
    w_bias,
    single_gain,
    w_query,
    w_key,
    w_value_gate,
    w_mix,
):
    chans, rows, width = pair.shape
    nq = C // chans
    nrow = lax.axis_size(ROW)
    part = rows // nq
    spots = part * width
    r = lax.axis_index(ROW)
    q = lax.axis_index(CHAN)
    core = lax.axis_index("core")
    live = token_mask.astype(F32)

    single_normed = layer_norm(single.astype(F32), single_gain[None, :], 1).astype(BF)
    own_keys = jnp.dot(single_normed, w_key, preferred_element_type=F32).astype(BF)
    own_values = jnp.dot(single_normed, w_value_gate[:, 0, :], preferred_element_type=F32).astype(BF)
    own_kv = jnp.concatenate([own_keys, own_values], axis=1)
    kv = swap(jnp.broadcast_to(own_kv[None], (nrow,) + own_kv.shape), ROW)
    queries = jnp.dot(single_normed, w_query, preferred_element_type=F32).astype(BF)
    head_gate = jax.nn.sigmoid(
        jnp.dot(single_normed, w_value_gate[:, 1, :], preferred_element_type=F32)
    )

    sent = pair.reshape(chans, nq, spots).transpose(1, 0, 2)
    full = swap(sent, CHAN).reshape(C, spots).astype(F32)
    normed = layer_norm(full, pair_gain[:, None], 0).astype(BF)
    live_rows = lax.dynamic_slice_in_dim(live, r * rows + q * part, part, 0)
    mask = (live_rows[:, None] * live[None, :]).reshape(1, spots)
    projected = jnp.einsum("cp,ckd->kdp", normed, w_ab, preferred_element_type=F32)
    left = (jax.nn.sigmoid(projected[0]) * projected[1] * mask).astype(BF)
    right = (jax.nn.sigmoid(projected[2]) * projected[3] * mask).astype(BF)

    edges = swap(jnp.stack([left, right], axis=1), OWN)
    left_owned = edges[:, 0].reshape(C * part, width)
    right_here = edges[:, 1].reshape(C // nq, rows, width)
    right_there = lax.ppermute(right_here, "core", [(0, 1), (1, 0)])
    first = core == 0
    right_owned = jnp.stack(
        [
            jnp.where(first, right_here, right_there),
            jnp.where(first, right_there, right_here),
        ],
        axis=1,
    ).reshape(2 * C * part, width)
    owned = lax.dot_general(
        left_owned, right_owned, (((1,), (1,)), ((), ())), preferred_element_type=F32
    ).astype(BF)
    product = swap(owned.reshape(C, part, width), OWN).reshape(C, spots)

    product_normed = layer_norm(product.astype(F32), x_gain[:, None], 0).astype(BF)
    out_gate = jax.nn.sigmoid(
        jnp.einsum("cp,cd->dp", normed, w_out_gate, preferred_element_type=F32)
    )
    update = jnp.einsum("cp,cd->dp", product_normed, w_tri_out, preferred_element_type=F32)
    renewed = (full + out_gate * update).astype(BF)
    bias_input = layer_norm(renewed.astype(F32), bias_gain[:, None], 0).astype(BF)
    bias = jnp.einsum("cp,ch->hp", bias_input, w_bias, preferred_element_type=F32)

    head_size = D // H
    local_width = w_query.shape[1]
    heads = local_width // head_size
    bias = swap(bias.reshape(nq, heads, spots), CHAN)
    bias = bias.transpose(1, 0, 2).reshape(heads, rows, width)
    pair_out = swap(renewed.reshape(nq, chans, spots), CHAN)
    pair_out = pair_out.transpose(1, 0, 2).reshape(chans, rows, width)

    keys = kv[..., :local_width].reshape(-1, heads, head_size)
    values = kv[..., local_width:].reshape(-1, heads, head_size)
    query_heads = queries.reshape(rows, heads, head_size)
    scores = jnp.einsum("ihe,jhe->hij", query_heads, keys, preferred_element_type=F32)
    scores = scores / jnp.sqrt(F32(head_size)) + bias
    scores = jnp.where(live[None, None, :] > 0, scores, -jnp.inf)
    top = jnp.max(scores, axis=2, keepdims=True)
    raised = jnp.exp(scores - top)
    weights = (raised / jnp.sum(raised, axis=2, keepdims=True)).astype(BF)
    mixed = jnp.einsum("hij,jhe->ihe", weights, values, preferred_element_type=F32)
    heads_out = (mixed.reshape(rows, local_width) * head_gate).astype(BF)
    terms = jnp.dot(heads_out, w_mix, preferred_element_type=F32).astype(BF)
    terms = swap(terms.reshape(rows, nq, -1).transpose(1, 0, 2), CHAN)
    attended = jnp.sum(terms.astype(F32), axis=0).astype(BF)
    return (pair_out, attended)


def solution(mesh):
    split = Mesh(mesh.devices.reshape(4, 4, 2, 4, 2), ROW + CHAN)
    return jax.shard_map(
        body,
        mesh=split,
        in_specs=(
            P(CHAN, ROW, None),
            P(ROW, None),
            P(),
            P(),
            P(),
            P(),
            P(),
            P(),
            P(),
            P(),
            P(),
            P(None, CHAN),
            P(None, CHAN),
            P(None, None, CHAN),
            P(CHAN, None),
        ),
        out_specs=(P(CHAN, ROW, None), P(ROW, CHAN)),
        check_vma=False,
    )
```

time: 372 us -> 190 us (0.51)
  waiting for transfers between devices: 223 us -> 75.4 us
  other arithmetic: 21.5 us -> 6.71 us
  between operations: 14.2 us -> 1.06 us
  starting transfers between devices: 17.4 us -> 29.3 us
  blocking collectives: 64 us -> 53.8 us
  matrix products: 12.9 us -> 7.07 us
    all_gather x3 -> x0, waiting for transfers between devices: 170 us -> none  [the longest x2 100 us: gathered_by_axis(): shard = lax.all_gather(shard, axis, axis=dim, tiled=True)]
    all_gather x1 -> x0, blocking collectives: 41.5 us -> none  [sent_together(): whole = lax.all_gather(both, axis, axis=dim, tiled=True)]
    all_to_all x1 -> x2, blocking collectives: 22.5 us -> 53.8 us  [swap(): return lax.all_to_all(shard, axes, 0, 0, tiled=True)]
    all_to_all x3 -> x5, waiting for transfers between devices: 53.7 us -> 74.1 us  [swap(): return lax.all_to_all(shard, axes, 0, 0, tiled=True)]
    all_to_all x3 -> x5, starting transfers between devices: 17.1 us -> 29 us  [swap(): return lax.all_to_all(shard, axes, 0, 0, tiled=True)]
    unnamed x47 -> x36, local copies, waits for them, and re-layouts: 9.37 us -> 1.34 us
    reduce_sum x3, other arithmetic: 6.52 us -> 0.58 us  [layer_norm(): middle = jnp.mean(values, axis=axis, keepdims=True)]
    dot_general x11, matrix products: 12.9 us -> 7.07 us  [the longest x1 1.53 us: body(): jnp.einsum('cp,cd->dp', normed, w_out_gate, preferred_element_type=F32)]
  transfers between devices with their start and end apart: 6 -> 6, of which waited for: 6 -> 6; matrix products, arithmetic and copies ran while one was open for 2% -> 6% of each run, Pallas kernels for 0% -> 0%
where the time goes in v1:
time: 190 us; the launch traced here: 189 us
  waiting for transfers between devices  75.4 us (40%)
  blocking collectives  53.8 us (28%)
  starting transfers between devices  29.3 us (15%)
  local copies, waits for them, and re-layouts  16 us (8%)
  matrix products  7.07 us (4%)
  other arithmetic  6.71 us (4%)
    all_to_all x5, waiting for transfers between devices, swap(): return lax.all_to_all(shard, axes, 0, 0, tiled=True)  74.1 us
    all_to_all x2, blocking collectives, swap(): return lax.all_to_all(shard, axes, 0, 0, tiled=True)  53.8 us
    all_to_all x5, starting transfers between devices, swap(): return lax.all_to_all(shard, axes, 0, 0, tiled=True)  29 us
    slice x1, local copies, waits for them, and re-layouts, body(): right_here = edges[:, 1].reshape(C // nq, rows, width)  4.9 us
  transfers between devices with their start and end apart: 6, of which 6 were waited for; matrix products, arithmetic and copies ran while one was open for 6% of the time, Pallas kernels for 0%

profile of v1, /device:TPU:32, one launch (start us, length us, event | category | flops | bytes accessed | tf_op | source)
XLA Modules:
  0.0 189.4 jit_solution(11583804023795444919)
XLA Ops:
  0.6 1.4 reshape.263
  2.1 0.9 copy.62
  3.0 10.3 %all-to-all-start = ((bf16[8,16,2304]{2,1,0:T(8,128)(2,1)}), bf16[8,16,2304]{2,1,0:T(8,128)(2,1)S(1)}, u32[]{:S(2)}, u32[]{:S(2)}) async-start(bf16[8,16,2304]{2,1,0:T(8,128)(2,1)} %bitcast.76), calls=%async_computation | async-start | bytes 1179648 | tf_op jit(solution)/shard_map/all_to_all | solution.py:26
  13.3 0.1 dynamic_slice.3
  13.5 20.8 %all-to-all-done = bf16[8,16,2304]{2,1,0:T(8,128)(2,1)S(1)} async-done(((bf16[8,16,2304]{2,1,0:T(8,128)(2,1)}), bf16[8,16,2304]{2,1,0:T(8,128)(2,1)S(1)}, u32[]{:S(2)}, u32[]{:S(2)}) %all-to-all-start) | async-done | bytes 589856 | tf_op jit(solution)/shard_map/all_to_all | solution.py:26
  34.3 0.1 convert_reduce_fusion.1
  34.5 0.2 multiply_reduce_fusion.1
  34.7 0.2 fusion.29
  34.9 0.8 copy-done.1
  35.7 0.8 convolution_bitcast_fusion
  36.5 1.1 fusion.20
  37.6 0.1 pad_maximum_fusion
  37.7 1.6 copy.38
  39.4 41.3 %all_to_all.35 = bf16[128,2,2304]{2,1,0:T(2,128)(2,1)S(1)} all-to-all(bf16[128,2,2304]{2,1,0:T(2,128)(2,1)S(1)} %copy.38), channel_id=1, replica_groups=mesh['x'=4,'zl'=4,'core'=2,'y'=4,'zh'=2] {'x','zl','y','zh'}, dimensions={0} | all-to-all | bytes 2359296 | tf_op jit(solution)/shard_map/all_to_all | solution.py:26
  80.7 4.9 %slice_reduce_fusion = (bf16[128,2304]{1,0:T(8,128)(2,1)S(1)}, bf16[128,2304]{1,0:T(8,128)(2,1)S(1)}) fusion(bf16[128,2,2304]{2,1,0:T(2,128)(2,1)S(1)} %all_to_all.35), kind=kLoop, calls=%fused_computation.20 | loop fusion | bytes 2359296 | tf_op jit(solution)/shard_map/slice | solution.py:77
  85.6 0.3 reshape_squeeze.7
  85.9 0.3 collective-permute-start
  86.2 0.1 copy-done.4
  86.3 0.1 convert_reduce_fusion.3
  86.4 0.2 fusion.51
  86.6 0.3 reshape_squeeze.6
  86.9 1.2 collective-permute-done
  88.1 0.1 select_bitcast_fusion.1
  88.2 0.1 pad_maximum_fusion.1
  88.3 0.1 copy.39
  88.4 0.7 convolution_convert_fusion
  89.1 1.1 reshape.265
  90.2 6.0 %all-to-all-start.2 = ((bf16[128,3,768]{2,1,0:T(4,128)(2,1)}), bf16[128,3,768]{2,1,0:T(4,128)(2,1)S(1)}, u32[]{:S(2)}, u32[]{:S(2)}) async-start(bf16[128,3,768]{2,1,0:T(4,128)(2,1)} %reshape.265), calls=%async_computation.2 | async-start | bytes 1572864 | tf_op jit(solution)/shard_map/all_to_all | solution.py:26
  96.3 0.2 convolution_convert_fusion.3
  96.5 0.2 convolution_convert_fusion.4
  96.7 0.1 pad_maximum_fusion.2
  96.8 0.2 convolution_convert_fusion.2
  97.0 1.5 fusion.3
  98.5 24.0 %all-to-all-done.2 = bf16[128,3,768]{2,1,0:T(4,128)(2,1)S(1)} async-done(((bf16[128,3,768]{2,1,0:T(4,128)(2,1)}), bf16[128,3,768]{2,1,0:T(4,128)(2,1)S(1)}, u32[]{:S(2)}, u32[]{:S(2)}) %all-to-all-start.2) | async-done | bytes 589856 | tf_op jit(solution)/shard_map/all_to_all | solution.py:26
  122.5 0.7 broadcast_in_dim.10
  123.2 3.9 %all-to-all-start.4 = ((bf16[32,24,96]{2,1,0:T(8,128)(2,1)}), bf16[32,24,96]{2,1,0:T(8,128)(2,1)S(1)}, u32[]{:S(2)}, u32[]{:S(2)}) async-start(bf16[32,24,96]{2,1,0:T(8,128)(2,1)} %broadcast_in_dim.10), calls=%async_computation.4 | async-start | bytes 393216 | tf_op jit(solution)/shard_map/all_to_all | solution.py:26
  127.1 0.4 convert_reduce_fusion.2
  127.5 0.6 multiply_reduce_fusion
  128.1 0.5 copy.40
  128.7 1.3 fusion.26
  130.1 1.2 convert_reduce_fusion
  131.3 1.2 fusion.9
  132.6 1.4 convolution_bitcast_fusion.1
  134.0 0.7 reshape.271
  134.7 0.6 all-to-all-done.4
  135.4 5.2 %all-to-all-start.5 = ((f32[8,2,2304]{2,1,0:T(2,128)}), f32[8,2,2304]{2,1,0:T(2,128)S(1)}, u32[]{:S(2)}, u32[]{:S(2)}) async-start(f32[8,2,2304]{2,1,0:T(2,128)} %reshape.271), calls=%async_computation.5 | async-start | bytes 294912 | tf_op jit(solution)/shard_map/all_to_all | solution.py:26
  140.5 0.1 reshape.269
  140.6 0.1 fusion.69
  140.7 0.2 reshape.281
  140.9 0.2 reshape.280
  141.1 11.6 %all-to-all-done.5 = f32[8,2,2304]{2,1,0:T(2,128)S(1)} async-done(((f32[8,2,2304]{2,1,0:T(2,128)}), f32[8,2,2304]{2,1,0:T(2,128)S(1)}, u32[]{:S(2)}, u32[]{:S(2)}) %all-to-all-start.5) | async-done | bytes 147488 | tf_op jit(solution)/shard_map/all_to_all | solution.py:26
  152.8 0.2 fusion.32
  153.0 0.2 fusion.70
  153.2 0.3 fusion.45
  153.6 0.4 convolution_convert_fusion.1
  153.9 0.1 reshape.274
  154.1 0.1 reshape.284
  154.2 12.5 %all_to_all.36 = bf16[8,2,576]{2,1,0:T(2,128)(2,1)S(1)} all-to-all(bf16[8,2,576]{2,1,0:T(2,128)(2,1)S(1)} %reshape.284), channel_id=1, replica_groups=mesh['x'=4,'zl'=4,'core'=2,'y'=4,'zh'=2] {'y','zh'}, dimensions={0} | all-to-all | bytes 36864 | tf_op jit(solution)/shard_map/all_to_all | solution.py:26
  166.7 3.5 %all-to-all-start.3 = ((bf16[8,16,2304]{2,1,0:T(8,128)(2,1)}), bf16[8,16,2304]{2,1,0:T(8,128)(2,1)S(1)}, u32[]{:S(2)}, u32[]{:S(2)}) async-start(bf16[8,16,2304]{2,1,0:T(8,128)(2,1)} %bitcast.11), calls=%async_computation.3 | async-start | bytes 1179648 | tf_op jit(solution)/shard_map/all_to_all | solution.py:26
  170.2 0.1 reshape.285
  170.4 0.6 reduce_sum.102
  171.0 17.1 %all-to-all-done.3 = bf16[8,16,2304]{2,1,0:T(8,128)(2,1)S(1)} async-done(((bf16[8,16,2304]{2,1,0:T(8,128)(2,1)}), bf16[8,16,2304]{2,1,0:T(8,128)(2,1)S(1)}, u32[]{:S(2)}, u32[]{:S(2)}) %all-to-all-start.3) | async-done | bytes 589856 | tf_op jit(solution)/shard_map/all_to_all | solution.py:26
  188.1 0.2 copy.41
  188.3 1.1 reshape.267
  (50 shorter events, 0.5 us)
Async XLA Ops:
  0.6 35.1 %copy-start = (bf16[128,4,128]{2,1,0:T(4,128)(2,1)S(1)}, bf16[128,4,128]{2,1,0:T(4,128)(2,1)}, u32[]{:S(2)}) copy-start(bf16[128,4,128]{2,1,0:T(4,128)(2,1)} %param.19) | copy-start | bytes 393220
  2.1 11.3 %copy-start.6 = (s32[768]{0:T(1024)S(1)}, s32[768]{0:T(1024)}, u32[]{:S(2)}) copy-start(s32[768]{0:T(1024)} %param.17) | copy-start | bytes 9220
  3.0 31.6 %copy-start.7 = (f32[128]{0:T(128)S(1)}, f32[128]{0:T(128)}, u32[]{:S(2)}) copy-start(f32[128]{0:T(128)} %param.18) | copy-start | bytes 1540
  3.0 31.3 %all-to-all-start = ((bf16[8,16,2304]{2,1,0:T(8,128)(2,1)}), bf16[8,16,2304]{2,1,0:T(8,128)(2,1)S(1)}, u32[]{:S(2)}, u32[]{:S(2)}) async-start(bf16[8,16,2304]{2,1,0:T(8,128)(2,1)} %bitcast.76), calls=%async_computation | async-start | bytes 1179648 | tf_op jit(solution)/shard_map/all_to_all | solution.py:26
  34.9 0.8 copy-start.1
  85.6 0.7 copy-start.4
  85.9 2.3 %collective-permute-start = (bf16[16,24,768]{2,1,0:T(8,128)(2,1)S(1)}, bf16[16,24,768]{2,1,0:T(8,128)(2,1)S(1)}, u32[]{:S(2)}, u32[]{:S(2)}) collective-permute-start(bf16[16,24,768]{2,1,0:T(8,128)(2,1)S(1)} %reshape_squeeze.7), channel_id=1, source_target_pairs={{0,8},{8,0},{1,9},{9,1},{2,10},{10,2},{3,11},{11,3},{4,12},{12,4},... | collective-permute-start | bytes 1769480 | tf_op jit(solution)/shard_map/ppermute | solution.py:78
  89.1 7.2 %copy-start.9 = (bf16[384,2,48]{0,2,1:T(8,128)(2,1)S(1)}, bf16[384,2,48]{0,2,1:T(8,128)(2,1)}, u32[]{:S(2)}) copy-start(bf16[384,2,48]{0,2,1:T(8,128)(2,1)} %param.28) | copy-start | bytes 221188
  89.1 7.2 %copy-start.15 = (f32[384]{0:T(512)S(1)}, f32[384]{0:T(512)}, u32[]{:S(2)}) copy-start(f32[384]{0:T(512)} %param.25) | copy-start | bytes 4612
  90.2 6.3 %copy-start.10 = (bf16[384,48]{0,1:T(8,128)(2,1)S(1)}, bf16[384,48]{0,1:T(8,128)(2,1)}, u32[]{:S(2)}) copy-start(bf16[384,48]{0,1:T(8,128)(2,1)} %param.27) | copy-start | bytes 110596
  90.2 6.6 %copy-start.11 = (bf16[384,48]{0,1:T(8,128)(2,1)S(1)}, bf16[384,48]{0,1:T(8,128)(2,1)}, u32[]{:S(2)}) copy-start(bf16[384,48]{0,1:T(8,128)(2,1)} %param.26) | copy-start | bytes 110596
  90.2 6.8 %copy-start.2 = (bf16[128,2304]{1,0:T(8,128)(2,1)S(1)}, bf16[128,2304]{1,0:T(8,128)(2,1)}, u32[]{:S(2)}) copy-start(bf16[128,2304]{1,0:T(8,128)(2,1)} %copy-done.1) | copy-start | bytes 1769476
  90.2 6.8 %copy-start.13 = (bf16[128,128]{1,0:T(8,128)(2,1)S(1)}, bf16[128,128]{1,0:T(8,128)(2,1)}, u32[]{:S(2)}) copy-start(bf16[128,128]{1,0:T(8,128)(2,1)} %param.20) | copy-start | bytes 98308
  90.2 32.3 %all-to-all-start.2 = ((bf16[128,3,768]{2,1,0:T(4,128)(2,1)}), bf16[128,3,768]{2,1,0:T(4,128)(2,1)S(1)}, u32[]{:S(2)}, u32[]{:S(2)}) async-start(bf16[128,3,768]{2,1,0:T(4,128)(2,1)} %reshape.265), calls=%async_computation.2 | async-start | bytes 1572864 | tf_op jit(solution)/shard_map/all_to_all | solution.py:26
  123.2 12.2 %all-to-all-start.4 = ((bf16[32,24,96]{2,1,0:T(8,128)(2,1)}), bf16[32,24,96]{2,1,0:T(8,128)(2,1)S(1)}, u32[]{:S(2)}, u32[]{:S(2)}) async-start(bf16[32,24,96]{2,1,0:T(8,128)(2,1)} %broadcast_in_dim.10), calls=%async_computation.4 | async-start | bytes 393216 | tf_op jit(solution)/shard_map/all_to_all | solution.py:26
  128.1 0.7 copy-start.8
  128.7 1.3 copy-start.3
  128.7 1.3 copy-start.5
  130.1 2.5 %copy-start.14 = (bf16[128,16]{0,1:T(8,128)(2,1)S(1)}, bf16[128,16]{0,1:T(8,128)(2,1)}, u32[]{:S(2)}) copy-start(bf16[128,16]{0,1:T(8,128)(2,1)} %param.24) | copy-start | bytes 12292
  130.1 2.5 %copy-start.16 = (f32[128]{0:T(128)S(1)}, f32[128]{0:T(128)}, u32[]{:S(2)}) copy-start(f32[128]{0:T(128)} %param.23) | copy-start | bytes 1540
  135.4 17.3 %all-to-all-start.5 = ((f32[8,2,2304]{2,1,0:T(2,128)}), f32[8,2,2304]{2,1,0:T(2,128)S(1)}, u32[]{:S(2)}, u32[]{:S(2)}) async-start(f32[8,2,2304]{2,1,0:T(2,128)} %reshape.271), calls=%async_computation.5 | async-start | bytes 294912 | tf_op jit(solution)/shard_map/all_to_all | solution.py:26
  152.7 0.9 copy-start.12
  166.7 21.4 %all-to-all-start.3 = ((bf16[8,16,2304]{2,1,0:T(8,128)(2,1)}), bf16[8,16,2304]{2,1,0:T(8,128)(2,1)S(1)}, u32[]{:S(2)}, u32[]{:S(2)}) async-start(bf16[8,16,2304]{2,1,0:T(8,128)(2,1)} %bitcast.11), calls=%async_computation.3 | async-start | bytes 1179648 | tf_op jit(solution)/shard_map/all_to_all | solution.py:26

commit v2 on v1

--- a/solution.py
+++ b/solution.py
@@ -26,7 +26,20 @@
     return lax.all_to_all(shard, axes, 0, 0, tiled=True)
 
 
-def body(
+def doubled(block, axis, bit):
+    size = lax.axis_size(axis)
+    there = lax.ppermute(block, axis, [(i, i ^ (1 << bit)) for i in range(size)])
+    low = (lax.axis_index(axis) >> bit) & 1 == 0
+    return jnp.concatenate([jnp.where(low, block, there), jnp.where(low, there, block)], axis=0)
+
+
+def edge(normed, w_gate, w_value, mask):
+    opened = jnp.einsum("cp,cd->dp", normed, w_gate, preferred_element_type=F32)
+    value = jnp.einsum("cp,cd->dp", normed, w_value, preferred_element_type=F32)
+    return (jax.nn.sigmoid(opened) * value * mask).astype(BF)
+
+
+def block(
     pair,
     single,
     token_mask,
@@ -45,7 +58,6 @@
 ):
     chans, rows, width = pair.shape
     nq = C // chans
-    nrow = lax.axis_size(ROW)
     part = rows // nq
     spots = part * width
     r = lax.axis_index(ROW)
@@ -57,7 +69,9 @@
     own_keys = jnp.dot(single_normed, w_key, preferred_element_type=F32).astype(BF)
     own_values = jnp.dot(single_normed, w_value_gate[:, 0, :], preferred_element_type=F32).astype(BF)
     own_kv = jnp.concatenate([own_keys, own_values], axis=1)
-    kv = swap(jnp.broadcast_to(own_kv[None], (nrow,) + own_kv.shape), ROW)
+    kv = own_kv
+    for axis, bit in (("core", 0), ("zl", 0), ("zl", 1), ("x", 0)):
+        kv = doubled(kv, axis, bit)
     queries = jnp.dot(single_normed, w_query, preferred_element_type=F32).astype(BF)
     head_gate = jax.nn.sigmoid(
         jnp.dot(single_normed, w_value_gate[:, 1, :], preferred_element_type=F32)
@@ -68,14 +82,14 @@
     normed = layer_norm(full, pair_gain[:, None], 0).astype(BF)
     live_rows = lax.dynamic_slice_in_dim(live, r * rows + q * part, part, 0)
     mask = (live_rows[:, None] * live[None, :]).reshape(1, spots)
-    projected = jnp.einsum("cp,ckd->kdp", normed, w_ab, preferred_element_type=F32)
-    left = (jax.nn.sigmoid(projected[0]) * projected[1] * mask).astype(BF)
-    right = (jax.nn.sigmoid(projected[2]) * projected[3] * mask).astype(BF)
-
-    edges = swap(jnp.stack([left, right], axis=1), OWN)
-    left_owned = edges[:, 0].reshape(C * part, width)
-    right_here = edges[:, 1].reshape(C // nq, rows, width)
+    left = edge(normed, w_ab[:, 0], w_ab[:, 1], mask).reshape(C, 2, spots // 2)
+    right = edge(normed, w_ab[:, 2], w_ab[:, 3], mask).reshape(C, 2, spots // 2)
+    edges = swap(jnp.concatenate([right, left], axis=2), OWN)
+    right_here = edges[:, :, : spots // 2].reshape(C // nq, rows, width)
     right_there = lax.ppermute(right_here, "core", [(0, 1), (1, 0)])
+    left_owned = edges[:, :, spots // 2 :].reshape(C * part, width)
+    left_owned, kv = lax.optimization_barrier((left_owned, kv))
+    kv = doubled(kv, "x", 1)
     first = core == 0
     right_owned = jnp.stack(
         [
@@ -87,7 +101,8 @@
     owned = lax.dot_general(
         left_owned, right_owned, (((1,), (1,)), ((), ())), preferred_element_type=F32
     ).astype(BF)
-    product = swap(owned.reshape(C, part, width), OWN).reshape(C, spots)
+    product = swap(owned.reshape(C, 2, spots // 2), OWN).reshape(C, spots)
+    product, kv = lax.optimization_barrier((product, kv))
 
     product_normed = layer_norm(product.astype(F32), x_gain[:, None], 0).astype(BF)
     out_gate = jax.nn.sigmoid(
@@ -103,11 +118,8 @@
     heads = local_width // head_size
     bias = swap(bias.reshape(nq, heads, spots), CHAN)
     bias = bias.transpose(1, 0, 2).reshape(heads, rows, width)
-    pair_out = swap(renewed.reshape(nq, chans, spots), CHAN)
-    pair_out = pair_out.transpose(1, 0, 2).reshape(chans, rows, width)
-
-    keys = kv[..., :local_width].reshape(-1, heads, head_size)
-    values = kv[..., local_width:].reshape(-1, heads, head_size)
+    keys = kv[:, :local_width].reshape(-1, heads, head_size)
+    values = kv[:, local_width:].reshape(-1, heads, head_size)
     query_heads = queries.reshape(rows, heads, head_size)
     scores = jnp.einsum("ihe,jhe->hij", query_heads, keys, preferred_element_type=F32)
     scores = scores / jnp.sqrt(F32(head_size)) + bias
@@ -118,7 +130,12 @@
     mixed = jnp.einsum("hij,jhe->ihe", weights, values, preferred_element_type=F32)
     heads_out = (mixed.reshape(rows, local_width) * head_gate).astype(BF)
     terms = jnp.dot(heads_out, w_mix, preferred_element_type=F32).astype(BF)
-    terms = swap(terms.reshape(rows, nq, -1).transpose(1, 0, 2), CHAN)
+    terms = terms.reshape(rows, nq, local_width).transpose(1, 0, 2).reshape(nq, -1, 128)
+    terms = jnp.pad(terms, ((0, 0), (0, chans - terms.shape[1]), (0, 0)))
+    sent = jnp.concatenate([renewed.reshape(nq, chans, spots), terms], axis=2)
+    both = swap(sent, CHAN)
+    pair_out = both[:, :, :spots].transpose(1, 0, 2).reshape(chans, rows, width)
+    terms = both[:, : rows * local_width // 128, spots:].reshape(nq, rows, local_width)
     attended = jnp.sum(terms.astype(F32), axis=0).astype(BF)
     return (pair_out, attended)
 
@@ -126,7 +143,7 @@
 def solution(mesh):
     split = Mesh(mesh.devices.reshape(4, 4, 2, 4, 2), ROW + CHAN)
     return jax.shard_map(
-        body,
+        block,
         mesh=split,
         in_specs=(
             P(CHAN, ROW, None),

time: 190 us -> 163 us (0.86)
  blocking collectives: 53.8 us -> 22 us
  starting transfers between devices: 29.3 us -> 40.6 us
  local copies, waits for them, and re-layouts: 16 us -> 9.76 us
  waiting for transfers between devices: 75.4 us -> 79.2 us
  other arithmetic: 6.71 us -> 4.4 us
  matrix products: 7.07 us -> 5 us
    all_to_all x2 -> x1, blocking collectives: 53.8 us -> 22 us  [swap(): return lax.all_to_all(shard, axes, 0, 0, tiled=True)]
    ppermute x1 -> x6, waiting for transfers between devices: 1.25 us -> 30.4 us  [the longest x5 30.4 us: doubled(): there = lax.ppermute(block, axis, [(i, i ^ 1 << bit) for i in range(size)])]
    all_to_all x5 -> x4, waiting for transfers between devices: 74.1 us -> 48.8 us  [swap(): return lax.all_to_all(shard, axes, 0, 0, tiled=True)]
    ppermute x1 -> x6, starting transfers between devices: 0.27 us -> 8.83 us  [the longest x5 8.74 us: doubled(): there = lax.ppermute(block, axis, [(i, i ^ 1 << bit) for i in range(size)])]
    slice x2 -> x5, local copies, waits for them, and re-layouts: 5.02 us -> 1.37 us  [the longest x1 0.81 us: block(): right_here = edges[:, :, :spots // 2].reshape(C // nq, rows, width)]
    all_to_all x5 -> x4, starting transfers between devices: 29 us -> 31.8 us  [swap(): return lax.all_to_all(shard, axes, 0, 0, tiled=True)]
    another operation x4 -> x0, local copies, waits for them, and re-layouts: 2.24 us -> none  [the longest x1 1.61 us: body(): edges = swap(jnp.stack([left, right], axis=1), OWN)]
    convert_element_type x4 -> x3, other arithmetic: 2.65 us -> 0.41 us  [the longest x2 0.4 us: block(): normed = layer_norm(full, pair_gain[:, None], 0).astype(BF)]
  transfers between devices with their start and end apart: 6 -> 10, of which waited for: 6 -> 9; matrix products, arithmetic and copies ran while one was open for 6% -> 2% of each run, Pallas kernels for 0% -> 0%
where the time goes in v2:
time: 163 us; the launch traced here: 162 us
  waiting for transfers between devices  79.2 us (49%)
  starting transfers between devices  40.6 us (25%)
  blocking collectives  22 us (13%)
  local copies, waits for them, and re-layouts  9.76 us (6%)
  matrix products  5 us (3%)
  other arithmetic  4.4 us (3%)
    all_to_all x4, waiting for transfers between devices, swap(): return lax.all_to_all(shard, axes, 0, 0, tiled=True)  48.8 us
    all_to_all x4, starting transfers between devices, swap(): return lax.all_to_all(shard, axes, 0, 0, tiled=True)  31.8 us
    ppermute x5, waiting for transfers between devices, doubled(): there = lax.ppermute(block, axis, [(i, i ^ 1 << bit) for i in range(size)])  30.4 us
    all_to_all x1, blocking collectives, swap(): return lax.all_to_all(shard, axes, 0, 0, tiled=True)  22 us
    ppermute x5, starting transfers between devices, doubled(): there = lax.ppermute(block, axis, [(i, i ^ 1 << bit) for i in range(size)])  8.74 us
  transfers between devices with their start and end apart: 10, of which 9 were waited for; matrix products, arithmetic and copies ran while one was open for 2% of the time, Pallas kernels for 0%

profile of v2, /device:TPU:32, one launch (start us, length us, event | category | flops | bytes accessed | tf_op | source)
XLA Modules:
  0.0 162.1 jit_solution(3471197917315692609)
XLA Ops:
  0.6 1.4 reshape.201
  2.1 0.9 copy.82
  3.0 10.2 %all-to-all-start = ((bf16[8,16,2304]{2,1,0:T(8,128)(2,1)}), bf16[8,16,2304]{2,1,0:T(8,128)(2,1)S(1)}, u32[]{:S(2)}, u32[]{:S(2)}) async-start(bf16[8,16,2304]{2,1,0:T(8,128)(2,1)} %bitcast.80), calls=%async_computation | async-start | bytes 1179648 | tf_op jit(solution)/shard_map/all_to_all | solution.py:26
  13.5 0.2 fusion.74
  13.7 20.5 %all-to-all-done = bf16[8,16,2304]{2,1,0:T(8,128)(2,1)S(1)} async-done(((bf16[8,16,2304]{2,1,0:T(8,128)(2,1)}), bf16[8,16,2304]{2,1,0:T(8,128)(2,1)S(1)}, u32[]{:S(2)}, u32[]{:S(2)}) %all-to-all-start) | async-done | bytes 589856 | tf_op jit(solution)/shard_map/all_to_all | solution.py:26
  34.2 0.1 convert_reduce_fusion.2
  34.3 0.2 multiply_reduce_fusion
  34.5 0.2 multiply_convert_fusion
  34.7 0.5 fusion.5
  35.2 0.4 fusion.17
  35.6 0.1 reshape.203
  35.7 0.5 fusion.8
  36.3 0.4 fusion.18
  36.6 0.1 reshape.202
  36.8 2.1 %pad_maximum_fusion = bf16[128,2,2304]{2,1,0:T(2,128)(2,1)} fusion(bf16[128,2,1152]{2,1,0:T(2,128)(2,1)S(1)} %reshape.203, bf16[128,2,1152]{2,1,0:T(2,128)(2,1)S(1)} %reshape.202), kind=kLoop, calls=%fused_computation.43 | loop fusion | flops 2359296 | bytes 2359296 | tf_op jit(solution)/shard_map/concatenate | solution.py:87
  38.9 8.0 %all-to-all-start.1 = ((bf16[128,2,2304]{2,1,0:T(2,128)(2,1)}), bf16[128,2,2304]{2,1,0:T(2,128)(2,1)S(1)}, u32[]{:S(2)}, u32[]{:S(2)}) async-start(bf16[128,2,2304]{2,1,0:T(2,128)(2,1)} %pad_maximum_fusion), calls=%async_computation.1 | async-start | bytes 2359296 | tf_op jit(solution)/shard_map/all_to_all | solution.py:26
  46.9 0.1 convert_reduce_fusion.3
  47.0 0.2 fusion.54
  47.2 0.2 convolution_convert_fusion.3
  47.4 0.2 convolution_convert_fusion.4
  47.7 1.2 collective-permute-done
  49.0 1.0 collective-permute-start.1
  50.0 21.0 %collective-permute-done.1 = bf16[48,96]{1,0:T(8,128)(2,1)S(1)} collective-permute-done((bf16[48,96]{1,0:T(8,128)(2,1)S(1)}, bf16[48,96]{1,0:T(8,128)(2,1)S(1)}, u32[]{:S(2)}, u32[]{:S(2)}) %collective-permute-start.1) | collective-permute-done | bytes 9248 | tf_op jit(solution)/shard_map/ppermute | solution.py:31
  71.0 3.3 %collective-permute-start.2 = (bf16[96,96]{1,0:T(8,128)(2,1)S(1)}, bf16[96,96]{1,0:T(8,128)(2,1)S(1)}, u32[]{:S(2)}, u32[]{:S(2)}) collective-permute-start(bf16[96,96]{1,0:T(8,128)(2,1)S(1)} %pad_maximum_fusion.5), channel_id=1, source_target_pairs={{0,32},{16,48},{32,0},{48,16},{1,33},{17,49},{33,1},{49,17},{2,34}... | collective-permute-start | bytes 55304 | tf_op jit(solution)/shard_map/ppermute | solution.py:31
  74.2 1.8 %collective-permute-done.2 = bf16[96,96]{1,0:T(8,128)(2,1)S(1)} collective-permute-done((bf16[96,96]{1,0:T(8,128)(2,1)S(1)}, bf16[96,96]{1,0:T(8,128)(2,1)S(1)}, u32[]{:S(2)}, u32[]{:S(2)}) %collective-permute-start.2) | collective-permute-done | bytes 18464 | tf_op jit(solution)/shard_map/ppermute | solution.py:31
  76.0 4.2 %all-to-all-done.1 = bf16[128,2,2304]{2,1,0:T(2,128)(2,1)S(1)} async-done(((bf16[128,2,2304]{2,1,0:T(2,128)(2,1)}), bf16[128,2,2304]{2,1,0:T(2,128)(2,1)S(1)}, u32[]{:S(2)}, u32[]{:S(2)}) %all-to-all-start.1) | async-done | bytes 1179680 | tf_op jit(solution)/shard_map/all_to_all | solution.py:26
  80.3 0.8 fusion.72
  81.1 0.4 reshape.205
  81.5 0.1 collective-permute-start.4
  81.6 1.1 collective-permute-start.3
  82.6 0.2 convolution_convert_fusion.2
  82.8 3.2 %collective-permute-done.3 = bf16[192,96]{1,0:T(8,128)(2,1)S(1)} collective-permute-done((bf16[192,96]{1,0:T(8,128)(2,1)S(1)}, bf16[192,96]{1,0:T(8,128)(2,1)S(1)}, u32[]{:S(2)}, u32[]{:S(2)}) %collective-permute-start.3) | collective-permute-done | bytes 36896 | tf_op jit(solution)/shard_map/ppermute | solution.py:31
  86.1 0.4 reshape.204
  86.5 0.1 pad_maximum_fusion.1
  86.7 0.7 convolution_convert_fusion
  87.3 1.2 reshape.207
  88.5 10.2 %all-to-all-start.2 = ((bf16[128,2,1152]{2,1,0:T(2,128)(2,1)}), bf16[128,2,1152]{2,1,0:T(2,128)(2,1)S(1)}, u32[]{:S(2)}, u32[]{:S(2)}) async-start(bf16[128,2,1152]{2,1,0:T(2,128)(2,1)} %reshape.207), calls=%async_computation.2 | async-start | bytes 1179648 | tf_op jit(solution)/shard_map/all_to_all | solution.py:26
  98.8 0.2 fusion.32
  99.0 3.4 %collective-permute-start.5 = (bf16[384,96]{1,0:T(8,128)(2,1)S(1)}, bf16[384,96]{1,0:T(8,128)(2,1)S(1)}, u32[]{:S(2)}, u32[]{:S(2)}) collective-permute-start(bf16[384,96]{1,0:T(8,128)(2,1)S(1)} %pad_maximum_fusion.3), channel_id=1, source_target_pairs={{0,128},{64,192},{128,0},{192,64},{1,129},{65,193},{129,1},{193,65... | collective-permute-start | bytes 221192 | tf_op jit(solution)/shard_map/ppermute | solution.py:31
  102.4 0.5 fusion.11
  102.9 3.3 %collective-permute-done.5 = bf16[384,96]{1,0:T(8,128)(2,1)S(1)} collective-permute-done((bf16[384,96]{1,0:T(8,128)(2,1)S(1)}, bf16[384,96]{1,0:T(8,128)(2,1)S(1)}, u32[]{:S(2)}, u32[]{:S(2)}) %collective-permute-start.5) | collective-permute-done | bytes 73760 | tf_op jit(solution)/shard_map/ppermute | solution.py:31
  106.3 13.9 %all-to-all-done.2 = bf16[128,2,1152]{2,1,0:T(2,128)(2,1)S(1)} async-done(((bf16[128,2,1152]{2,1,0:T(2,128)(2,1)}), bf16[128,2,1152]{2,1,0:T(2,128)(2,1)S(1)}, u32[]{:S(2)}, u32[]{:S(2)}) %all-to-all-start.2) | async-done | bytes 589856 | tf_op jit(solution)/shard_map/all_to_all | solution.py:26
  120.3 0.1 convert_reduce_fusion.1
  120.4 0.2 fusion.27
  120.6 0.4 copy-done.3
  121.0 0.4 convert_reduce_fusion
  121.4 0.2 fusion.24
  121.7 0.3 convolution_bitcast_fusion
  122.0 0.7 reshape.213
  122.7 3.4 %all-to-all-start.3 = ((f32[8,2,2304]{2,1,0:T(2,128)}), f32[8,2,2304]{2,1,0:T(2,128)S(1)}, u32[]{:S(2)}, u32[]{:S(2)}) async-start(f32[8,2,2304]{2,1,0:T(2,128)} %reshape.213), calls=%async_computation.3 | async-start | bytes 294912 | tf_op jit(solution)/shard_map/all_to_all | solution.py:26
  126.2 0.1 fusion.73
  126.3 0.1 copy.54
  126.5 0.1 copy.55
  126.6 10.1 %all-to-all-done.3 = f32[8,2,2304]{2,1,0:T(2,128)S(1)} async-done(((f32[8,2,2304]{2,1,0:T(2,128)}), f32[8,2,2304]{2,1,0:T(2,128)S(1)}, u32[]{:S(2)}, u32[]{:S(2)}) %all-to-all-start.3) | async-done | bytes 147488 | tf_op jit(solution)/shard_map/all_to_all | solution.py:26
  136.8 0.1 fusion.36
  136.9 0.2 fusion.75
  137.1 0.2 fusion.51
  137.4 0.4 convolution_convert_fusion.1
  137.8 0.1 reshape.216
  137.9 0.1 reshape.217
  138.1 22.0 %all_to_all.25 = bf16[8,16,2432]{2,1,0:T(8,128)(2,1)S(1)} all-to-all(bf16[8,16,2432]{2,1,0:T(8,128)(2,1)S(1)} %fusion.42), channel_id=1, replica_groups=mesh['x'=4,'zl'=4,'core'=2,'y'=4,'zh'=2] {'y','zh'}, dimensions={0} | all-to-all | bytes 1245184 | tf_op jit(solution)/shard_map/all_to_all | solution.py:26
  160.1 0.2 copy.60
  160.3 1.1 reshape.218
  161.4 0.7 reduce_sum.105
  (64 shorter events, 1.2 us)
Async XLA Ops:
  0.6 136.8 %copy-start = (bf16[48,384]{1,0:T(8,128)(2,1)S(1)}, bf16[48,384]{1,0:T(8,128)(2,1)}, u32[]{:S(2)}) copy-start(bf16[48,384]{1,0:T(8,128)(2,1)} %param.29) | copy-start | bytes 110596
  2.0 11.1 %copy-start.5 = (f32[128]{0:T(128)S(1)}, f32[128]{0:T(128)}, u32[]{:S(2)}) copy-start(f32[128]{0:T(128)} %param.18) | copy-start | bytes 1540
  2.0 11.2 %copy-start.4 = (s32[768]{0:T(1024)S(1)}, s32[768]{0:T(1024)}, u32[]{:S(2)}) copy-start(s32[768]{0:T(1024)} %param.17) | copy-start | bytes 9220
  2.1 11.4 %copy-start.1 = (bf16[128,4,128]{2,1,0:T(4,128)(2,1)S(1)}, bf16[128,4,128]{2,1,0:T(4,128)(2,1)}, u32[]{:S(2)}) copy-start(bf16[128,4,128]{2,1,0:T(4,128)(2,1)} %param.19) | copy-start | bytes 393220
  3.0 31.2 %all-to-all-start = ((bf16[8,16,2304]{2,1,0:T(8,128)(2,1)}), bf16[8,16,2304]{2,1,0:T(8,128)(2,1)S(1)}, u32[]{:S(2)}, u32[]{:S(2)}) async-start(bf16[8,16,2304]{2,1,0:T(8,128)(2,1)} %bitcast.80), calls=%async_computation | async-start | bytes 1179648 | tf_op jit(solution)/shard_map/all_to_all | solution.py:26
  38.9 8.0 %copy-start.2 = (bf16[24,384]{1,0:T(8,128)(2,1)S(1)}, bf16[24,384]{1,0:T(8,128)(2,1)}, u32[]{:S(2)}) copy-start(bf16[24,384]{1,0:T(8,128)(2,1)} %param.16) | copy-start | bytes 55300
  38.9 8.3 %copy-start.7 = (bf16[384,2,48]{0,2,1:T(8,128)(2,1)S(1)}, bf16[384,2,48]{0,2,1:T(8,128)(2,1)}, u32[]{:S(2)}) copy-start(bf16[384,2,48]{0,2,1:T(8,128)(2,1)} %param.28) | copy-start | bytes 221188
  38.9 8.4 %copy-start.12 = (f32[384]{0:T(512)S(1)}, f32[384]{0:T(512)}, u32[]{:S(2)}) copy-start(f32[384]{0:T(512)} %param.25) | copy-start | bytes 4612
  38.9 8.6 %copy-start.8 = (bf16[384,48]{0,1:T(8,128)(2,1)S(1)}, bf16[384,48]{0,1:T(8,128)(2,1)}, u32[]{:S(2)}) copy-start(bf16[384,48]{0,1:T(8,128)(2,1)} %param.27) | copy-start | bytes 110596
  38.9 41.4 %all-to-all-start.1 = ((bf16[128,2,2304]{2,1,0:T(2,128)(2,1)}), bf16[128,2,2304]{2,1,0:T(2,128)(2,1)S(1)}, u32[]{:S(2)}, u32[]{:S(2)}) async-start(bf16[128,2,2304]{2,1,0:T(2,128)(2,1)} %pad_maximum_fusion), calls=%async_computation.1 | async-start | bytes 2359296 | tf_op jit(solution)/shard_map/all_to_all | solution.py:26
  47.7 1.2 collective-permute-start
  49.0 21.9 %collective-permute-start.1 = (bf16[48,96]{1,0:T(8,128)(2,1)S(1)}, bf16[48,96]{1,0:T(8,128)(2,1)S(1)}, u32[]{:S(2)}, u32[]{:S(2)}) collective-permute-start(bf16[48,96]{1,0:T(8,128)(2,1)S(1)} %pad_maximum_fusion.6), channel_id=1, source_target_pairs={{0,16},{16,0},{32,48},{48,32},{1,17},{17,1},{33,49},{49,33},{2,18}... | collective-permute-start | bytes 27656 | tf_op jit(solution)/shard_map/ppermute | solution.py:31
  71.0 5.1 %collective-permute-start.2 = (bf16[96,96]{1,0:T(8,128)(2,1)S(1)}, bf16[96,96]{1,0:T(8,128)(2,1)S(1)}, u32[]{:S(2)}, u32[]{:S(2)}) collective-permute-start(bf16[96,96]{1,0:T(8,128)(2,1)S(1)} %pad_maximum_fusion.5), channel_id=1, source_target_pairs={{0,32},{16,48},{32,0},{48,16},{1,33},{17,49},{33,1},{49,17},{2,34}... | collective-permute-start | bytes 55304 | tf_op jit(solution)/shard_map/ppermute | solution.py:31
  81.1 1.6 copy-start.9
  81.5 5.0 %collective-permute-start.4 = (bf16[16,24,768]{2,1,0:T(8,128)(2,1)S(1)}, bf16[16,24,768]{2,1,0:T(8,128)(2,1)S(1)}, u32[]{:S(2)}, u32[]{:S(2)}) collective-permute-start(bf16[16,24,768]{2,1,0:T(8,128)(2,1)S(1)} %reshape.205), channel_id=1, source_target_pairs={{0,8},{8,0},{1,9},{9,1},{2,10},{10,2},{3,11},{11,3},{4,12},{12,4},... | collective-permute-start | bytes 1769480 | tf_op jit(solution)/shard_map/ppermute | solution.py:89
  81.6 4.4 %collective-permute-start.3 = (bf16[192,96]{1,0:T(8,128)(2,1)S(1)}, bf16[192,96]{1,0:T(8,128)(2,1)S(1)}, u32[]{:S(2)}, u32[]{:S(2)}) collective-permute-start(bf16[192,96]{1,0:T(8,128)(2,1)S(1)} %pad_maximum_fusion.4), channel_id=1, source_target_pairs={{0,64},{64,0},{128,192},{192,128},{1,65},{65,1},{129,193},{193,129... | collective-permute-start | bytes 110600 | tf_op jit(solution)/shard_map/ppermute | solution.py:31
  88.5 13.9 %copy-start.10 = (bf16[128,128]{1,0:T(8,128)(2,1)S(1)}, bf16[128,128]{1,0:T(8,128)(2,1)}, u32[]{:S(2)}) copy-start(bf16[128,128]{1,0:T(8,128)(2,1)} %param.20) | copy-start | bytes 98308
  88.5 31.7 %all-to-all-start.2 = ((bf16[128,2,1152]{2,1,0:T(2,128)(2,1)}), bf16[128,2,1152]{2,1,0:T(2,128)(2,1)S(1)}, u32[]{:S(2)}, u32[]{:S(2)}) async-start(bf16[128,2,1152]{2,1,0:T(2,128)(2,1)} %reshape.207), calls=%async_computation.2 | async-start | bytes 1179648 | tf_op jit(solution)/shard_map/all_to_all | solution.py:26
  99.0 7.3 %collective-permute-start.5 = (bf16[384,96]{1,0:T(8,128)(2,1)S(1)}, bf16[384,96]{1,0:T(8,128)(2,1)S(1)}, u32[]{:S(2)}, u32[]{:S(2)}) collective-permute-start(bf16[384,96]{1,0:T(8,128)(2,1)S(1)} %pad_maximum_fusion.3), channel_id=1, source_target_pairs={{0,128},{64,192},{128,0},{192,64},{1,129},{65,193},{129,1},{193,65... | collective-permute-start | bytes 221192 | tf_op jit(solution)/shard_map/ppermute | solution.py:31
  120.2 0.8 copy-start.3
  120.2 0.8 copy-start.6
  121.0 0.7 copy-start.11
  121.0 0.7 copy-start.13
  122.7 14.0 %all-to-all-start.3 = ((f32[8,2,2304]{2,1,0:T(2,128)}), f32[8,2,2304]{2,1,0:T(2,128)S(1)}, u32[]{:S(2)}, u32[]{:S(2)}) async-start(f32[8,2,2304]{2,1,0:T(2,128)} %reshape.213), calls=%async_computation.3 | async-start | bytes 294912 | tf_op jit(solution)/shard_map/all_to_all | solution.py:26

commit v3 on v2

--- a/solution.py
+++ b/solution.py
@@ -8,6 +8,7 @@
 H = 16
 C = 128
 EPS = 1e-05
+LANES = 128
 ROW = ("x", "zl", "core")
 CHAN = ("y", "zh")
 OWN = ("x", "zl", "y", "zh")
@@ -26,11 +27,16 @@
     return lax.all_to_all(shard, axes, 0, 0, tiled=True)
 
 
-def doubled(block, axis, bit):
+def doubled(block, axis, bit, dim):
     size = lax.axis_size(axis)
     there = lax.ppermute(block, axis, [(i, i ^ (1 << bit)) for i in range(size)])
     low = (lax.axis_index(axis) >> bit) & 1 == 0
-    return jnp.concatenate([jnp.where(low, block, there), jnp.where(low, there, block)], axis=0)
+    return jnp.concatenate([jnp.where(low, block, there), jnp.where(low, there, block)], axis=dim)
+
+
+def filled(*parts):
+    wide = jnp.concatenate(parts, axis=1)
+    return jnp.pad(wide, ((0, 0), (0, LANES - wide.shape[1])))
 
 
 def edge(normed, w_gate, w_value, mask):
@@ -68,14 +74,30 @@
     single_normed = layer_norm(single.astype(F32), single_gain[None, :], 1).astype(BF)
     own_keys = jnp.dot(single_normed, w_key, preferred_element_type=F32).astype(BF)
     own_values = jnp.dot(single_normed, w_value_gate[:, 0, :], preferred_element_type=F32).astype(BF)
-    own_kv = jnp.concatenate([own_keys, own_values], axis=1)
-    kv = own_kv
-    for axis, bit in (("core", 0), ("zl", 0), ("zl", 1), ("x", 0)):
-        kv = doubled(kv, axis, bit)
     queries = jnp.dot(single_normed, w_query, preferred_element_type=F32).astype(BF)
     head_gate = jax.nn.sigmoid(
         jnp.dot(single_normed, w_value_gate[:, 1, :], preferred_element_type=F32)
     )
+    gate_high = lax.reduce_precision(head_gate, 8, 7)
+    gate_rest = (head_gate - gate_high).astype(BF)
+    local = w_query.shape[1]
+    kv = filled(own_keys, own_values)
+    rest = jnp.concatenate(
+        [filled(queries, gate_high.astype(BF)), filled(gate_rest)]
+        + [w_mix[:, k : k + LANES] for k in range(0, D, LANES)]
+    )
+    both = doubled(jnp.concatenate([kv, rest])[None], "zh", 0, 0)
+    kv, rest = both[:, :rows], both[:, rows:]
+    kv = doubled(kv, "zl", 0, 1)
+    kv = doubled(kv, "zl", 1, 1)
+    both = jnp.concatenate([kv, rest], axis=1)
+    both = doubled(both, "y", 0, 0)
+    both = doubled(both, "y", 1, 0)
+    kv, rest = both[:, : kv.shape[1]], both[:, kv.shape[1] :]
+    kv = doubled(kv[:, None, None], "x", 1, 1)
+    kv = doubled(kv, "x", 0, 2)
+    kv = doubled(kv.reshape(nq, -1, 1, rows, LANES), "core", 0, 2)
+    kv = kv.reshape(nq, -1, LANES)
 
     sent = pair.reshape(chans, nq, spots).transpose(1, 0, 2)
     full = swap(sent, CHAN).reshape(C, spots).astype(F32)
@@ -88,8 +110,6 @@
     right_here = edges[:, :, : spots // 2].reshape(C // nq, rows, width)
     right_there = lax.ppermute(right_here, "core", [(0, 1), (1, 0)])
     left_owned = edges[:, :, spots // 2 :].reshape(C * part, width)
-    left_owned, kv = lax.optimization_barrier((left_owned, kv))
-    kv = doubled(kv, "x", 1)
     first = core == 0
     right_owned = jnp.stack(
         [
@@ -102,7 +122,6 @@
         left_owned, right_owned, (((1,), (1,)), ((), ())), preferred_element_type=F32
     ).astype(BF)
     product = swap(owned.reshape(C, 2, spots // 2), OWN).reshape(C, spots)
-    product, kv = lax.optimization_barrier((product, kv))
 
     product_normed = layer_norm(product.astype(F32), x_gain[:, None], 0).astype(BF)
     out_gate = jax.nn.sigmoid(
@@ -113,30 +132,34 @@
     bias_input = layer_norm(renewed.astype(F32), bias_gain[:, None], 0).astype(BF)
     bias = jnp.einsum("cp,ch->hp", bias_input, w_bias, preferred_element_type=F32)
 
+    heads = H // nq
     head_size = D // H
-    local_width = w_query.shape[1]
-    heads = local_width // head_size
-    bias = swap(bias.reshape(nq, heads, spots), CHAN)
-    bias = bias.transpose(1, 0, 2).reshape(heads, rows, width)
-    keys = kv[:, :local_width].reshape(-1, heads, head_size)
-    values = kv[:, local_width:].reshape(-1, heads, head_size)
-    query_heads = queries.reshape(rows, heads, head_size)
-    scores = jnp.einsum("ihe,jhe->hij", query_heads, keys, preferred_element_type=F32)
-    scores = scores / jnp.sqrt(F32(head_size)) + bias
+    at = q * part
+    mine = lax.dynamic_slice_in_dim(rest, at, part, 1)
+    gate_mine = mine[..., local : 2 * local].astype(F32) + lax.dynamic_slice_in_dim(
+        rest, rows + at, part, 1
+    )[..., :local].astype(F32)
+    is_head = (jnp.arange(local)[None, :] // head_size == jnp.arange(heads)[:, None])[:, None]
+    queries = jnp.where(is_head, mine[:, None, :, :local], 0).reshape(nq, heads * part, local)
+    scores = jnp.einsum("qaf,qjf->qaj", queries, kv[..., :local], preferred_element_type=F32)
+    scores = scores / jnp.sqrt(F32(head_size)) + bias.reshape(nq, heads * part, width)
     scores = jnp.where(live[None, None, :] > 0, scores, -jnp.inf)
     top = jnp.max(scores, axis=2, keepdims=True)
     raised = jnp.exp(scores - top)
     weights = (raised / jnp.sum(raised, axis=2, keepdims=True)).astype(BF)
-    mixed = jnp.einsum("hij,jhe->ihe", weights, values, preferred_element_type=F32)
-    heads_out = (mixed.reshape(rows, local_width) * head_gate).astype(BF)
-    terms = jnp.dot(heads_out, w_mix, preferred_element_type=F32).astype(BF)
-    terms = terms.reshape(rows, nq, local_width).transpose(1, 0, 2).reshape(nq, -1, 128)
-    terms = jnp.pad(terms, ((0, 0), (0, chans - terms.shape[1]), (0, 0)))
-    sent = jnp.concatenate([renewed.reshape(nq, chans, spots), terms], axis=2)
+    mixed = jnp.einsum(
+        "qaj,qjf->qaf", weights, kv[..., local : 2 * local], preferred_element_type=F32
+    )
+    mixed = jnp.where(is_head, mixed.reshape(nq, heads, part, local), 0).sum(axis=1)
+    heads_out = (mixed * gate_mine).astype(BF).transpose(1, 0, 2).reshape(part, D)
+    mix = rest[:, 2 * rows :].reshape(nq, D // LANES, local, LANES).transpose(0, 2, 1, 3)
+    summed = jnp.dot(heads_out, mix.reshape(D, D), preferred_element_type=F32).astype(BF)
+    summed = summed.reshape(part, nq, local).transpose(1, 0, 2)
+    summed = jnp.pad(summed, ((0, 0), (0, chans - part), (0, LANES - local)))
+    sent = jnp.concatenate([renewed.reshape(nq, chans, spots), summed], axis=2)
     both = swap(sent, CHAN)
     pair_out = both[:, :, :spots].transpose(1, 0, 2).reshape(chans, rows, width)
-    terms = both[:, : rows * local_width // 128, spots:].reshape(nq, rows, local_width)
-    attended = jnp.sum(terms.astype(F32), axis=0).astype(BF)
+    attended = both[:, :part, spots : spots + local].reshape(rows, local)
     return (pair_out, attended)
 
 

time: 163 us -> 191 us (1.17)
  starting transfers between devices: 40.6 us -> 55.3 us
  other arithmetic: 4.4 us -> 12.5 us
  local copies, waits for them, and re-layouts: 9.76 us -> 15.8 us
  waiting for transfers between devices: 79.2 us -> 73.7 us
  blocking collectives: 22 us -> 24.6 us
    all_to_all x4 -> x3, waiting for transfers between devices: 48.8 us -> 18.9 us  [swap(): return lax.all_to_all(shard, axes, 0, 0, tiled=True)]
    ppermute x5 -> x8, waiting for transfers between devices: 30.4 us -> 54.8 us  [doubled(): there = lax.ppermute(block, axis, [(i, i ^ 1 << bit) for i in range(size)])]
    ppermute x5 -> x8, starting transfers between devices: 8.74 us -> 18.4 us  [doubled(): there = lax.ppermute(block, axis, [(i, i ^ 1 << bit) for i in range(size)])]
    all_to_all x4 -> x3, starting transfers between devices: 31.8 us -> 36.8 us  [swap(): return lax.all_to_all(shard, axes, 0, 0, tiled=True)]
    all_to_all x1, blocking collectives: 22 us -> 24.6 us  [swap(): return lax.all_to_all(shard, axes, 0, 0, tiled=True)]
    select_n x5 -> x7, other arithmetic: 0.15 us -> 2.68 us  [doubled(): jnp.where(low, block, there)]
    unnamed x29 -> x40, local copies, waits for them, and re-layouts: 0.55 us -> 3.03 us
  transfers between devices with their start and end apart: 10 -> 12, of which waited for: 9 -> 8; matrix products, arithmetic and copies ran while one was open for 2% -> 10% of each run, Pallas kernels for 0% -> 0%
where the time goes in v3:
time: 191 us; the launch traced here: 190 us
  waiting for transfers between devices  73.7 us (39%)
  starting transfers between devices  55.3 us (29%)
  blocking collectives  24.6 us (13%)
  local copies, waits for them, and re-layouts  15.8 us (8%)
  other arithmetic  12.5 us (7%)
  matrix products  6.84 us (4%)
    ppermute x8, waiting for transfers between devices, doubled(): there = lax.ppermute(block, axis, [(i, i ^ 1 << bit) for i in range(size)])  54.8 us
    all_to_all x3, starting transfers between devices, swap(): return lax.all_to_all(shard, axes, 0, 0, tiled=True)  36.8 us
    all_to_all x1, blocking collectives, swap(): return lax.all_to_all(shard, axes, 0, 0, tiled=True)  24.6 us
    all_to_all x3, waiting for transfers between devices, swap(): return lax.all_to_all(shard, axes, 0, 0, tiled=True)  18.9 us
    ppermute x8, starting transfers between devices, doubled(): there = lax.ppermute(block, axis, [(i, i ^ 1 << bit) for i in range(size)])  18.4 us
  transfers between devices with their start and end apart: 12, of which 8 were waited for; matrix products, arithmetic and copies ran while one was open for 10% of the time, Pallas kernels for 0%

profile of v3, /device:TPU:32, one launch (start us, length us, event | category | flops | bytes accessed | tf_op | source)
XLA Modules:
  0.0 190.1 jit_solution(7075635608624111885)
XLA Ops:
  0.6 1.4 reshape.249
  2.1 0.9 copy.115
  3.0 10.3 %all-to-all-start = ((bf16[8,16,2304]{2,1,0:T(8,128)(2,1)}), bf16[8,16,2304]{2,1,0:T(8,128)(2,1)S(1)}, u32[]{:S(2)}, u32[]{:S(2)}) async-start(bf16[8,16,2304]{2,1,0:T(8,128)(2,1)} %bitcast.91), calls=%async_computation | async-start | bytes 1179648 | tf_op jit(solution)/shard_map/all_to_all | solution.py:27
  13.5 0.2 fusion.66
  13.7 0.2 convolution_convert_fusion.2
  13.9 0.2 fusion.74
  14.1 0.2 convolution_convert_fusion.3
  14.3 0.2 convolution_convert_fusion.1
  14.8 6.0 %collective-permute-start.1 = (bf16[1,216,128]{2,0,1:T(2,128)(2,1)S(1)}, bf16[1,216,128]{2,0,1:T(2,128)(2,1)S(1)}, u32[]{:S(2)}, u32[]{:S(2)}) collective-permute-start(bf16[1,216,128]{2,0,1:T(2,128)(2,1)S(1)} %copy.74), channel_id=1, source_target_pairs={{0,1},{1,0},{2,3},{3,2},{4,5},{5,4},{6,7},{7,6},{8,9},{9,8},{10,11... | collective-permute-start | bytes 165896 | tf_op jit(solution)/shard_map/ppermute | solution.py:32
  20.8 0.2 fusion.87
  21.2 15.6 %collective-permute-done.1 = bf16[1,216,128]{2,0,1:T(2,128)(2,1)S(1)} collective-permute-done((bf16[1,216,128]{2,0,1:T(2,128)(2,1)S(1)}, bf16[1,216,128]{2,0,1:T(2,128)(2,1)S(1)}, u32[]{:S(2)}, u32[]{:S(2)}) %collective-permute-start.1) | collective-permute-done | bytes 55328 | tf_op jit(solution)/shard_map/ppermute | solution.py:32
  36.8 0.2 broadcast_select_fusion.9
  37.1 0.4 collective-permute-start.2
  37.6 3.2 %collective-permute-done.2 = bf16[2,24,128]{2,0,1:T(2,128)(2,1)S(1)} collective-permute-done((bf16[2,24,128]{2,0,1:T(2,128)(2,1)S(1)}, bf16[2,24,128]{2,0,1:T(2,128)(2,1)S(1)}, u32[]{:S(2)}, u32[]{:S(2)}) %collective-permute-start.2) | collective-permute-done | bytes 12320 | tf_op jit(solution)/shard_map/ppermute | solution.py:32
  41.2 0.2 multiply_convert_fusion.1
  41.4 0.5 fusion.8
  41.9 0.4 fusion.18
  42.4 0.5 fusion.5
  43.0 0.4 fusion.17
  43.5 2.1 %pad_maximum_fusion.1 = bf16[128,2,2304]{2,1,0:T(2,128)(2,1)} fusion(bf16[128,2,1152]{2,1,0:T(2,128)(2,1)S(1)} %reshape.251, bf16[128,2,1152]{2,1,0:T(2,128)(2,1)S(1)} %reshape.250), kind=kLoop, calls=%fused_computation.41 | loop fusion | flops 2359296 | bytes 2359296 | tf_op jit(solution)/shard_map/concatenate | solution.py:109
  45.6 10.2 %all-to-all-start.1 = ((bf16[128,2,2304]{2,1,0:T(2,128)(2,1)}), bf16[128,2,2304]{2,1,0:T(2,128)(2,1)S(1)}, u32[]{:S(2)}, u32[]{:S(2)}) async-start(bf16[128,2,2304]{2,1,0:T(2,128)(2,1)} %pad_maximum_fusion.1), calls=%async_computation.1 | async-start | bytes 2359296 | tf_op jit(solution)/shard_map/all_to_all | solution.py:27
  55.8 2.5 %collective-permute-start.3 = (bf16[2,48,128]{2,0,1:T(2,128)(2,1)S(1)}, bf16[2,48,128]{2,0,1:T(2,128)(2,1)S(1)}, u32[]{:S(2)}, u32[]{:S(2)}) collective-permute-start(bf16[2,48,128]{2,0,1:T(2,128)(2,1)S(1)} %pad_maximum_fusion.7), channel_id=1, source_target_pairs={{0,32},{16,48},{32,0},{48,16},{1,33},{17,49},{33,1},{49,17},{2,34}... | collective-permute-start | bytes 73736 | tf_op jit(solution)/shard_map/ppermute | solution.py:32
  58.3 21.2 %collective-permute-done.3 = bf16[2,48,128]{2,0,1:T(2,128)(2,1)S(1)} collective-permute-done((bf16[2,48,128]{2,0,1:T(2,128)(2,1)S(1)}, bf16[2,48,128]{2,0,1:T(2,128)(2,1)S(1)}, u32[]{:S(2)}, u32[]{:S(2)}) %collective-permute-start.3) | collective-permute-done | bytes 24608 | tf_op jit(solution)/shard_map/ppermute | solution.py:32
  79.6 0.3 fusion.62
  79.8 1.3 collective-permute-start.4
  81.1 4.1 %collective-permute-done.4 = bf16[2,288,128]{2,0,1:T(2,128)(2,1)S(1)} collective-permute-done((bf16[2,288,128]{2,0,1:T(2,128)(2,1)S(1)}, bf16[2,288,128]{2,0,1:T(2,128)(2,1)S(1)}, u32[]{:S(2)}, u32[]{:S(2)}) %collective-permute-start.4) | collective-permute-done | bytes 147488 | tf_op jit(solution)/shard_map/ppermute | solution.py:32
  85.2 0.3 pad_maximum_fusion.6
  85.6 3.0 %collective-permute-start.5 = (bf16[4,288,128]{2,0,1:T(4,128)(2,1)S(1)}, bf16[4,288,128]{2,0,1:T(4,128)(2,1)S(1)}, u32[]{:S(2)}, u32[]{:S(2)}) collective-permute-start(bf16[4,288,128]{2,0,1:T(4,128)(2,1)S(1)} %pad_maximum_fusion.6), channel_id=1, source_target_pairs={{0,4},{2,6},{4,0},{6,2},{1,5},{3,7},{5,1},{7,3},{8,12},{10,14},{12... | collective-permute-start | bytes 884744 | tf_op jit(solution)/shard_map/ppermute | solution.py:32
  88.6 5.3 %collective-permute-done.5 = bf16[4,288,128]{2,0,1:T(4,128)(2,1)S(1)} collective-permute-done((bf16[4,288,128]{2,0,1:T(4,128)(2,1)S(1)}, bf16[4,288,128]{2,0,1:T(4,128)(2,1)S(1)}, u32[]{:S(2)}, u32[]{:S(2)}) %collective-permute-start.5) | collective-permute-done | bytes 294944 | tf_op jit(solution)/shard_map/ppermute | solution.py:32
  93.9 0.5 broadcast_select_fusion.6
  94.5 3.8 %collective-permute-start.6 = (bf16[8,1,1,96,128]{4,0,3,2,1:T(8,128)(2,1)S(1)}, bf16[8,1,1,96,128]{4,0,3,2,1:T(8,128)(2,1)S(1)}, u32[]{:S(2)}, u32[]{:S(2)}) collective-permute-start(bf16[8,1,1,96,128]{4,0,3,2,1:T(8,128)(2,1)S(1)} %fusion.60), channel_id=1, source_target_pairs={{0,128},{64,192},{128,0},{192,64},{1,129},{65,193},{129,1},{193,65... | collective-permute-start | bytes 589832 | tf_op jit(solution)/shard_map/ppermute | solution.py:32
  98.4 1.0 copy.82
  99.5 3.4 %collective-permute-done.6 = bf16[8,1,1,96,128]{4,0,3,2,1:T(8,128)(2,1)S(1)} collective-permute-done((bf16[8,1,1,96,128]{4,0,3,2,1:T(8,128)(2,1)S(1)}, bf16[8,1,1,96,128]{4,0,3,2,1:T(8,128)(2,1)S(1)}, u32[]{:S(2)}, u32[]{:S(2)}) %collective-permute-start.6) | collective-permute-done | bytes 196640 | tf_op jit(solution)/shard_map/ppermute | solution.py:32
  102.9 0.8 pad_maximum_fusion.4
  103.7 1.3 collective-permute-start.7
  105.0 1.6 fusion.86
  106.6 2.1 %reshape.253 = bf16[16,24,768]{2,1,0:T(8,128)(2,1)S(1)} reshape(bf16[128,2,1152]{2,1,0:T(2,128)(2,1)} %get-tuple-element.6) | data formatting | bytes 1179648 | tf_op jit(solution)/shard_map/reshape | solution.py:110
  108.8 0.2 fusion.54
  109.1 0.7 copy-done.5
  109.8 2.0 %collective-permute-done.7 = bf16[8,2,1,96,128]{4,0,3,2,1:T(8,128)(2,1)} collective-permute-done((bf16[8,2,1,96,128]{4,0,3,2,1:T(8,128)(2,1)}, bf16[8,2,1,96,128]{4,0,3,2,1:T(8,128)(2,1)}, u32[]{:S(2)}, u32[]{:S(2)}) %collective-permute-start.7) | collective-permute-done | bytes 393248 | tf_op jit(solution)/shard_map/ppermute | solution.py:32
  111.8 1.1 broadcast_select_fusion.3
  113.2 1.2 reshape.252
  114.4 1.1 select_bitcast_fusion.1
  115.6 0.9 copy-done.3
  116.6 0.7 convolution_convert_fusion
  117.3 1.2 reshape.255
  118.4 16.3 %all-to-all-start.2 = ((bf16[128,2,1152]{2,1,0:T(2,128)(2,1)}), bf16[128,2,1152]{2,1,0:T(2,128)(2,1)S(1)}, u32[]{:S(2)}, u32[]{:S(2)}) async-start(bf16[128,2,1152]{2,1,0:T(2,128)(2,1)} %reshape.255), calls=%async_computation.2 | async-start | bytes 1179648 | tf_op jit(solution)/shard_map/all_to_all | solution.py:27
  134.8 0.2 fusion.31
  135.0 1.5 fusion.11
  136.6 1.2 broadcast_select_fusion.1
  138.0 0.3 copy.77
  138.2 18.9 %all-to-all-done.2 = bf16[128,2,1152]{2,1,0:T(2,128)(2,1)S(1)} async-done(((bf16[128,2,1152]{2,1,0:T(2,128)(2,1)}), bf16[128,2,1152]{2,1,0:T(2,128)(2,1)S(1)}, u32[]{:S(2)}, u32[]{:S(2)}) %all-to-all-start.2) | async-done | bytes 589856 | tf_op jit(solution)/shard_map/all_to_all | solution.py:27
  157.1 0.5 convert_reduce_fusion.2
  157.7 0.8 multiply_reduce_fusion
  158.7 1.2 copy-done.2
  159.8 0.4 convert_reduce_fusion
  160.5 0.3 convolution_bitcast_fusion
  160.9 0.5 fusion.39
  161.4 0.2 fusion.88
  161.6 0.7 fusion.19
  162.3 0.8 fusion.79
  163.5 24.6 %all_to_all.20 = bf16[8,16,2432]{2,1,0:T(8,128)(2,1)S(1)} all-to-all(bf16[8,16,2432]{2,1,0:T(8,128)(2,1)S(1)} %fusion.46), channel_id=1, replica_groups=mesh['x'=4,'zl'=4,'core'=2,'y'=4,'zh'=2] {'y','zh'}, dimensions={0} | all-to-all | bytes 1245184 | tf_op jit(solution)/shard_map/all_to_all | solution.py:27
  188.4 1.1 reshape.265
  189.4 0.6 reshape.266
  (98 shorter events, 3.6 us)
Async XLA Ops:
  0.6 13.5 %copy-start = (bf16[384,48]{0,1:T(8,128)(2,1)S(1)}, bf16[384,48]{0,1:T(8,128)(2,1)}, u32[]{:S(2)}) copy-start(bf16[384,48]{0,1:T(8,128)(2,1)} %param.27) | copy-start | bytes 110596
  2.0 11.3 %copy-start.6 = (bf16[24,384]{1,0:T(8,128)(2,1)S(1)}, bf16[24,384]{1,0:T(8,128)(2,1)}, u32[]{:S(2)}) copy-start(bf16[24,384]{1,0:T(8,128)(2,1)} %param.16) | copy-start | bytes 55300
  2.0 11.6 %copy-start.12 = (bf16[384,2,48]{0,2,1:T(8,128)(2,1)S(1)}, bf16[384,2,48]{0,2,1:T(8,128)(2,1)}, u32[]{:S(2)}) copy-start(bf16[384,2,48]{0,2,1:T(8,128)(2,1)} %param.28) | copy-start | bytes 221188
  2.1 11.6 %copy-start.16 = (f32[384]{0:T(512)S(1)}, f32[384]{0:T(512)}, u32[]{:S(2)}) copy-start(f32[384]{0:T(512)} %param.25) | copy-start | bytes 4612
  2.1 12.2 %copy-start.13 = (bf16[384,48]{0,1:T(8,128)(2,1)S(1)}, bf16[384,48]{0,1:T(8,128)(2,1)}, u32[]{:S(2)}) copy-start(bf16[384,48]{0,1:T(8,128)(2,1)} %param.26) | copy-start | bytes 110596
  3.0 11.7 %copy-start.7 = (bf16[48,384]{1,0:T(8,128)(2,1)S(1)}, bf16[48,384]{1,0:T(8,128)(2,1)}, u32[]{:S(2)}) copy-start(bf16[48,384]{1,0:T(8,128)(2,1)} %param.29) | copy-start | bytes 110596
  3.0 17.8 %copy-start.4 = (bf16[128,4,128]{2,1,0:T(4,128)(2,1)S(1)}, bf16[128,4,128]{2,1,0:T(4,128)(2,1)}, u32[]{:S(2)}) copy-start(bf16[128,4,128]{2,1,0:T(4,128)(2,1)} %param.19) | copy-start | bytes 393220
  3.0 18.1 %copy-start.9 = (s32[768]{0:T(1024)S(1)}, s32[768]{0:T(1024)}, u32[]{:S(2)}) copy-start(s32[768]{0:T(1024)} %param.17) | copy-start | bytes 9220
  3.0 37.9 %all-to-all-start = ((bf16[8,16,2304]{2,1,0:T(8,128)(2,1)}), bf16[8,16,2304]{2,1,0:T(8,128)(2,1)S(1)}, u32[]{:S(2)}, u32[]{:S(2)}) async-start(bf16[8,16,2304]{2,1,0:T(8,128)(2,1)} %bitcast.91), calls=%async_computation | async-start | bytes 1179648 | tf_op jit(solution)/shard_map/all_to_all | solution.py:27
  13.3 24.2 %copy-start.10 = (f32[128]{0:T(128)S(1)}, f32[128]{0:T(128)}, u32[]{:S(2)}) copy-start(f32[128]{0:T(128)} %param.18) | copy-start | bytes 1540
  14.8 21.9 %collective-permute-start.1 = (bf16[1,216,128]{2,0,1:T(2,128)(2,1)S(1)}, bf16[1,216,128]{2,0,1:T(2,128)(2,1)S(1)}, u32[]{:S(2)}, u32[]{:S(2)}) collective-permute-start(bf16[1,216,128]{2,0,1:T(2,128)(2,1)S(1)} %copy.74), channel_id=1, source_target_pairs={{0,1},{1,0},{2,3},{3,2},{4,5},{5,4},{6,7},{7,6},{8,9},{9,8},{10,11... | collective-permute-start | bytes 165896 | tf_op jit(solution)/shard_map/ppermute | solution.py:32
  37.1 3.8 %collective-permute-start.2 = (bf16[2,24,128]{2,0,1:T(2,128)(2,1)S(1)}, bf16[2,24,128]{2,0,1:T(2,128)(2,1)S(1)}, u32[]{:S(2)}, u32[]{:S(2)}) collective-permute-start(bf16[2,24,128]{2,0,1:T(2,128)(2,1)S(1)} %pad_maximum_fusion.8), channel_id=1, source_target_pairs={{0,16},{16,0},{32,48},{48,32},{1,17},{17,1},{33,49},{49,33},{2,18}... | collective-permute-start | bytes 36872 | tf_op jit(solution)/shard_map/ppermute | solution.py:32
  45.6 59.4 %all-to-all-start.1 = ((bf16[128,2,2304]{2,1,0:T(2,128)(2,1)}), bf16[128,2,2304]{2,1,0:T(2,128)(2,1)S(1)}, u32[]{:S(2)}, u32[]{:S(2)}) async-start(bf16[128,2,2304]{2,1,0:T(2,128)(2,1)} %pad_maximum_fusion.1), calls=%async_computation.1 | async-start | bytes 2359296 | tf_op jit(solution)/shard_map/all_to_all | solution.py:27
  55.8 23.7 %collective-permute-start.3 = (bf16[2,48,128]{2,0,1:T(2,128)(2,1)S(1)}, bf16[2,48,128]{2,0,1:T(2,128)(2,1)S(1)}, u32[]{:S(2)}, u32[]{:S(2)}) collective-permute-start(bf16[2,48,128]{2,0,1:T(2,128)(2,1)S(1)} %pad_maximum_fusion.7), channel_id=1, source_target_pairs={{0,32},{16,48},{32,0},{48,16},{1,33},{17,49},{33,1},{49,17},{2,34}... | collective-permute-start | bytes 73736 | tf_op jit(solution)/shard_map/ppermute | solution.py:32
  79.8 5.4 %collective-permute-start.4 = (bf16[2,288,128]{2,0,1:T(2,128)(2,1)S(1)}, bf16[2,288,128]{2,0,1:T(2,128)(2,1)S(1)}, u32[]{:S(2)}, u32[]{:S(2)}) collective-permute-start(bf16[2,288,128]{2,0,1:T(2,128)(2,1)S(1)} %fusion.62), channel_id=1, source_target_pairs={{0,2},{2,0},{4,6},{6,4},{1,3},{3,1},{5,7},{7,5},{8,10},{10,8},{12,... | collective-permute-start | bytes 442376 | tf_op jit(solution)/shard_map/ppermute | solution.py:32
  85.6 8.3 %collective-permute-start.5 = (bf16[4,288,128]{2,0,1:T(4,128)(2,1)S(1)}, bf16[4,288,128]{2,0,1:T(4,128)(2,1)S(1)}, u32[]{:S(2)}, u32[]{:S(2)}) collective-permute-start(bf16[4,288,128]{2,0,1:T(4,128)(2,1)S(1)} %pad_maximum_fusion.6), channel_id=1, source_target_pairs={{0,4},{2,6},{4,0},{6,2},{1,5},{3,7},{5,1},{7,3},{8,12},{10,14},{12... | collective-permute-start | bytes 884744 | tf_op jit(solution)/shard_map/ppermute | solution.py:32
  94.5 8.4 %collective-permute-start.6 = (bf16[8,1,1,96,128]{4,0,3,2,1:T(8,128)(2,1)S(1)}, bf16[8,1,1,96,128]{4,0,3,2,1:T(8,128)(2,1)S(1)}, u32[]{:S(2)}, u32[]{:S(2)}) collective-permute-start(bf16[8,1,1,96,128]{4,0,3,2,1:T(8,128)(2,1)S(1)} %fusion.60), channel_id=1, source_target_pairs={{0,128},{64,192},{128,0},{192,64},{1,129},{65,193},{129,1},{193,65... | collective-permute-start | bytes 589832 | tf_op jit(solution)/shard_map/ppermute | solution.py:32
  103.7 8.1 %collective-permute-start.7 = (bf16[8,2,1,96,128]{4,0,3,2,1:T(8,128)(2,1)}, bf16[8,2,1,96,128]{4,0,3,2,1:T(8,128)(2,1)}, u32[]{:S(2)}, u32[]{:S(2)}) collective-permute-start(bf16[8,2,1,96,128]{4,0,3,2,1:T(8,128)(2,1)} %pad_maximum_fusion.4), channel_id=1, source_target_pairs={{0,64},{64,0},{128,192},{192,128},{1,65},{65,1},{129,193},{193,129... | collective-permute-start | bytes 1179656 | tf_op jit(solution)/shard_map/ppermute | solution.py:32
  108.7 5.6 %collective-permute-start = (bf16[16,24,768]{2,1,0:T(8,128)(2,1)S(1)}, bf16[16,24,768]{2,1,0:T(8,128)(2,1)}, u32[]{:S(2)}, u32[]{:S(2)}) collective-permute-start(bf16[16,24,768]{2,1,0:T(8,128)(2,1)S(1)} %reshape.253), channel_id=1, source_target_pairs={{0,8},{8,0},{1,9},{9,1},{2,10},{10,2},{3,11},{11,3},{4,12},{12,4},... | collective-permute-start | bytes 1769480 | tf_op jit(solution)/shard_map/ppermute | solution.py:111
  109.1 0.7 copy-start.5
  113.1 23.5 %collective-permute-start.8 = (bf16[8,16,1,24,128]{4,3,1,0,2:T(8,128)(2,1)S(1)}, bf16[8,16,1,24,128]{4,3,1,0,2:T(8,128)(2,1)}, u32[]{:S(2)}, u32[]{:S(2)}) collective-permute-start(bf16[8,16,1,24,128]{4,3,1,0,2:T(8,128)(2,1)S(1)} %bitcast.107), channel_id=1, source_target_pairs={{0,8},{8,0},{1,9},{9,1},{2,10},{10,2},{3,11},{11,3},{4,12},{12,4},... | collective-permute-start | bytes 2359304 | tf_op jit(solution)/shard_map/ppermute | solution.py:32
  115.5 1.1 copy-start.3
  118.4 16.6 %copy-start.14 = (bf16[128,128]{1,0:T(8,128)(2,1)S(1)}, bf16[128,128]{1,0:T(8,128)(2,1)}, u32[]{:S(2)}) copy-start(bf16[128,128]{1,0:T(8,128)(2,1)} %param.20) | copy-start | bytes 98308
  118.4 38.7 %all-to-all-start.2 = ((bf16[128,2,1152]{2,1,0:T(2,128)(2,1)}), bf16[128,2,1152]{2,1,0:T(2,128)(2,1)S(1)}, u32[]{:S(2)}, u32[]{:S(2)}) async-start(bf16[128,2,1152]{2,1,0:T(2,128)(2,1)} %reshape.255), calls=%async_computation.2 | async-start | bytes 1179648 | tf_op jit(solution)/shard_map/all_to_all | solution.py:27
  157.7 1.0 copy-start.8
  157.7 1.0 copy-start.11
  158.6 1.3 copy-start.2
  159.8 0.7 copy-start.15
  159.8 0.7 copy-start.17
  161.6 1.6 copy-start.1

commit v4 on v3

--- a/solution.py
+++ b/solution.py
@@ -35,8 +35,8 @@
 
 
 def filled(*parts):
-    wide = jnp.concatenate(parts, axis=1)
-    return jnp.pad(wide, ((0, 0), (0, LANES - wide.shape[1])))
+    wide = jnp.concatenate(parts, axis=-1)
+    return jnp.pad(wide, [(0, 0)] * (wide.ndim - 1) + [(0, LANES - wide.shape[-1])])
 
 
 def edge(normed, w_gate, w_value, mask):
@@ -71,33 +71,37 @@
     core = lax.axis_index("core")
     live = token_mask.astype(F32)
 
+    local = w_query.shape[1]
+    weights = [w_query, w_key, w_value_gate[:, 0, :], w_value_gate[:, 1, :]]
+    weights = jnp.concatenate([w.T for w in weights] + [w_mix], axis=0)
+    weights = doubled(weights[None], "zh", 0, 0)
     single_normed = layer_norm(single.astype(F32), single_gain[None, :], 1).astype(BF)
-    own_keys = jnp.dot(single_normed, w_key, preferred_element_type=F32).astype(BF)
-    own_values = jnp.dot(single_normed, w_value_gate[:, 0, :], preferred_element_type=F32).astype(BF)
-    queries = jnp.dot(single_normed, w_query, preferred_element_type=F32).astype(BF)
-    head_gate = jax.nn.sigmoid(
-        jnp.dot(single_normed, w_value_gate[:, 1, :], preferred_element_type=F32)
+    projected = jnp.einsum(
+        "tf,zof->zto", single_normed, weights[:, : 4 * local], preferred_element_type=F32
     )
+    head_gate = jax.nn.sigmoid(projected[..., 3 * local :])
     gate_high = lax.reduce_precision(head_gate, 8, 7)
     gate_rest = (head_gate - gate_high).astype(BF)
-    local = w_query.shape[1]
-    kv = filled(own_keys, own_values)
+    kv = filled(projected[..., local : 3 * local].astype(BF))
     rest = jnp.concatenate(
-        [filled(queries, gate_high.astype(BF)), filled(gate_rest)]
-        + [w_mix[:, k : k + LANES] for k in range(0, D, LANES)]
+        [
+            filled(projected[..., :local].astype(BF), gate_high.astype(BF)),
+            filled(gate_rest),
+        ]
+        + [weights[:, 4 * local :, k : k + LANES] for k in range(0, D, LANES)],
+        axis=1,
     )
-    both = doubled(jnp.concatenate([kv, rest])[None], "zh", 0, 0)
-    kv, rest = both[:, :rows], both[:, rows:]
-    kv = doubled(kv, "zl", 0, 1)
-    kv = doubled(kv, "zl", 1, 1)
-    both = jnp.concatenate([kv, rest], axis=1)
-    both = doubled(both, "y", 0, 0)
-    both = doubled(both, "y", 1, 0)
-    kv, rest = both[:, : kv.shape[1]], both[:, kv.shape[1] :]
-    kv = doubled(kv[:, None, None], "x", 1, 1)
-    kv = doubled(kv, "x", 0, 2)
-    kv = doubled(kv.reshape(nq, -1, 1, rows, LANES), "core", 0, 2)
+    kv = kv[None, None, :, None, None, None, None, None]
+    kv = doubled(kv, "y", 1, 0)
+    kv = doubled(kv, "x", 1, 3)
+    kv = doubled(kv, "zl", 1, 5)
+    kv = doubled(kv, "zl", 0, 6)
+    kv = doubled(kv, "y", 0, 1)
+    kv = doubled(kv, "x", 0, 4)
+    kv = doubled(kv, "core", 0, 7)
     kv = kv.reshape(nq, -1, LANES)
+    rest = doubled(rest, "y", 0, 0)
+    rest = doubled(rest, "y", 1, 0)
 
     sent = pair.reshape(chans, nq, spots).transpose(1, 0, 2)
     full = swap(sent, CHAN).reshape(C, spots).astype(F32)

time: 191 us -> 187 us (0.979)
  waiting for transfers between devices: 73.7 us -> 61.6 us
  other arithmetic: 12.5 us -> 20.4 us
    ppermute x8 -> x10, waiting for transfers between devices: 54.8 us -> 42 us  [doubled(): there = lax.ppermute(block, axis, [(i, i ^ 1 << bit) for i in range(size)])]
    ppermute x8 -> x10, starting transfers between devices: 18.4 us -> 25.4 us  [doubled(): there = lax.ppermute(block, axis, [(i, i ^ 1 << bit) for i in range(size)])]
    all_to_all x3, starting transfers between devices: 36.8 us -> 30.2 us  [swap(): return lax.all_to_all(shard, axes, 0, 0, tiled=True)]
    concatenate x7 -> x11, other arithmetic: 1.75 us -> 6.94 us  [doubled(): jnp.concatenate([jnp.where(low, block, there), jnp.where(low, there, bloc...]
    select_n x7 -> x9, other arithmetic: 2.68 us -> 6.39 us  [doubled(): jnp.where(low, block, there)]
    unnamed x40 -> x36, local copies, waits for them, and re-layouts: 3.03 us -> 5.6 us
  transfers between devices with their start and end apart: 12 -> 14, of which waited for: 8 -> 8; matrix products, arithmetic and copies ran while one was open for 10% -> 16% of each run, Pallas kernels for 0% -> 0%
where the time goes in v4:
time: 187 us; the launch traced here: 186 us
  waiting for transfers between devices  61.6 us (33%)
  starting transfers between devices  55.7 us (30%)
  blocking collectives  24.6 us (13%)
  other arithmetic  20.4 us (11%)
  local copies, waits for them, and re-layouts  16.6 us (9%)
  matrix products  6.21 us (3%)
    ppermute x10, waiting for transfers between devices, doubled(): there = lax.ppermute(block, axis, [(i, i ^ 1 << bit) for i in range(size)])  42 us
    all_to_all x3, starting transfers between devices, swap(): return lax.all_to_all(shard, axes, 0, 0, tiled=True)  30.2 us
    ppermute x10, starting transfers between devices, doubled(): there = lax.ppermute(block, axis, [(i, i ^ 1 << bit) for i in range(size)])  25.4 us
    all_to_all x1, blocking collectives, swap(): return lax.all_to_all(shard, axes, 0, 0, tiled=True)  24.6 us
    all_to_all x3, waiting for transfers between devices, swap(): return lax.all_to_all(shard, axes, 0, 0, tiled=True)  19.6 us
    concatenate x11, other arithmetic, doubled(): jnp.concatenate([jnp.where(low, block, there), jnp.where(low, there, bloc...  6.94 us
    select_n x9, other arithmetic, doubled(): jnp.where(low, block, there)  6.39 us
    unnamed x36, local copies, waits for them, and re-layouts  5.6 us
  transfers between devices with their start and end apart: 14, of which 8 were waited for; matrix products, arithmetic and copies ran while one was open for 16% of the time, Pallas kernels for 0%

profile of v4, /device:TPU:32, one launch (start us, length us, event | category | flops | bytes accessed | tf_op | source)
XLA Modules:
  0.0 186.4 jit_solution(5809470093699867265)
XLA Ops:
  0.7 0.8 bitcast_dynamic-update-slice_fusion.3
  1.5 0.8 bitcast_dynamic-update-slice_fusion.2
  2.3 0.8 bitcast_dynamic-update-slice_fusion.1
  3.0 0.8 bitcast_dynamic-update-slice_fusion
  3.8 0.8 constant_dynamic-update-slice_fusion
  4.6 0.3 copy.96
  4.9 6.4 %collective-permute-start.1 = (bf16[1,240,384]{2,0,1:T(2,128)(2,1)S(1)}, bf16[1,240,384]{2,0,1:T(2,128)(2,1)S(1)}, u32[]{:S(2)}, u32[]{:S(2)}) collective-permute-start(bf16[1,240,384]{2,0,1:T(2,128)(2,1)S(1)} %copy.96), channel_id=1, source_target_pairs={{0,1},{1,0},{2,3},{3,2},{4,5},{5,4},{6,7},{7,6},{8,9},{9,8},{10,11... | collective-permute-start | bytes 552968 | tf_op jit(solution)/shard_map/ppermute | solution.py:32
  11.3 0.3 reshape.246
  11.6 0.9 copy.143
  12.5 4.5 %all-to-all-start = ((bf16[8,16,2304]{2,1,0:T(8,128)(2,1)}), bf16[8,16,2304]{2,1,0:T(8,128)(2,1)S(1)}, u32[]{:S(2)}, u32[]{:S(2)}) async-start(bf16[8,16,2304]{2,1,0:T(8,128)(2,1)} %bitcast.103), calls=%async_computation | async-start | bytes 1179648 | tf_op jit(solution)/shard_map/all_to_all | solution.py:27
  17.9 15.3 %collective-permute-done.1 = bf16[1,240,384]{2,0,1:T(2,128)(2,1)S(1)} collective-permute-done((bf16[1,240,384]{2,0,1:T(2,128)(2,1)S(1)}, bf16[1,240,384]{2,0,1:T(2,128)(2,1)S(1)}, u32[]{:S(2)}, u32[]{:S(2)}) %collective-permute-start.1) | collective-permute-done | bytes 184352 | tf_op jit(solution)/shard_map/ppermute | solution.py:32
  33.3 0.8 broadcast_select_fusion.5
  34.0 0.7 slice_maximum_fusion
  35.2 3.3 %collective-permute-start.4 = (bf16[1,1,2,1,1,1,1,1,24,128]{9,2,8,7,6,5,4,3,1,0:T(2,128)(2,1)S(1)}, bf16[1,1,2,1,1,1,1,1,24,128]{9,2,8,7,6,5,4,3,1,0:T(2,128)(2,1)S(1)}, u32[]{:S(2)}, u32[]{:S(2)}) collective-permute-start(bf16[1,1,2,1,1,1,1,1,24,128]{9,2,8,7,6,5,4,3,1,0:T(2,128)(2,1)S(1)} %pad_bitcast_fusion), channel_id=1, source_target_pairs={{0,4},{2,6},{4,0},{6,2},{1,5},{3,7},{5,1},{7,3},{8,12},{10,14},{12... | collective-permute-start | bytes 36872 | tf_op jit(solution)/shard_map/ppermute | solution.py:32
  38.8 4.2 %all-to-all-done = bf16[8,16,2304]{2,1,0:T(8,128)(2,1)S(1)} async-done(((bf16[8,16,2304]{2,1,0:T(8,128)(2,1)}), bf16[8,16,2304]{2,1,0:T(8,128)(2,1)S(1)}, u32[]{:S(2)}, u32[]{:S(2)}) %all-to-all-start) | async-done | bytes 589856 | tf_op jit(solution)/shard_map/all_to_all | solution.py:27
  43.5 0.5 fusion.8
  44.1 0.4 fusion.18
  44.6 0.5 fusion.5
  45.1 0.4 fusion.17
  45.6 2.1 %pad_maximum_fusion.1 = bf16[128,2,2304]{2,1,0:T(2,128)(2,1)} fusion(bf16[128,2,1152]{2,1,0:T(2,128)(2,1)S(1)} %reshape.248, bf16[128,2,1152]{2,1,0:T(2,128)(2,1)S(1)} %reshape.247), kind=kLoop, calls=%fused_computation.43 | loop fusion | flops 2359296 | bytes 2359296 | tf_op jit(solution)/shard_map/concatenate | solution.py:113
  47.7 11.3 %all-to-all-start.1 = ((bf16[128,2,2304]{2,1,0:T(2,128)(2,1)}), bf16[128,2,2304]{2,1,0:T(2,128)(2,1)S(1)}, u32[]{:S(2)}, u32[]{:S(2)}) async-start(bf16[128,2,2304]{2,1,0:T(2,128)(2,1)} %pad_maximum_fusion.1), calls=%async_computation.1 | async-start | bytes 2359296 | tf_op jit(solution)/shard_map/all_to_all | solution.py:27
  59.1 3.4 %collective-permute-start.5 = (bf16[2,1,2,1,1,1,1,1,24,128]{9,2,8,7,6,5,4,3,1,0:T(2,128)(2,1)S(1)}, bf16[2,1,2,1,1,1,1,1,24,128]{9,2,8,7,6,5,4,3,1,0:T(2,128)(2,1)S(1)}, u32[]{:S(2)}, u32[]{:S(2)}) collective-permute-start(bf16[2,1,2,1,1,1,1,1,24,128]{9,2,8,7,6,5,4,3,1,0:T(2,128)(2,1)S(1)} %pad_maximum_fusion.11), channel_id=1, source_target_pairs={{0,128},{64,192},{128,0},{192,64},{1,129},{65,193},{129,1},{193,65... | collective-permute-start | bytes 73736 | tf_op jit(solution)/shard_map/ppermute | solution.py:32
  62.6 2.2 %collective-permute-done.5 = bf16[2,1,2,1,1,1,1,1,24,128]{9,2,8,7,6,5,4,3,1,0:T(2,128)(2,1)S(1)} collective-permute-done((bf16[2,1,2,1,1,1,1,1,24,128]{9,2,8,7,6,5,4,3,1,0:T(2,128)(2,1)S(1)}, bf16[2,1,2,1,1,1,1,1,24,128]{9,2,8,7,6,5,4,3,1,0:T(2,128)(2,1)S(1)}, u32[]{:S(2)}, u32[]{:S(2)}) %collective-permute-start.5) | collective-permute-done | bytes 24608 | tf_op jit(solution)/shard_map/ppermute | solution.py:32
  64.9 2.7 %collective-permute-start.6 = (bf16[2,1,2,2,1,1,1,1,24,128]{9,2,8,7,6,5,4,3,1,0:T(2,128)(2,1)S(1)}, bf16[2,1,2,2,1,1,1,1,24,128]{9,2,8,7,6,5,4,3,1,0:T(2,128)(2,1)S(1)}, u32[]{:S(2)}, u32[]{:S(2)}) collective-permute-start(bf16[2,1,2,2,1,1,1,1,24,128]{9,2,8,7,6,5,4,3,1,0:T(2,128)(2,1)S(1)} %pad_maximum_fusion.9), channel_id=1, source_target_pairs={{0,32},{16,48},{32,0},{48,16},{1,33},{17,49},{33,1},{49,17},{2,34}... | collective-permute-start | bytes 147464 | tf_op jit(solution)/shard_map/ppermute | solution.py:32
  67.7 1.7 collective-permute-start.2
  69.4 15.6 %collective-permute-done.6 = bf16[2,1,2,2,1,1,1,1,24,128]{9,2,8,7,6,5,4,3,1,0:T(2,128)(2,1)S(1)} collective-permute-done((bf16[2,1,2,2,1,1,1,1,24,128]{9,2,8,7,6,5,4,3,1,0:T(2,128)(2,1)S(1)}, bf16[2,1,2,2,1,1,1,1,24,128]{9,2,8,7,6,5,4,3,1,0:T(2,128)(2,1)S(1)}, u32[]{:S(2)}, u32[]{:S(2)}) %collective-permute-start.6) | collective-permute-done | bytes 49184 | tf_op jit(solution)/shard_map/ppermute | solution.py:32
  85.3 2.6 %collective-permute-start.7 = (bf16[2,1,2,2,1,2,1,1,24,128]{9,2,8,7,6,5,4,3,1,0:T(2,128)(2,1)S(1)}, bf16[2,1,2,2,1,2,1,1,24,128]{9,2,8,7,6,5,4,3,1,0:T(2,128)(2,1)S(1)}, u32[]{:S(2)}, u32[]{:S(2)}) collective-permute-start(bf16[2,1,2,2,1,2,1,1,24,128]{9,2,8,7,6,5,4,3,1,0:T(2,128)(2,1)S(1)} %pad_maximum_fusion.8), channel_id=1, source_target_pairs={{0,16},{16,0},{32,48},{48,32},{1,17},{17,1},{33,49},{49,33},{2,18}... | collective-permute-start | bytes 294920 | tf_op jit(solution)/shard_map/ppermute | solution.py:32
  88.1 3.0 %collective-permute-start.3 = (bf16[4,192,128]{2,0,1:T(4,128)(2,1)S(1)}, bf16[4,192,128]{2,0,1:T(4,128)(2,1)S(1)}, u32[]{:S(2)}, u32[]{:S(2)}) collective-permute-start(bf16[4,192,128]{2,0,1:T(4,128)(2,1)S(1)} %pad_maximum_fusion.6), channel_id=1, source_target_pairs={{0,4},{2,6},{4,0},{6,2},{1,5},{3,7},{5,1},{7,3},{8,12},{10,14},{12... | collective-permute-start | bytes 589832 | tf_op jit(solution)/shard_map/ppermute | solution.py:32
  91.1 0.2 broadcast_select_fusion.9
  91.3 0.3 pad_maximum_fusion.7
  91.6 0.8 collective-permute-start.8
  92.4 4.9 %collective-permute-done.3 = bf16[4,192,128]{2,0,1:T(4,128)(2,1)S(1)} collective-permute-done((bf16[4,192,128]{2,0,1:T(4,128)(2,1)S(1)}, bf16[4,192,128]{2,0,1:T(4,128)(2,1)S(1)}, u32[]{:S(2)}, u32[]{:S(2)}) %collective-permute-start.3) | collective-permute-done | bytes 196640 | tf_op jit(solution)/shard_map/ppermute | solution.py:32
  97.4 0.3 broadcast_select_fusion.12
  97.7 0.6 collective-permute-done.8
  98.3 0.4 broadcast_select_fusion.7
  98.7 1.3 pad_maximum_fusion.4
  100.0 1.5 collective-permute-start.9
  101.5 1.6 fusion.80
  103.2 0.4 reshape.250
  103.8 1.0 copy.105
  104.8 3.3 %collective-permute-done.9 = bf16[2,2,2,2,1,2,2,1,24,128]{9,2,8,7,6,5,4,3,1,0:T(2,128)(2,1)} collective-permute-done((bf16[2,2,2,2,1,2,2,1,24,128]{9,2,8,7,6,5,4,3,1,0:T(2,128)(2,1)}, bf16[2,2,2,2,1,2,2,1,24,128]{9,2,8,7,6,5,4,3,1,0:T(2,128)(2,1)}, u32[]{:S(2)}, u32[]{:S(2)}) %collective-permute-start.9) | collective-permute-done | bytes 393248 | tf_op jit(solution)/shard_map/ppermute | solution.py:32
  108.1 1.9 %broadcast_select_fusion.3 = (bf16[2,2,2,2,1,2,2,1,24,128]{9,2,8,7,6,5,4,3,1,0:T(2,128)(2,1)S(1)}, bf16[2,2,2,2,1,2,2,1,24,128]{9,2,8,7,6,5,4,3,1,0:T(2,128)(2,1)S(1)}) fusion(bf16[2,2,2,2,1,2,2,1,24,128]{9,2,8,7,6,5,4,3,1,0:T(2,128)(2,1)} %collective-permute-done.9, pred[]{:T(512)S(6)} %eq.56, ...), kind=kLoop, calls=%fused_computation.62 | loop fusion | flops 589824 | bytes 1572865 | tf_op jit(solution)/shard_map/jit(_where)/select_n | solution.py:34
  110.0 2.0 %pad_maximum_fusion.3 = bf16[2,2,2,2,2,2,2,1,24,128]{9,2,8,7,6,5,4,3,1,0:T(2,128)(2,1)} fusion(bf16[2,2,2,2,1,2,2,1,24,128]{9,2,8,7,6,5,4,3,1,0:T(2,128)(2,1)S(1)} %get-tuple-element.11, bf16[2,2,2,2,1,2,2,1,24,128]{9,2,8,7,6,5,4,3,1,0:T(2,128)(2,1)S(1)} %get-tuple-element.10), kind=kLoop, calls=%fused_computation.60 | loop fusion | flops 393216 | bytes 1572864 | tf_op jit(solution)/shard_map/concatenate | solution.py:34
  112.0 1.2 reshape.249
  113.2 1.1 select_bitcast_fusion.1
  114.5 0.9 copy-done.5
  115.4 0.7 convolution_convert_fusion
  116.1 1.2 reshape.252
  117.3 14.5 %all-to-all-start.2 = ((bf16[128,2,1152]{2,1,0:T(2,128)(2,1)}), bf16[128,2,1152]{2,1,0:T(2,128)(2,1)S(1)}, u32[]{:S(2)}, u32[]{:S(2)}) async-start(bf16[128,2,1152]{2,1,0:T(2,128)(2,1)} %reshape.252), calls=%async_computation.2 | async-start | bytes 1179648 | tf_op jit(solution)/shard_map/all_to_all | solution.py:27
  132.0 1.5 fusion.11
  133.5 2.8 %broadcast_select_fusion.1 = (bf16[2,2,2,2,2,2,2,1,24,128]{9,2,8,7,6,5,4,3,1,0:T(2,128)(2,1)S(1)}, bf16[2,2,2,2,2,2,2,1,24,128]{9,2,8,7,6,5,4,3,1,0:T(2,128)(2,1)S(1)}) fusion(bf16[2,2,2,2,2,2,2,1,24,128]{9,2,8,7,6,5,4,3,1,0:T(2,128)(2,1)} %collective-permute-done.10, pred[]{:T(512)S(6)} %eq.55, ...), kind=kLoop, calls=%fused_computation.32 | loop fusion | flops 1179648 | bytes 3145729 | tf_op jit(solution)/shard_map/jit(_where)/select_n | solution.py:34
  136.4 2.1 %pad_maximum_fusion = bf16[2,2,2,2,2,2,2,2,24,128]{9,2,8,7,6,5,4,3,1,0:T(2,128)(2,1)S(1)} fusion(bf16[2,2,2,2,2,2,2,1,24,128]{9,2,8,7,6,5,4,3,1,0:T(2,128)(2,1)S(1)} %get-tuple-element.5, bf16[2,2,2,2,2,2,2,1,24,128]{9,2,8,7,6,5,4,3,1,0:T(2,128)(2,1)S(1)} %get-tuple-element.4), kind=kLoop, calls=%fused_computation.30 | loop fusion | flops 786432 | bytes 3145728 | tf_op jit(solution)/shard_map/concatenate | solution.py:34
  138.4 0.3 copy.100
  138.8 15.3 %all-to-all-done.2 = bf16[128,2,1152]{2,1,0:T(2,128)(2,1)S(1)} async-done(((bf16[128,2,1152]{2,1,0:T(2,128)(2,1)}), bf16[128,2,1152]{2,1,0:T(2,128)(2,1)S(1)}, u32[]{:S(2)}, u32[]{:S(2)}) %all-to-all-start.2) | async-done | bytes 589856 | tf_op jit(solution)/shard_map/all_to_all | solution.py:27
  154.1 0.5 convert_reduce_fusion.2
  154.7 0.8 multiply_reduce_fusion
  155.6 1.2 copy-done.3
  156.8 0.4 convert_reduce_fusion
  157.5 0.3 convolution_bitcast_fusion
  157.8 0.5 fusion.39
  158.6 0.7 fusion.19
  159.9 24.6 %all_to_all.20 = bf16[8,16,2432]{2,1,0:T(8,128)(2,1)S(1)} all-to-all(bf16[8,16,2432]{2,1,0:T(8,128)(2,1)S(1)} %fusion.43), channel_id=1, replica_groups=mesh['x'=4,'zl'=4,'core'=2,'y'=4,'zh'=2] {'y','zh'}, dimensions={0} | all-to-all | bytes 1245184 | tf_op jit(solution)/shard_map/all_to_all | solution.py:27
  184.7 1.1 reshape.261
  185.8 0.6 reshape.262
  (105 shorter events, 5.2 us)
Async XLA Ops:
  0.6 155.0 %copy-start = (bf16[128,128]{1,0:T(8,128)(2,1)S(1)}, bf16[128,128]{1,0:T(8,128)(2,1)}, u32[]{:S(2)}) copy-start(bf16[128,128]{1,0:T(8,128)(2,1)} %param.22) | copy-start | bytes 98308
  0.6 10.6 %copy-start.4 = (bf16[16,24,768]{2,1,0:T(8,128)(2,1)S(1)}, bf16[16,24,768]{2,1,0:T(8,128)(2,1)}, u32[]{:S(2)}) copy-start(bf16[16,24,768]{2,1,0:T(8,128)(2,1)} %param.15) | copy-start | bytes 1769476
  4.9 28.4 %collective-permute-start.1 = (bf16[1,240,384]{2,0,1:T(2,128)(2,1)S(1)}, bf16[1,240,384]{2,0,1:T(2,128)(2,1)S(1)}, u32[]{:S(2)}, u32[]{:S(2)}) collective-permute-start(bf16[1,240,384]{2,0,1:T(2,128)(2,1)S(1)} %copy.96), channel_id=1, source_target_pairs={{0,1},{1,0},{2,3},{3,2},{4,5},{5,4},{6,7},{7,6},{8,9},{9,8},{10,11... | collective-permute-start | bytes 552968 | tf_op jit(solution)/shard_map/ppermute | solution.py:32
  11.6 5.5 %copy-start.8 = (s32[768]{0:T(1024)S(1)}, s32[768]{0:T(1024)}, u32[]{:S(2)}) copy-start(s32[768]{0:T(1024)} %param.17) | copy-start | bytes 9220
  11.6 5.5 %copy-start.7 = (bf16[24,384]{1,0:T(8,128)(2,1)S(1)}, bf16[24,384]{1,0:T(8,128)(2,1)}, u32[]{:S(2)}) copy-start(bf16[24,384]{1,0:T(8,128)(2,1)} %param.16) | copy-start | bytes 55300
  11.6 6.0 %copy-start.9 = (f32[128]{0:T(128)S(1)}, f32[128]{0:T(128)}, u32[]{:S(2)}) copy-start(f32[128]{0:T(128)} %param.18) | copy-start | bytes 1540
  11.6 6.1 %copy-start.6 = (bf16[128,4,128]{2,1,0:T(4,128)(2,1)S(1)}, bf16[128,4,128]{2,1,0:T(4,128)(2,1)}, u32[]{:S(2)}) copy-start(bf16[128,4,128]{2,1,0:T(4,128)(2,1)} %param.19) | copy-start | bytes 393220
  12.5 30.5 %all-to-all-start = ((bf16[8,16,2304]{2,1,0:T(8,128)(2,1)}), bf16[8,16,2304]{2,1,0:T(8,128)(2,1)S(1)}, u32[]{:S(2)}, u32[]{:S(2)}) async-start(bf16[8,16,2304]{2,1,0:T(8,128)(2,1)} %bitcast.103), calls=%async_computation | async-start | bytes 1179648 | tf_op jit(solution)/shard_map/all_to_all | solution.py:27
  17.9 16.8 %copy-start.13 = (f32[384]{0:T(512)S(1)}, f32[384]{0:T(512)}, u32[]{:S(2)}) copy-start(f32[384]{0:T(512)} %param.25) | copy-start | bytes 4612
  35.2 23.8 %collective-permute-start.4 = (bf16[1,1,2,1,1,1,1,1,24,128]{9,2,8,7,6,5,4,3,1,0:T(2,128)(2,1)S(1)}, bf16[1,1,2,1,1,1,1,1,24,128]{9,2,8,7,6,5,4,3,1,0:T(2,128)(2,1)S(1)}, u32[]{:S(2)}, u32[]{:S(2)}) collective-permute-start(bf16[1,1,2,1,1,1,1,1,24,128]{9,2,8,7,6,5,4,3,1,0:T(2,128)(2,1)S(1)} %pad_bitcast_fusion), channel_id=1, source_target_pairs={{0,4},{2,6},{4,0},{6,2},{1,5},{3,7},{5,1},{7,3},{8,12},{10,14},{12... | collective-permute-start | bytes 36872 | tf_op jit(solution)/shard_map/ppermute | solution.py:32
  47.7 53.8 %all-to-all-start.1 = ((bf16[128,2,2304]{2,1,0:T(2,128)(2,1)}), bf16[128,2,2304]{2,1,0:T(2,128)(2,1)S(1)}, u32[]{:S(2)}, u32[]{:S(2)}) async-start(bf16[128,2,2304]{2,1,0:T(2,128)(2,1)} %pad_maximum_fusion.1), calls=%async_computation.1 | async-start | bytes 2359296 | tf_op jit(solution)/shard_map/all_to_all | solution.py:27
  59.1 5.7 %collective-permute-start.5 = (bf16[2,1,2,1,1,1,1,1,24,128]{9,2,8,7,6,5,4,3,1,0:T(2,128)(2,1)S(1)}, bf16[2,1,2,1,1,1,1,1,24,128]{9,2,8,7,6,5,4,3,1,0:T(2,128)(2,1)S(1)}, u32[]{:S(2)}, u32[]{:S(2)}) collective-permute-start(bf16[2,1,2,1,1,1,1,1,24,128]{9,2,8,7,6,5,4,3,1,0:T(2,128)(2,1)S(1)} %pad_maximum_fusion.11), channel_id=1, source_target_pairs={{0,128},{64,192},{128,0},{192,64},{1,129},{65,193},{129,1},{193,65... | collective-permute-start | bytes 73736 | tf_op jit(solution)/shard_map/ppermute | solution.py:32
  64.9 20.1 %collective-permute-start.6 = (bf16[2,1,2,2,1,1,1,1,24,128]{9,2,8,7,6,5,4,3,1,0:T(2,128)(2,1)S(1)}, bf16[2,1,2,2,1,1,1,1,24,128]{9,2,8,7,6,5,4,3,1,0:T(2,128)(2,1)S(1)}, u32[]{:S(2)}, u32[]{:S(2)}) collective-permute-start(bf16[2,1,2,2,1,1,1,1,24,128]{9,2,8,7,6,5,4,3,1,0:T(2,128)(2,1)S(1)} %pad_maximum_fusion.9), channel_id=1, source_target_pairs={{0,32},{16,48},{32,0},{48,16},{1,33},{17,49},{33,1},{49,17},{2,34}... | collective-permute-start | bytes 147464 | tf_op jit(solution)/shard_map/ppermute | solution.py:32
  67.7 20.2 %collective-permute-start.2 = (bf16[2,192,128]{2,0,1:T(2,128)(2,1)S(1)}, bf16[2,192,128]{2,0,1:T(2,128)(2,1)S(1)}, u32[]{:S(2)}, u32[]{:S(2)}) collective-permute-start(bf16[2,192,128]{2,0,1:T(2,128)(2,1)S(1)} %fusion.62), channel_id=1, source_target_pairs={{0,2},{2,0},{4,6},{6,4},{1,3},{3,1},{5,7},{7,5},{8,10},{10,8},{12,... | collective-permute-start | bytes 294920 | tf_op jit(solution)/shard_map/ppermute | solution.py:32
  85.3 5.8 %collective-permute-start.7 = (bf16[2,1,2,2,1,2,1,1,24,128]{9,2,8,7,6,5,4,3,1,0:T(2,128)(2,1)S(1)}, bf16[2,1,2,2,1,2,1,1,24,128]{9,2,8,7,6,5,4,3,1,0:T(2,128)(2,1)S(1)}, u32[]{:S(2)}, u32[]{:S(2)}) collective-permute-start(bf16[2,1,2,2,1,2,1,1,24,128]{9,2,8,7,6,5,4,3,1,0:T(2,128)(2,1)S(1)} %pad_maximum_fusion.8), channel_id=1, source_target_pairs={{0,16},{16,0},{32,48},{48,32},{1,17},{17,1},{33,49},{49,33},{2,18}... | collective-permute-start | bytes 294920 | tf_op jit(solution)/shard_map/ppermute | solution.py:32
  88.1 9.2 %collective-permute-start.3 = (bf16[4,192,128]{2,0,1:T(4,128)(2,1)S(1)}, bf16[4,192,128]{2,0,1:T(4,128)(2,1)S(1)}, u32[]{:S(2)}, u32[]{:S(2)}) collective-permute-start(bf16[4,192,128]{2,0,1:T(4,128)(2,1)S(1)} %pad_maximum_fusion.6), channel_id=1, source_target_pairs={{0,4},{2,6},{4,0},{6,2},{1,5},{3,7},{5,1},{7,3},{8,12},{10,14},{12... | collective-permute-start | bytes 589832 | tf_op jit(solution)/shard_map/ppermute | solution.py:32
  91.6 6.7 %collective-permute-start.8 = (bf16[2,1,2,2,1,2,2,1,24,128]{9,2,8,7,6,5,4,3,1,0:T(2,128)(2,1)S(1)}, bf16[2,1,2,2,1,2,2,1,24,128]{9,2,8,7,6,5,4,3,1,0:T(2,128)(2,1)S(1)}, u32[]{:S(2)}, u32[]{:S(2)}) collective-permute-start(bf16[2,1,2,2,1,2,2,1,24,128]{9,2,8,7,6,5,4,3,1,0:T(2,128)(2,1)S(1)} %pad_maximum_fusion.7), channel_id=1, source_target_pairs={{0,2},{2,0},{4,6},{6,4},{1,3},{3,1},{5,7},{7,5},{8,10},{10,8},{12,... | collective-permute-start | bytes 589832 | tf_op jit(solution)/shard_map/ppermute | solution.py:32
  100.0 8.1 %collective-permute-start.9 = (bf16[2,2,2,2,1,2,2,1,24,128]{9,2,8,7,6,5,4,3,1,0:T(2,128)(2,1)}, bf16[2,2,2,2,1,2,2,1,24,128]{9,2,8,7,6,5,4,3,1,0:T(2,128)(2,1)}, u32[]{:S(2)}, u32[]{:S(2)}) collective-permute-start(bf16[2,2,2,2,1,2,2,1,24,128]{9,2,8,7,6,5,4,3,1,0:T(2,128)(2,1)} %pad_maximum_fusion.4), channel_id=1, source_target_pairs={{0,64},{64,0},{128,192},{192,128},{1,65},{65,1},{129,193},{193,129... | collective-permute-start | bytes 1179656 | tf_op jit(solution)/shard_map/ppermute | solution.py:32
  103.5 9.7 %collective-permute-start = (bf16[16,24,768]{2,1,0:T(8,128)(2,1)S(1)}, bf16[16,24,768]{2,1,0:T(8,128)(2,1)}, u32[]{:S(2)}, u32[]{:S(2)}) collective-permute-start(bf16[16,24,768]{2,1,0:T(8,128)(2,1)S(1)} %reshape.250), channel_id=1, source_target_pairs={{0,8},{8,0},{1,9},{9,1},{2,10},{10,2},{3,11},{11,3},{4,12},{12,4},... | collective-permute-start | bytes 1769480 | tf_op jit(solution)/shard_map/ppermute | solution.py:115
  110.0 2.0 %copy-start.1 = (bf16[128,2,1152]{2,1,0:T(2,128)(2,1)S(1)}, bf16[128,2,1152]{2,1,0:T(2,128)(2,1)}, u32[]{:S(2)}) copy-start(bf16[128,2,1152]{2,1,0:T(2,128)(2,1)} %get-tuple-element.9) | copy-start | bytes 1769476
  112.0 21.5 %collective-permute-start.10 = (bf16[2,2,2,2,2,2,2,1,24,128]{9,2,8,7,6,5,4,3,1,0:T(2,128)(2,1)}, bf16[2,2,2,2,2,2,2,1,24,128]{9,2,8,7,6,5,4,3,1,0:T(2,128)(2,1)}, u32[]{:S(2)}, u32[]{:S(2)}) collective-permute-start(bf16[2,2,2,2,2,2,2,1,24,128]{9,2,8,7,6,5,4,3,1,0:T(2,128)(2,1)} %pad_maximum_fusion.3), channel_id=1, source_target_pairs={{0,8},{8,0},{1,9},{9,1},{2,10},{10,2},{3,11},{11,3},{4,12},{12,4},... | collective-permute-start | bytes 2359304 | tf_op jit(solution)/shard_map/ppermute | solution.py:32
  114.4 1.1 copy-start.5
  117.3 14.7 %copy-start.11 = (bf16[128,128]{1,0:T(8,128)(2,1)S(1)}, bf16[128,128]{1,0:T(8,128)(2,1)}, u32[]{:S(2)}) copy-start(bf16[128,128]{1,0:T(8,128)(2,1)} %param.20) | copy-start | bytes 98308
  117.3 36.8 %all-to-all-start.2 = ((bf16[128,2,1152]{2,1,0:T(2,128)(2,1)}), bf16[128,2,1152]{2,1,0:T(2,128)(2,1)S(1)}, u32[]{:S(2)}, u32[]{:S(2)}) async-start(bf16[128,2,1152]{2,1,0:T(2,128)(2,1)} %reshape.252), calls=%async_computation.2 | async-start | bytes 1179648 | tf_op jit(solution)/shard_map/all_to_all | solution.py:27
  154.7 1.0 copy-start.10
  155.5 1.3 copy-start.3
  156.8 0.7 copy-start.12
  156.8 0.7 copy-start.14
  158.6 1.0 copy-start.2

commit v5 on v3

--- a/solution.py
+++ b/solution.py
@@ -35,8 +35,8 @@
 
 
 def filled(*parts):
-    wide = jnp.concatenate(parts, axis=1)
-    return jnp.pad(wide, ((0, 0), (0, LANES - wide.shape[1])))
+    wide = jnp.concatenate(parts, axis=-1)
+    return jnp.pad(wide, [(0, 0)] * (wide.ndim - 1) + [(0, LANES - wide.shape[-1])])
 
 
 def edge(normed, w_gate, w_value, mask):
@@ -71,6 +71,7 @@
     core = lax.axis_index("core")
     live = token_mask.astype(F32)
 
+    local = w_query.shape[1]
     single_normed = layer_norm(single.astype(F32), single_gain[None, :], 1).astype(BF)
     own_keys = jnp.dot(single_normed, w_key, preferred_element_type=F32).astype(BF)
     own_values = jnp.dot(single_normed, w_value_gate[:, 0, :], preferred_element_type=F32).astype(BF)
@@ -80,24 +81,26 @@
     )
     gate_high = lax.reduce_precision(head_gate, 8, 7)
     gate_rest = (head_gate - gate_high).astype(BF)
-    local = w_query.shape[1]
-    kv = filled(own_keys, own_values)
     rest = jnp.concatenate(
         [filled(queries, gate_high.astype(BF)), filled(gate_rest)]
         + [w_mix[:, k : k + LANES] for k in range(0, D, LANES)]
     )
+    kv = filled(own_keys, own_values)[None, None, None]
+    kv = doubled(kv, "y", 1, 0)
+    kv = doubled(kv, "x", 1, 1)
+    kv = doubled(kv, "zl", 1, 2)
+    kv = kv.reshape(-1, LANES)
+    split = kv.shape[0]
     both = doubled(jnp.concatenate([kv, rest])[None], "zh", 0, 0)
-    kv, rest = both[:, :rows], both[:, rows:]
-    kv = doubled(kv, "zl", 0, 1)
-    kv = doubled(kv, "zl", 1, 1)
-    both = jnp.concatenate([kv, rest], axis=1)
-    both = doubled(both, "y", 0, 0)
-    both = doubled(both, "y", 1, 0)
-    kv, rest = both[:, : kv.shape[1]], both[:, kv.shape[1] :]
-    kv = doubled(kv[:, None, None], "x", 1, 1)
-    kv = doubled(kv, "x", 0, 2)
-    kv = doubled(kv.reshape(nq, -1, 1, rows, LANES), "core", 0, 2)
+    kv = both[:, :split].reshape(2, 2, 1, 2, 1, 2, 1, 1, rows, LANES)
+    rest = both[:, split:]
+    kv = doubled(kv, "y", 0, 2)
+    kv = doubled(kv, "x", 0, 4)
+    kv = doubled(kv, "zl", 0, 6)
+    kv = doubled(kv, "core", 0, 7)
     kv = kv.reshape(nq, -1, LANES)
+    rest = doubled(rest[:, None, None], "y", 0, 2)
+    rest = doubled(rest, "y", 1, 1).reshape(nq, -1, LANES)
 
     sent = pair.reshape(chans, nq, spots).transpose(1, 0, 2)
     full = swap(sent, CHAN).reshape(C, spots).astype(F32)
@@ -130,7 +133,8 @@
     update = jnp.einsum("cp,cd->dp", product_normed, w_tri_out, preferred_element_type=F32)
     renewed = (full + out_gate * update).astype(BF)
     bias_input = layer_norm(renewed.astype(F32), bias_gain[:, None], 0).astype(BF)
-    bias = jnp.einsum("cp,ch->hp", bias_input, w_bias, preferred_element_type=F32)
+    by_head = w_bias.reshape(C, nq // 2, 2, -1).transpose(0, 2, 1, 3).reshape(w_bias.shape)
+    bias = jnp.einsum("cp,ch->hp", bias_input, by_head, preferred_element_type=F32)
 
     heads = H // nq
     head_size = D // H

time: 191 us -> 174 us (0.911)
  waiting for transfers between devices: 73.7 us -> 62.9 us
  local copies, waits for them, and re-layouts: 15.8 us -> 11.8 us
    ppermute x8 -> x10, waiting for transfers between devices: 54.8 us -> 41.8 us  [doubled(): there = lax.ppermute(block, axis, [(i, i ^ 1 << bit) for i in range(size)])]
    all_to_all x3, starting transfers between devices: 36.8 us -> 32.3 us  [swap(): return lax.all_to_all(shard, axes, 0, 0, tiled=True)]
    ppermute x8 -> x10, starting transfers between devices: 18.4 us -> 21.5 us  [doubled(): there = lax.ppermute(block, axis, [(i, i ^ 1 << bit) for i in range(size)])]
    all_to_all x3, waiting for transfers between devices: 18.9 us -> 21.1 us  [swap(): return lax.all_to_all(shard, axes, 0, 0, tiled=True)]
  transfers between devices with their start and end apart: 12 -> 14, of which waited for: 8 -> 11; matrix products, arithmetic and copies ran while one was open for 10% -> 8% of each run, Pallas kernels for 0% -> 0%
where the time goes in v5:
time: 174 us; the launch traced here: 173 us
  waiting for transfers between devices  62.9 us (36%)
  starting transfers between devices  53.9 us (31%)
  blocking collectives  24.6 us (14%)
  local copies, waits for them, and re-layouts  11.8 us (7%)
  other arithmetic  11.8 us (7%)
  matrix products  6.86 us (4%)
    ppermute x10, waiting for transfers between devices, doubled(): there = lax.ppermute(block, axis, [(i, i ^ 1 << bit) for i in range(size)])  41.8 us
    all_to_all x3, starting transfers between devices, swap(): return lax.all_to_all(shard, axes, 0, 0, tiled=True)  32.3 us
    all_to_all x1, blocking collectives, swap(): return lax.all_to_all(shard, axes, 0, 0, tiled=True)  24.6 us
    ppermute x10, starting transfers between devices, doubled(): there = lax.ppermute(block, axis, [(i, i ^ 1 << bit) for i in range(size)])  21.5 us
    all_to_all x3, waiting for transfers between devices, swap(): return lax.all_to_all(shard, axes, 0, 0, tiled=True)  21.1 us
  transfers between devices with their start and end apart: 14, of which 11 were waited for; matrix products, arithmetic and copies ran while one was open for 8% of the time, Pallas kernels for 0%

profile of v5, /device:TPU:32, one launch (start us, length us, event | category | flops | bytes accessed | tf_op | source)
XLA Modules:
  0.0 173.2 jit_solution(6385867733530137364)
XLA Ops:
  0.6 1.4 reshape.261
  2.1 0.9 copy.108
  3.0 10.3 %all-to-all-start = ((bf16[8,16,2304]{2,1,0:T(8,128)(2,1)}), bf16[8,16,2304]{2,1,0:T(8,128)(2,1)S(1)}, u32[]{:S(2)}, u32[]{:S(2)}) async-start(bf16[8,16,2304]{2,1,0:T(8,128)(2,1)} %bitcast.107), calls=%async_computation | async-start | bytes 1179648 | tf_op jit(solution)/shard_map/all_to_all | solution.py:27
  13.5 0.2 fusion.61
  13.7 0.2 convolution_convert_fusion.3
  13.9 0.2 convolution_convert_fusion.2
  14.2 3.6 %collective-permute-start.1 = (bf16[1,1,1,24,128]{4,3,2,1,0:T(8,128)(2,1)S(1)}, bf16[1,1,1,24,128]{4,3,2,1,0:T(8,128)(2,1)S(1)}, u32[]{:S(2)}, u32[]{:S(2)}) collective-permute-start(bf16[1,1,1,24,128]{4,3,2,1,0:T(8,128)(2,1)S(1)} %fusion.76), channel_id=1, source_target_pairs={{0,4},{2,6},{4,0},{6,2},{1,5},{3,7},{5,1},{7,3},{8,12},{10,14},{12... | collective-permute-start | bytes 18440 | tf_op jit(solution)/shard_map/ppermute | solution.py:32
  17.7 0.2 fusion.69
  18.0 0.2 fusion.83
  18.2 0.2 convolution_convert_fusion.1
  18.5 2.0 %collective-permute-done.1 = bf16[1,1,1,24,128]{4,3,2,1,0:T(8,128)(2,1)S(1)} collective-permute-done((bf16[1,1,1,24,128]{4,3,2,1,0:T(8,128)(2,1)S(1)}, bf16[1,1,1,24,128]{4,3,2,1,0:T(8,128)(2,1)S(1)}, u32[]{:S(2)}, u32[]{:S(2)}) %collective-permute-start.1) | collective-permute-done | bytes 6176 | tf_op jit(solution)/shard_map/ppermute | solution.py:32
  20.6 3.1 %collective-permute-start.2 = (bf16[2,1,1,24,128]{4,3,2,1,0:T(8,128)(2,1)S(1)}, bf16[2,1,1,24,128]{4,3,2,1,0:T(8,128)(2,1)S(1)}, u32[]{:S(2)}, u32[]{:S(2)}) collective-permute-start(bf16[2,1,1,24,128]{4,3,2,1,0:T(8,128)(2,1)S(1)} %pad_maximum_fusion.11), channel_id=1, source_target_pairs={{0,128},{64,192},{128,0},{192,64},{1,129},{65,193},{129,1},{193,65... | collective-permute-start | bytes 36872 | tf_op jit(solution)/shard_map/ppermute | solution.py:32
  23.8 2.1 %collective-permute-done.2 = bf16[2,1,1,24,128]{4,3,2,1,0:T(8,128)(2,1)S(1)} collective-permute-done((bf16[2,1,1,24,128]{4,3,2,1,0:T(8,128)(2,1)S(1)}, bf16[2,1,1,24,128]{4,3,2,1,0:T(8,128)(2,1)S(1)}, u32[]{:S(2)}, u32[]{:S(2)}) %collective-permute-start.2) | collective-permute-done | bytes 12320 | tf_op jit(solution)/shard_map/ppermute | solution.py:32
  25.9 1.6 collective-permute-start.3
  27.6 5.0 %collective-permute-done.3 = bf16[2,2,1,24,128]{4,3,2,1,0:T(8,128)(2,1)S(1)} collective-permute-done((bf16[2,2,1,24,128]{4,3,2,1,0:T(8,128)(2,1)S(1)}, bf16[2,2,1,24,128]{4,3,2,1,0:T(8,128)(2,1)S(1)}, u32[]{:S(2)}, u32[]{:S(2)}) %collective-permute-start.3) | collective-permute-done | bytes 24608 | tf_op jit(solution)/shard_map/ppermute | solution.py:32
  32.7 1.9 %all-to-all-done = bf16[8,16,2304]{2,1,0:T(8,128)(2,1)S(1)} async-done(((bf16[8,16,2304]{2,1,0:T(8,128)(2,1)}), bf16[8,16,2304]{2,1,0:T(8,128)(2,1)S(1)}, u32[]{:S(2)}, u32[]{:S(2)}) %all-to-all-start) | async-done | bytes 589856 | tf_op jit(solution)/shard_map/all_to_all | solution.py:27
  34.9 0.2 multiply_convert_fusion.1
  35.1 0.5 fusion.8
  35.6 0.4 fusion.18
  36.1 0.5 fusion.5
  36.7 0.4 fusion.17
  37.2 2.1 %pad_maximum_fusion.1 = bf16[128,2,2304]{2,1,0:T(2,128)(2,1)} fusion(bf16[128,2,1152]{2,1,0:T(2,128)(2,1)S(1)} %reshape.263, bf16[128,2,1152]{2,1,0:T(2,128)(2,1)S(1)} %reshape.262), kind=kLoop, calls=%fused_computation.41 | loop fusion | flops 2359296 | bytes 2359296 | tf_op jit(solution)/shard_map/concatenate | solution.py:112
  39.3 11.0 %all-to-all-start.1 = ((bf16[128,2,2304]{2,1,0:T(2,128)(2,1)}), bf16[128,2,2304]{2,1,0:T(2,128)(2,1)S(1)}, u32[]{:S(2)}, u32[]{:S(2)}) async-start(bf16[128,2,2304]{2,1,0:T(2,128)(2,1)} %pad_maximum_fusion.1), calls=%async_computation.1 | async-start | bytes 2359296 | tf_op jit(solution)/shard_map/all_to_all | solution.py:27
  50.3 4.6 %collective-permute-start.4 = (bf16[1,384,128]{2,1,0:T(8,128)(2,1)S(1)}, bf16[1,384,128]{2,1,0:T(8,128)(2,1)S(1)}, u32[]{:S(2)}, u32[]{:S(2)}) collective-permute-start(bf16[1,384,128]{2,1,0:T(8,128)(2,1)S(1)} %bitcast.126), channel_id=1, source_target_pairs={{0,1},{1,0},{2,3},{3,2},{4,5},{5,4},{6,7},{7,6},{8,9},{9,8},{10,11... | collective-permute-start | bytes 294920 | tf_op jit(solution)/shard_map/ppermute | solution.py:32
  54.9 26.1 %collective-permute-done.4 = bf16[1,384,128]{2,1,0:T(8,128)(2,1)S(1)} collective-permute-done((bf16[1,384,128]{2,1,0:T(8,128)(2,1)S(1)}, bf16[1,384,128]{2,1,0:T(8,128)(2,1)S(1)}, u32[]{:S(2)}, u32[]{:S(2)}) %collective-permute-start.4) | collective-permute-done | bytes 98336 | tf_op jit(solution)/shard_map/ppermute | solution.py:32
  81.0 1.5 collective-permute-start.7
  82.6 0.7 collective-permute-start.5
  83.2 2.4 %collective-permute-done.7 = bf16[2,2,1,2,1,2,1,1,24,128]{9,8,7,6,5,4,3,2,1,0:T(8,128)(2,1)S(1)} collective-permute-done((bf16[2,2,1,2,1,2,1,1,24,128]{9,8,7,6,5,4,3,2,1,0:T(8,128)(2,1)S(1)}, bf16[2,2,1,2,1,2,1,1,24,128]{9,8,7,6,5,4,3,2,1,0:T(8,128)(2,1)S(1)}, u32[]{:S(2)}, u32[]{:S(2)}) %collective-permute-start.7) | collective-permute-done | bytes 98336 | tf_op jit(solution)/shard_map/ppermute | solution.py:32
  85.7 1.7 collective-permute-start.8
  87.6 3.3 %collective-permute-start.6 = (bf16[2,1,2,192,128]{4,3,2,1,0:T(8,128)(2,1)S(1)}, bf16[2,1,2,192,128]{4,3,2,1,0:T(8,128)(2,1)S(1)}, u32[]{:S(2)}, u32[]{:S(2)}) collective-permute-start(bf16[2,1,2,192,128]{4,3,2,1,0:T(8,128)(2,1)S(1)} %pad_maximum_fusion.6), channel_id=1, source_target_pairs={{0,4},{2,6},{4,0},{6,2},{1,5},{3,7},{5,1},{7,3},{8,12},{10,14},{12... | collective-permute-start | bytes 589832 | tf_op jit(solution)/shard_map/ppermute | solution.py:32
  90.9 0.6 collective-permute-done.8
  91.5 0.8 pad_maximum_fusion.5
  92.3 1.5 collective-permute-start.9
  93.9 1.0 collective-permute-done.6
  94.9 0.8 broadcast_select_fusion.7
  95.7 0.8 fusion.82
  96.6 0.4 reshape.265
  97.1 0.4 copy-done.4
  97.9 2.5 %collective-permute-done.9 = bf16[2,2,2,2,2,2,1,1,24,128]{9,8,7,6,5,4,3,2,1,0:T(8,128)(2,1)} collective-permute-done((bf16[2,2,2,2,2,2,1,1,24,128]{9,8,7,6,5,4,3,2,1,0:T(8,128)(2,1)}, bf16[2,2,2,2,2,2,1,1,24,128]{9,8,7,6,5,4,3,2,1,0:T(8,128)(2,1)}, u32[]{:S(2)}, u32[]{:S(2)}) %collective-permute-start.9) | collective-permute-done | bytes 393248 | tf_op jit(solution)/shard_map/ppermute | solution.py:32
  100.4 1.1 broadcast_select_fusion.3
  101.5 1.0 pad_maximum_fusion.3
  102.5 1.2 reshape.264
  103.6 1.1 select_bitcast_fusion.1
  104.9 0.9 copy-done.6
  105.9 0.7 convolution_convert_fusion
  106.5 1.2 reshape.267
  107.7 11.0 %all-to-all-start.2 = ((bf16[128,2,1152]{2,1,0:T(2,128)(2,1)}), bf16[128,2,1152]{2,1,0:T(2,128)(2,1)S(1)}, u32[]{:S(2)}, u32[]{:S(2)}) async-start(bf16[128,2,1152]{2,1,0:T(2,128)(2,1)} %reshape.267), calls=%async_computation.2 | async-start | bytes 1179648 | tf_op jit(solution)/shard_map/all_to_all | solution.py:27
  118.7 0.2 fusion.31
  118.9 1.6 fusion.11
  120.5 1.3 broadcast_select_fusion.1
  121.9 19.2 %all-to-all-done.2 = bf16[128,2,1152]{2,1,0:T(2,128)(2,1)S(1)} async-done(((bf16[128,2,1152]{2,1,0:T(2,128)(2,1)}), bf16[128,2,1152]{2,1,0:T(2,128)(2,1)S(1)}, u32[]{:S(2)}, u32[]{:S(2)}) %all-to-all-start.2) | async-done | bytes 589856 | tf_op jit(solution)/shard_map/all_to_all | solution.py:27
  141.1 0.5 convert_reduce_fusion.2
  141.6 0.8 multiply_reduce_fusion
  142.6 1.2 copy-done.3
  143.8 0.4 convert_reduce_fusion
  144.2 0.2 fusion.26
  144.4 0.3 convolution_bitcast_fusion
  144.8 0.5 fusion.39
  145.3 0.2 fusion.84
  145.5 0.7 fusion.19
  146.6 24.6 %all_to_all.20 = bf16[8,16,2432]{2,1,0:T(8,128)(2,1)S(1)} all-to-all(bf16[8,16,2432]{2,1,0:T(8,128)(2,1)S(1)} %fusion.46), channel_id=1, replica_groups=mesh['x'=4,'zl'=4,'core'=2,'y'=4,'zh'=2] {'y','zh'}, dimensions={0} | all-to-all | bytes 1245184 | tf_op jit(solution)/shard_map/all_to_all | solution.py:27
  171.3 0.2 copy.72
  171.5 1.1 reshape.281
  172.6 0.6 reshape.282
  (109 shorter events, 3.1 us)
Async XLA Ops:
  0.6 13.0 %copy-start = (bf16[384,48]{0,1:T(8,128)(2,1)S(1)}, bf16[384,48]{0,1:T(8,128)(2,1)}, u32[]{:S(2)}) copy-start(bf16[384,48]{0,1:T(8,128)(2,1)} %param.27) | copy-start | bytes 110596
  2.0 11.3 %copy-start.8 = (bf16[24,384]{1,0:T(8,128)(2,1)S(1)}, bf16[24,384]{1,0:T(8,128)(2,1)}, u32[]{:S(2)}) copy-start(bf16[24,384]{1,0:T(8,128)(2,1)} %param.16) | copy-start | bytes 55300
  2.0 11.6 %copy-start.18 = (f32[384]{0:T(512)S(1)}, f32[384]{0:T(512)}, u32[]{:S(2)}) copy-start(f32[384]{0:T(512)} %param.25) | copy-start | bytes 4612
  2.1 11.8 %copy-start.15 = (bf16[384,2,48]{0,2,1:T(8,128)(2,1)S(1)}, bf16[384,2,48]{0,2,1:T(8,128)(2,1)}, u32[]{:S(2)}) copy-start(bf16[384,2,48]{0,2,1:T(8,128)(2,1)} %param.28) | copy-start | bytes 221188
  2.1 15.9 %copy-start.7 = (bf16[128,4,128]{2,1,0:T(4,128)(2,1)S(1)}, bf16[128,4,128]{2,1,0:T(4,128)(2,1)}, u32[]{:S(2)}) copy-start(bf16[128,4,128]{2,1,0:T(4,128)(2,1)} %param.19) | copy-start | bytes 393220
  3.0 15.2 %copy-start.16 = (bf16[384,48]{0,1:T(8,128)(2,1)S(1)}, bf16[384,48]{0,1:T(8,128)(2,1)}, u32[]{:S(2)}) copy-start(bf16[384,48]{0,1:T(8,128)(2,1)} %param.26) | copy-start | bytes 110596
  3.0 15.4 %copy-start.11 = (s32[768]{0:T(1024)S(1)}, s32[768]{0:T(1024)}, u32[]{:S(2)}) copy-start(s32[768]{0:T(1024)} %param.17) | copy-start | bytes 9220
  3.0 24.5 %copy-start.13 = (f32[128]{0:T(128)S(1)}, f32[128]{0:T(128)}, u32[]{:S(2)}) copy-start(f32[128]{0:T(128)} %param.18) | copy-start | bytes 1540
  3.0 29.6 %copy-start.9 = (bf16[48,384]{1,0:T(8,128)(2,1)S(1)}, bf16[48,384]{1,0:T(8,128)(2,1)}, u32[]{:S(2)}) copy-start(bf16[48,384]{1,0:T(8,128)(2,1)} %param.29) | copy-start | bytes 110596
  3.0 31.6 %all-to-all-start = ((bf16[8,16,2304]{2,1,0:T(8,128)(2,1)}), bf16[8,16,2304]{2,1,0:T(8,128)(2,1)S(1)}, u32[]{:S(2)}, u32[]{:S(2)}) async-start(bf16[8,16,2304]{2,1,0:T(8,128)(2,1)} %bitcast.107), calls=%async_computation | async-start | bytes 1179648 | tf_op jit(solution)/shard_map/all_to_all | solution.py:27
  14.2 6.3 %collective-permute-start.1 = (bf16[1,1,1,24,128]{4,3,2,1,0:T(8,128)(2,1)S(1)}, bf16[1,1,1,24,128]{4,3,2,1,0:T(8,128)(2,1)S(1)}, u32[]{:S(2)}, u32[]{:S(2)}) collective-permute-start(bf16[1,1,1,24,128]{4,3,2,1,0:T(8,128)(2,1)S(1)} %fusion.76), channel_id=1, source_target_pairs={{0,4},{2,6},{4,0},{6,2},{1,5},{3,7},{5,1},{7,3},{8,12},{10,14},{12... | collective-permute-start | bytes 18440 | tf_op jit(solution)/shard_map/ppermute | solution.py:32
  20.6 5.3 %collective-permute-start.2 = (bf16[2,1,1,24,128]{4,3,2,1,0:T(8,128)(2,1)S(1)}, bf16[2,1,1,24,128]{4,3,2,1,0:T(8,128)(2,1)S(1)}, u32[]{:S(2)}, u32[]{:S(2)}) collective-permute-start(bf16[2,1,1,24,128]{4,3,2,1,0:T(8,128)(2,1)S(1)} %pad_maximum_fusion.11), channel_id=1, source_target_pairs={{0,128},{64,192},{128,0},{192,64},{1,129},{65,193},{129,1},{193,65... | collective-permute-start | bytes 36872 | tf_op jit(solution)/shard_map/ppermute | solution.py:32
  25.9 6.6 %collective-permute-start.3 = (bf16[2,2,1,24,128]{4,3,2,1,0:T(8,128)(2,1)S(1)}, bf16[2,2,1,24,128]{4,3,2,1,0:T(8,128)(2,1)S(1)}, u32[]{:S(2)}, u32[]{:S(2)}) collective-permute-start(bf16[2,2,1,24,128]{4,3,2,1,0:T(8,128)(2,1)S(1)} %pad_maximum_fusion.10), channel_id=1, source_target_pairs={{0,32},{16,48},{32,0},{48,16},{1,33},{17,49},{33,1},{49,17},{2,34}... | collective-permute-start | bytes 73736 | tf_op jit(solution)/shard_map/ppermute | solution.py:32
  39.3 43.2 %copy-start.12 = (bf16[128,16]{0,1:T(8,128)(2,1)S(1)}, bf16[128,16]{0,1:T(8,128)(2,1)}, u32[]{:S(2)}) copy-start(bf16[128,16]{0,1:T(8,128)(2,1)} %param.24) | copy-start | bytes 12292
  39.3 56.4 %all-to-all-start.1 = ((bf16[128,2,2304]{2,1,0:T(2,128)(2,1)}), bf16[128,2,2304]{2,1,0:T(2,128)(2,1)S(1)}, u32[]{:S(2)}, u32[]{:S(2)}) async-start(bf16[128,2,2304]{2,1,0:T(2,128)(2,1)} %pad_maximum_fusion.1), calls=%async_computation.1 | async-start | bytes 2359296 | tf_op jit(solution)/shard_map/all_to_all | solution.py:27
  50.3 30.6 %collective-permute-start.4 = (bf16[1,384,128]{2,1,0:T(8,128)(2,1)S(1)}, bf16[1,384,128]{2,1,0:T(8,128)(2,1)S(1)}, u32[]{:S(2)}, u32[]{:S(2)}) collective-permute-start(bf16[1,384,128]{2,1,0:T(8,128)(2,1)S(1)} %bitcast.126), channel_id=1, source_target_pairs={{0,1},{1,0},{2,3},{3,2},{4,5},{5,4},{6,7},{7,6},{8,9},{9,8},{10,11... | collective-permute-start | bytes 294920 | tf_op jit(solution)/shard_map/ppermute | solution.py:32
  81.0 4.7 %collective-permute-start.7 = (bf16[2,2,1,2,1,2,1,1,24,128]{9,8,7,6,5,4,3,2,1,0:T(8,128)(2,1)S(1)}, bf16[2,2,1,2,1,2,1,1,24,128]{9,8,7,6,5,4,3,2,1,0:T(8,128)(2,1)S(1)}, u32[]{:S(2)}, u32[]{:S(2)}) collective-permute-start(bf16[2,2,1,2,1,2,1,1,24,128]{9,8,7,6,5,4,3,2,1,0:T(8,128)(2,1)S(1)} %bitcast.124), channel_id=1, source_target_pairs={{0,2},{2,0},{4,6},{6,4},{1,3},{3,1},{5,7},{7,5},{8,10},{10,8},{12,... | collective-permute-start | bytes 294920 | tf_op jit(solution)/shard_map/ppermute | solution.py:32
  82.6 5.0 %collective-permute-start.5 = (bf16[2,1,1,192,128]{4,3,2,1,0:T(8,128)(2,1)S(1)}, bf16[2,1,1,192,128]{4,3,2,1,0:T(8,128)(2,1)S(1)}, u32[]{:S(2)}, u32[]{:S(2)}) collective-permute-start(bf16[2,1,1,192,128]{4,3,2,1,0:T(8,128)(2,1)S(1)} %get-tuple-element.19), channel_id=1, source_target_pairs={{0,2},{2,0},{4,6},{6,4},{1,3},{3,1},{5,7},{7,5},{8,10},{10,8},{12,... | collective-permute-start | bytes 294920 | tf_op jit(solution)/shard_map/ppermute | solution.py:32
  85.7 5.8 %collective-permute-start.8 = (bf16[2,2,2,2,1,2,1,1,24,128]{9,8,7,6,5,4,3,2,1,0:T(8,128)(2,1)S(1)}, bf16[2,2,2,2,1,2,1,1,24,128]{9,8,7,6,5,4,3,2,1,0:T(8,128)(2,1)S(1)}, u32[]{:S(2)}, u32[]{:S(2)}) collective-permute-start(bf16[2,2,2,2,1,2,1,1,24,128]{9,8,7,6,5,4,3,2,1,0:T(8,128)(2,1)S(1)} %pad_maximum_fusion.7), channel_id=1, source_target_pairs={{0,64},{64,0},{128,192},{192,128},{1,65},{65,1},{129,193},{193,129... | collective-permute-start | bytes 589832 | tf_op jit(solution)/shard_map/ppermute | solution.py:32
  87.6 7.3 %collective-permute-start.6 = (bf16[2,1,2,192,128]{4,3,2,1,0:T(8,128)(2,1)S(1)}, bf16[2,1,2,192,128]{4,3,2,1,0:T(8,128)(2,1)S(1)}, u32[]{:S(2)}, u32[]{:S(2)}) collective-permute-start(bf16[2,1,2,192,128]{4,3,2,1,0:T(8,128)(2,1)S(1)} %pad_maximum_fusion.6), channel_id=1, source_target_pairs={{0,4},{2,6},{4,0},{6,2},{1,5},{3,7},{5,1},{7,3},{8,12},{10,14},{12... | collective-permute-start | bytes 589832 | tf_op jit(solution)/shard_map/ppermute | solution.py:32
  91.5 5.0 %copy-start.1 = (bf16[2,2,2,2,1,2,1,1,24,128]{9,8,7,6,5,4,3,2,1,0:T(8,128)(2,1)}, bf16[2,2,2,2,1,2,1,1,24,128]{9,8,7,6,5,4,3,2,1,0:T(8,128)(2,1)S(1)}, u32[]{:S(2)}) copy-start(bf16[2,2,2,2,1,2,1,1,24,128]{9,8,7,6,5,4,3,2,1,0:T(8,128)(2,1)S(1)} %get-tuple-element.16) | copy-start | bytes 589828
  92.3 8.1 %collective-permute-start.9 = (bf16[2,2,2,2,2,2,1,1,24,128]{9,8,7,6,5,4,3,2,1,0:T(8,128)(2,1)}, bf16[2,2,2,2,2,2,1,1,24,128]{9,8,7,6,5,4,3,2,1,0:T(8,128)(2,1)}, u32[]{:S(2)}, u32[]{:S(2)}) collective-permute-start(bf16[2,2,2,2,2,2,1,1,24,128]{9,8,7,6,5,4,3,2,1,0:T(8,128)(2,1)} %pad_maximum_fusion.5), channel_id=1, source_target_pairs={{0,16},{16,0},{32,48},{48,32},{1,17},{17,1},{33,49},{49,33},{2,18}... | collective-permute-start | bytes 1179656 | tf_op jit(solution)/shard_map/ppermute | solution.py:32
  96.5 0.9 copy-start.4
  96.6 1.0 copy-start.5
  96.9 3.5 %copy-start.2 = (bf16[2,2,2,2,1,2,1,1,24,128]{9,8,7,6,5,4,3,2,1,0:T(8,128)(2,1)S(1)}, bf16[2,2,2,2,1,2,1,1,24,128]{9,8,7,6,5,4,3,2,1,0:T(8,128)(2,1)}, u32[]{:S(2)}) copy-start(bf16[2,2,2,2,1,2,1,1,24,128]{9,8,7,6,5,4,3,2,1,0:T(8,128)(2,1)} %copy-done.1) | copy-start | bytes 589828
  97.0 6.7 %collective-permute-start = (bf16[16,24,768]{2,1,0:T(8,128)(2,1)S(1)}, bf16[16,24,768]{2,1,0:T(8,128)(2,1)}, u32[]{:S(2)}, u32[]{:S(2)}) collective-permute-start(bf16[16,24,768]{2,1,0:T(8,128)(2,1)S(1)} %reshape.265), channel_id=1, source_target_pairs={{0,8},{8,0},{1,9},{9,1},{2,10},{10,2},{3,11},{11,3},{4,12},{12,4},... | collective-permute-start | bytes 1769480 | tf_op jit(solution)/shard_map/ppermute | solution.py:114
  102.5 18.1 %collective-permute-start.10 = (bf16[2,2,2,2,2,2,2,1,24,128]{9,8,7,6,5,4,3,2,1,0:T(8,128)(2,1)}, bf16[2,2,2,2,2,2,2,1,24,128]{9,8,7,6,5,4,3,2,1,0:T(8,128)(2,1)}, u32[]{:S(2)}, u32[]{:S(2)}) collective-permute-start(bf16[2,2,2,2,2,2,2,1,24,128]{9,8,7,6,5,4,3,2,1,0:T(8,128)(2,1)} %pad_maximum_fusion.3), channel_id=1, source_target_pairs={{0,8},{8,0},{1,9},{9,1},{2,10},{10,2},{3,11},{11,3},{4,12},{12,4},... | collective-permute-start | bytes 2359304 | tf_op jit(solution)/shard_map/ppermute | solution.py:32
  104.8 1.1 copy-start.6
  107.7 11.2 %copy-start.17 = (bf16[128,128]{1,0:T(8,128)(2,1)S(1)}, bf16[128,128]{1,0:T(8,128)(2,1)}, u32[]{:S(2)}) copy-start(bf16[128,128]{1,0:T(8,128)(2,1)} %param.20) | copy-start | bytes 98308
  107.7 33.3 %all-to-all-start.2 = ((bf16[128,2,1152]{2,1,0:T(2,128)(2,1)}), bf16[128,2,1152]{2,1,0:T(2,128)(2,1)S(1)}, u32[]{:S(2)}, u32[]{:S(2)}) async-start(bf16[128,2,1152]{2,1,0:T(2,128)(2,1)} %reshape.267), calls=%async_computation.2 | async-start | bytes 1179648 | tf_op jit(solution)/shard_map/all_to_all | solution.py:27
  141.6 1.0 copy-start.10
  141.6 1.0 copy-start.14
  142.5 1.3 copy-start.3
  143.8 0.7 copy-start.19

commit v6 on v5

--- a/solution.py
+++ b/solution.py
@@ -32,6 +32,12 @@
     there = lax.ppermute(block, axis, [(i, i ^ (1 << bit)) for i in range(size)])
     low = (lax.axis_index(axis) >> bit) & 1 == 0
     return jnp.concatenate([jnp.where(low, block, there), jnp.where(low, there, block)], axis=dim)
+
+
+def rows_in_order(spread, part, nq):
+    width = spread.shape[1] // part
+    pieces = [spread[:, width * t : width * (t + 1)].reshape(-1, nq, width) for t in range(part)]
+    return jnp.concatenate(pieces, axis=1)
 
 
 def filled(*parts):
@@ -102,17 +108,23 @@
     rest = doubled(rest[:, None, None], "y", 0, 2)
     rest = doubled(rest, "y", 1, 1).reshape(nq, -1, LANES)
 
-    sent = pair.reshape(chans, nq, spots).transpose(1, 0, 2)
+    sent = jnp.concatenate([pair[:, nq * t : nq * (t + 1)] for t in range(part)], axis=2)
+    sent = sent.transpose(1, 0, 2)
     full = swap(sent, CHAN).reshape(C, spots).astype(F32)
     normed = layer_norm(full, pair_gain[:, None], 0).astype(BF)
-    live_rows = lax.dynamic_slice_in_dim(live, r * rows + q * part, part, 0)
+    live_rows = lax.dynamic_slice_in_dim(live, r * rows, rows, 0).reshape(part, nq)
+    live_rows = lax.dynamic_index_in_dim(live_rows, q, 1, keepdims=False)
     mask = (live_rows[:, None] * live[None, :]).reshape(1, spots)
-    left = edge(normed, w_ab[:, 0], w_ab[:, 1], mask).reshape(C, 2, spots // 2)
-    right = edge(normed, w_ab[:, 2], w_ab[:, 3], mask).reshape(C, 2, spots // 2)
-    edges = swap(jnp.concatenate([right, left], axis=2), OWN)
-    right_here = edges[:, :, : spots // 2].reshape(C // nq, rows, width)
+    half = spots // 2
+    left = edge(normed, w_ab[:, 0], w_ab[:, 1], mask)
+    right = edge(normed, w_ab[:, 2], w_ab[:, 3], mask)
+    sent = [right[:, :half], left[:, :half], right[:, half:], left[:, half:]]
+    sent = jnp.concatenate(sent, axis=1).reshape(C, 2, spots)
+
+    edges = swap(sent, OWN)
+    right_here = rows_in_order(edges[:, :, :half].reshape(C, spots), part, nq)
     right_there = lax.ppermute(right_here, "core", [(0, 1), (1, 0)])
-    left_owned = edges[:, :, spots // 2 :].reshape(C * part, width)
+    left_owned = edges[:, :, half:].reshape(C, spots)
     first = core == 0
     right_owned = jnp.stack(
         [
@@ -121,10 +133,17 @@
         ],
         axis=1,
     ).reshape(2 * C * part, width)
-    owned = lax.dot_general(
-        left_owned, right_owned, (((1,), (1,)), ((), ())), preferred_element_type=F32
-    ).astype(BF)
-    product = swap(owned.reshape(C, 2, spots // 2), OWN).reshape(C, spots)
+    owned = [
+        lax.dot_general(
+            left_owned[:, width * t : width * (t + 1)],
+            right_owned,
+            (((1,), (1,)), ((), ())),
+            preferred_element_type=F32,
+        ).astype(BF)
+        for t in range(part)
+    ]
+    owned = jnp.concatenate(owned, axis=1).reshape(C, 2, half)
+    product = swap(owned, OWN).reshape(C, spots)
 
     product_normed = layer_norm(product.astype(F32), x_gain[:, None], 0).astype(BF)
     out_gate = jax.nn.sigmoid(
@@ -138,11 +157,10 @@
 
     heads = H // nq
     head_size = D // H
-    at = q * part
-    mine = lax.dynamic_slice_in_dim(rest, at, part, 1)
-    gate_mine = mine[..., local : 2 * local].astype(F32) + lax.dynamic_slice_in_dim(
-        rest, rows + at, part, 1
-    )[..., :local].astype(F32)
+    mine = rest[:, : 2 * rows].reshape(nq, 2 * part, nq, LANES)
+    mine = lax.dynamic_index_in_dim(mine, q, 2, keepdims=False)
+    gate_mine = mine[:, :part, local : 2 * local].astype(F32) + mine[:, part:, :local].astype(F32)
+    mine = mine[:, :part]
     is_head = (jnp.arange(local)[None, :] // head_size == jnp.arange(heads)[:, None])[:, None]
     queries = jnp.where(is_head, mine[:, None, :, :local], 0).reshape(nq, heads * part, local)
     scores = jnp.einsum("qaf,qjf->qaj", queries, kv[..., :local], preferred_element_type=F32)
@@ -162,8 +180,9 @@
     summed = jnp.pad(summed, ((0, 0), (0, chans - part), (0, LANES - local)))
     sent = jnp.concatenate([renewed.reshape(nq, chans, spots), summed], axis=2)
     both = swap(sent, CHAN)
-    pair_out = both[:, :, :spots].transpose(1, 0, 2).reshape(chans, rows, width)
-    attended = both[:, :part, spots : spots + local].reshape(rows, local)
+    pair_out = both[:, :, :spots].transpose(1, 0, 2).reshape(chans * nq, spots)
+    pair_out = rows_in_order(pair_out, part, nq)
+    attended = both[:, :part, spots : spots + local].transpose(1, 0, 2).reshape(rows, local)
     return (pair_out, attended)
 
 

time: 174 us -> 170 us (0.977)
  local copies, waits for them, and re-layouts: 11.8 us -> 7.85 us
  other arithmetic: 11.8 us -> 10 us
    reshape x9 -> x6, local copies, waits for them, and re-layouts: 7.02 us -> 2.31 us  [the longest x1 1.18 us: block(): sent = jnp.concatenate(sent, axis=1).reshape(C, 2, spots)]
  transfers between devices with their start and end apart: 14 -> 14, of which waited for: 11 -> 11; matrix products, arithmetic and copies ran while one was open for 8% -> 7% of each run, Pallas kernels for 0% -> 0%
where the time goes in v6:
time: 170 us
  waiting for transfers between devices  64.1 us (38%)
  starting transfers between devices  54.1 us (32%)
  blocking collectives  24.6 us (14%)
  other arithmetic  10 us (6%)
  local copies, waits for them, and re-layouts  7.85 us (5%)
  matrix products  7.78 us (5%)
    ppermute x10, waiting for transfers between devices, doubled(): there = lax.ppermute(block, axis, [(i, i ^ 1 << bit) for i in range(size)])  42.9 us
    all_to_all x3, starting transfers between devices, swap(): return lax.all_to_all(shard, axes, 0, 0, tiled=True)  32.3 us
    all_to_all x1, blocking collectives, swap(): return lax.all_to_all(shard, axes, 0, 0, tiled=True)  24.6 us
    ppermute x10, starting transfers between devices, doubled(): there = lax.ppermute(block, axis, [(i, i ^ 1 << bit) for i in range(size)])  21.5 us
    all_to_all x3, waiting for transfers between devices, swap(): return lax.all_to_all(shard, axes, 0, 0, tiled=True)  21.1 us
  transfers between devices with their start and end apart: 14, of which 11 were waited for; matrix products, arithmetic and copies ran while one was open for 7% of the time, Pallas kernels for 0%

profile of v6, /device:TPU:32, one launch (start us, length us, event | category | flops | bytes accessed | tf_op | source)
XLA Modules:
  0.0 169.7 jit_solution(9797634934473268574)
XLA Ops:
  0.6 1.2 fusion.88
  2.0 0.9 maximum_bitcast_fusion
  2.9 10.3 %all-to-all-start = ((bf16[8,16,2304]{2,1,0:T(8,128)(2,1)}), bf16[8,16,2304]{2,1,0:T(8,128)(2,1)S(1)}, u32[]{:S(2)}, u32[]{:S(2)}) async-start(bf16[8,16,2304]{2,1,0:T(8,128)(2,1)} %maximum_bitcast_fusion), calls=%async_computation | async-start | bytes 1179648 | tf_op jit(solution)/shard_map/all_to_all | solution.py:27
  13.3 0.2 fusion.64
  13.5 0.2 convolution_convert_fusion.5
  13.7 0.2 convolution_convert_fusion.4
  14.0 3.6 %collective-permute-start.1 = (bf16[1,1,1,24,128]{4,3,2,1,0:T(8,128)(2,1)S(1)}, bf16[1,1,1,24,128]{4,3,2,1,0:T(8,128)(2,1)S(1)}, u32[]{:S(2)}, u32[]{:S(2)}) collective-permute-start(bf16[1,1,1,24,128]{4,3,2,1,0:T(8,128)(2,1)S(1)} %fusion.79), channel_id=1, source_target_pairs={{0,4},{2,6},{4,0},{6,2},{1,5},{3,7},{5,1},{7,3},{8,12},{10,14},{12... | collective-permute-start | bytes 18440 | tf_op jit(solution)/shard_map/ppermute | solution.py:32
  17.6 0.2 fusion.72
  17.8 0.2 fusion.89
  18.0 0.2 convolution_convert_fusion.3
  18.4 0.2 dynamic-slice_reduce_fusion
  18.6 1.8 %collective-permute-done.1 = bf16[1,1,1,24,128]{4,3,2,1,0:T(8,128)(2,1)S(1)} collective-permute-done((bf16[1,1,1,24,128]{4,3,2,1,0:T(8,128)(2,1)S(1)}, bf16[1,1,1,24,128]{4,3,2,1,0:T(8,128)(2,1)S(1)}, u32[]{:S(2)}, u32[]{:S(2)}) %collective-permute-start.1) | collective-permute-done | bytes 6176 | tf_op jit(solution)/shard_map/ppermute | solution.py:32
  20.4 3.1 %collective-permute-start.2 = (bf16[2,1,1,24,128]{4,3,2,1,0:T(8,128)(2,1)S(1)}, bf16[2,1,1,24,128]{4,3,2,1,0:T(8,128)(2,1)S(1)}, u32[]{:S(2)}, u32[]{:S(2)}) collective-permute-start(bf16[2,1,1,24,128]{4,3,2,1,0:T(8,128)(2,1)S(1)} %pad_maximum_fusion.14), channel_id=1, source_target_pairs={{0,128},{64,192},{128,0},{192,64},{1,129},{65,193},{129,1},{193,65... | collective-permute-start | bytes 36872 | tf_op jit(solution)/shard_map/ppermute | solution.py:32
  23.6 2.1 %collective-permute-done.2 = bf16[2,1,1,24,128]{4,3,2,1,0:T(8,128)(2,1)S(1)} collective-permute-done((bf16[2,1,1,24,128]{4,3,2,1,0:T(8,128)(2,1)S(1)}, bf16[2,1,1,24,128]{4,3,2,1,0:T(8,128)(2,1)S(1)}, u32[]{:S(2)}, u32[]{:S(2)}) %collective-permute-start.2) | collective-permute-done | bytes 12320 | tf_op jit(solution)/shard_map/ppermute | solution.py:32
  25.7 1.6 collective-permute-start.3
  27.4 5.0 %collective-permute-done.3 = bf16[2,2,1,24,128]{4,3,2,1,0:T(8,128)(2,1)S(1)} collective-permute-done((bf16[2,2,1,24,128]{4,3,2,1,0:T(8,128)(2,1)S(1)}, bf16[2,2,1,24,128]{4,3,2,1,0:T(8,128)(2,1)S(1)}, u32[]{:S(2)}, u32[]{:S(2)}) %collective-permute-start.3) | collective-permute-done | bytes 24608 | tf_op jit(solution)/shard_map/ppermute | solution.py:32
  32.5 1.9 %all-to-all-done = bf16[8,16,2304]{2,1,0:T(8,128)(2,1)S(1)} async-done(((bf16[8,16,2304]{2,1,0:T(8,128)(2,1)}), bf16[8,16,2304]{2,1,0:T(8,128)(2,1)S(1)}, u32[]{:S(2)}, u32[]{:S(2)}) %all-to-all-start) | async-done | bytes 589856 | tf_op jit(solution)/shard_map/all_to_all | solution.py:27
  34.6 0.2 multiply_reduce_fusion.1
  34.8 0.2 multiply_convert_fusion.1
  35.0 0.5 fusion.5
  35.5 0.5 fusion.8
  36.0 0.4 fusion.17
  36.4 0.4 fusion.18
  36.9 1.2 reshape.279
  38.1 11.0 %all-to-all-start.1 = ((bf16[128,2,2304]{2,1,0:T(2,128)(2,1)}), bf16[128,2,2304]{2,1,0:T(2,128)(2,1)S(1)}, u32[]{:S(2)}, u32[]{:S(2)}) async-start(bf16[128,2,2304]{2,1,0:T(2,128)(2,1)} %reshape.279), calls=%async_computation.1 | async-start | bytes 2359296 | tf_op jit(solution)/shard_map/all_to_all | solution.py:27
  49.1 4.6 %collective-permute-start.4 = (bf16[1,384,128]{2,1,0:T(8,128)(2,1)S(1)}, bf16[1,384,128]{2,1,0:T(8,128)(2,1)S(1)}, u32[]{:S(2)}, u32[]{:S(2)}) collective-permute-start(bf16[1,384,128]{2,1,0:T(8,128)(2,1)S(1)} %bitcast.164), channel_id=1, source_target_pairs={{0,1},{1,0},{2,3},{3,2},{4,5},{5,4},{6,7},{7,6},{8,9},{9,8},{10,11... | collective-permute-start | bytes 294920 | tf_op jit(solution)/shard_map/ppermute | solution.py:32
  53.7 26.1 %collective-permute-done.4 = bf16[1,384,128]{2,1,0:T(8,128)(2,1)S(1)} collective-permute-done((bf16[1,384,128]{2,1,0:T(8,128)(2,1)S(1)}, bf16[1,384,128]{2,1,0:T(8,128)(2,1)S(1)}, u32[]{:S(2)}, u32[]{:S(2)}) %collective-permute-start.4) | collective-permute-done | bytes 98336 | tf_op jit(solution)/shard_map/ppermute | solution.py:32
  79.8 1.5 collective-permute-start.7
  81.4 0.7 collective-permute-start.5
  82.1 2.4 %collective-permute-done.7 = bf16[2,2,1,2,1,2,1,1,24,128]{9,8,7,6,5,4,3,2,1,0:T(8,128)(2,1)S(1)} collective-permute-done((bf16[2,2,1,2,1,2,1,1,24,128]{9,8,7,6,5,4,3,2,1,0:T(8,128)(2,1)S(1)}, bf16[2,2,1,2,1,2,1,1,24,128]{9,8,7,6,5,4,3,2,1,0:T(8,128)(2,1)S(1)}, u32[]{:S(2)}, u32[]{:S(2)}) %collective-permute-start.7) | collective-permute-done | bytes 98336 | tf_op jit(solution)/shard_map/ppermute | solution.py:32
  84.6 1.7 %collective-permute-start.8 = (bf16[2,2,2,2,1,2,1,1,24,128]{9,8,7,6,5,4,3,2,1,0:T(8,128)(2,1)S(1)}, bf16[2,2,2,2,1,2,1,1,24,128]{9,8,7,6,5,4,3,2,1,0:T(8,128)(2,1)S(1)}, u32[]{:S(2)}, u32[]{:S(2)}) collective-permute-start(bf16[2,2,2,2,1,2,1,1,24,128]{9,8,7,6,5,4,3,2,1,0:T(8,128)(2,1)S(1)} %pad_maximum_fusion.10), channel_id=1, source_target_pairs={{0,64},{64,0},{128,192},{192,128},{1,65},{65,1},{129,193},{193,129... | collective-permute-start | bytes 589832 | tf_op jit(solution)/shard_map/ppermute | solution.py:32
  86.5 3.3 %collective-permute-start.6 = (bf16[2,1,2,192,128]{4,3,2,1,0:T(8,128)(2,1)S(1)}, bf16[2,1,2,192,128]{4,3,2,1,0:T(8,128)(2,1)S(1)}, u32[]{:S(2)}, u32[]{:S(2)}) collective-permute-start(bf16[2,1,2,192,128]{4,3,2,1,0:T(8,128)(2,1)S(1)} %pad_maximum_fusion.9), channel_id=1, source_target_pairs={{0,4},{2,6},{4,0},{6,2},{1,5},{3,7},{5,1},{7,3},{8,12},{10,14},{12... | collective-permute-start | bytes 589832 | tf_op jit(solution)/shard_map/ppermute | solution.py:32
  89.8 0.6 collective-permute-done.8
  90.4 0.8 pad_maximum_fusion.8
  91.1 1.5 collective-permute-start.9
  92.7 1.0 collective-permute-done.6
  93.8 0.8 fusion.85
  94.8 0.3 collective-permute-start
  95.4 3.8 %collective-permute-done.9 = bf16[2,2,2,2,2,2,1,1,24,128]{9,8,7,6,5,4,3,2,1,0:T(8,128)(2,1)} collective-permute-done((bf16[2,2,2,2,2,2,1,1,24,128]{9,8,7,6,5,4,3,2,1,0:T(8,128)(2,1)}, bf16[2,2,2,2,2,2,1,1,24,128]{9,8,7,6,5,4,3,2,1,0:T(8,128)(2,1)}, u32[]{:S(2)}, u32[]{:S(2)}) %collective-permute-start.9) | collective-permute-done | bytes 393248 | tf_op jit(solution)/shard_map/ppermute | solution.py:32
  99.2 1.1 broadcast_select_fusion.3
  100.3 1.0 pad_maximum_fusion.3
  101.4 0.3 select_bitcast_fusion.1
  101.8 0.5 convolution_convert_fusion.2
  102.3 0.5 convolution_convert_fusion.1
  102.9 0.5 convolution_convert_fusion
  103.5 0.9 reshape.286
  104.4 11.0 %all-to-all-start.2 = ((bf16[128,2,1152]{2,1,0:T(2,128)(2,1)}), bf16[128,2,1152]{2,1,0:T(2,128)(2,1)S(1)}, u32[]{:S(2)}, u32[]{:S(2)}) async-start(bf16[128,2,1152]{2,1,0:T(2,128)(2,1)} %reshape.286), calls=%async_computation.2 | async-start | bytes 1179648 | tf_op jit(solution)/shard_map/all_to_all | solution.py:27
  115.4 0.2 fusion.31
  115.6 1.5 fusion.11
  117.2 1.3 broadcast_select_fusion.1
  118.6 19.2 %all-to-all-done.2 = bf16[128,2,1152]{2,1,0:T(2,128)(2,1)S(1)} async-done(((bf16[128,2,1152]{2,1,0:T(2,128)(2,1)}), bf16[128,2,1152]{2,1,0:T(2,128)(2,1)S(1)}, u32[]{:S(2)}, u32[]{:S(2)}) %all-to-all-start.2) | async-done | bytes 589856 | tf_op jit(solution)/shard_map/all_to_all | solution.py:27
  137.8 0.5 convert_reduce_fusion.2
  138.4 0.8 multiply_reduce_fusion
  139.3 1.2 copy-done.1
  140.5 0.4 convert_reduce_fusion
  140.9 0.2 fusion.26
  141.1 0.3 convolution_bitcast_fusion
  141.5 0.5 fusion.39
  142.0 0.2 fusion.90
  142.2 0.7 fusion.19
  143.4 24.6 %all_to_all.20 = bf16[8,16,2432]{2,1,0:T(8,128)(2,1)S(1)} all-to-all(bf16[8,16,2432]{2,1,0:T(8,128)(2,1)S(1)} %fusion.46), channel_id=1, replica_groups=mesh['x'=4,'zl'=4,'core'=2,'y'=4,'zh'=2] {'y','zh'}, dimensions={0} | all-to-all | bytes 1245184 | tf_op jit(solution)/shard_map/all_to_all | solution.py:27
  168.0 0.2 copy.159
  168.3 0.6 copy.162
  168.9 0.9 pad_maximum_fusion.6
  (112 shorter events, 3.2 us)
Async XLA Ops:
  0.6 12.9 %copy-start = (bf16[384,48]{0,1:T(8,128)(2,1)S(1)}, bf16[384,48]{0,1:T(8,128)(2,1)}, u32[]{:S(2)}) copy-start(bf16[384,48]{0,1:T(8,128)(2,1)} %param.27) | copy-start | bytes 110596
  1.9 11.3 %copy-start.3 = (bf16[24,384]{1,0:T(8,128)(2,1)S(1)}, bf16[24,384]{1,0:T(8,128)(2,1)}, u32[]{:S(2)}) copy-start(bf16[24,384]{1,0:T(8,128)(2,1)} %param.16) | copy-start | bytes 55300
  2.0 11.6 %copy-start.13 = (f32[384]{0:T(512)S(1)}, f32[384]{0:T(512)}, u32[]{:S(2)}) copy-start(f32[384]{0:T(512)} %param.25) | copy-start | bytes 4612
  2.0 11.8 %copy-start.10 = (bf16[384,2,48]{0,2,1:T(8,128)(2,1)S(1)}, bf16[384,2,48]{0,2,1:T(8,128)(2,1)}, u32[]{:S(2)}) copy-start(bf16[384,2,48]{0,2,1:T(8,128)(2,1)} %param.28) | copy-start | bytes 221188
  2.0 15.8 %copy-start.2 = (bf16[128,4,128]{2,1,0:T(4,128)(2,1)S(1)}, bf16[128,4,128]{2,1,0:T(4,128)(2,1)}, u32[]{:S(2)}) copy-start(bf16[128,4,128]{2,1,0:T(4,128)(2,1)} %param.19) | copy-start | bytes 393220
  2.8 15.2 %copy-start.11 = (bf16[384,48]{0,1:T(8,128)(2,1)S(1)}, bf16[384,48]{0,1:T(8,128)(2,1)}, u32[]{:S(2)}) copy-start(bf16[384,48]{0,1:T(8,128)(2,1)} %param.26) | copy-start | bytes 110596
  2.8 15.4 %copy-start.6 = (s32[768]{0:T(1024)S(1)}, s32[768]{0:T(1024)}, u32[]{:S(2)}) copy-start(s32[768]{0:T(1024)} %param.17) | copy-start | bytes 9220
  2.9 24.5 %copy-start.8 = (f32[128]{0:T(128)S(1)}, f32[128]{0:T(128)}, u32[]{:S(2)}) copy-start(f32[128]{0:T(128)} %param.18) | copy-start | bytes 1540
  2.9 29.6 %copy-start.4 = (bf16[48,384]{1,0:T(8,128)(2,1)S(1)}, bf16[48,384]{1,0:T(8,128)(2,1)}, u32[]{:S(2)}) copy-start(bf16[48,384]{1,0:T(8,128)(2,1)} %param.29) | copy-start | bytes 110596
  2.9 31.6 %all-to-all-start = ((bf16[8,16,2304]{2,1,0:T(8,128)(2,1)}), bf16[8,16,2304]{2,1,0:T(8,128)(2,1)S(1)}, u32[]{:S(2)}, u32[]{:S(2)}) async-start(bf16[8,16,2304]{2,1,0:T(8,128)(2,1)} %maximum_bitcast_fusion), calls=%async_computation | async-start | bytes 1179648 | tf_op jit(solution)/shard_map/all_to_all | solution.py:27
  14.0 6.3 %collective-permute-start.1 = (bf16[1,1,1,24,128]{4,3,2,1,0:T(8,128)(2,1)S(1)}, bf16[1,1,1,24,128]{4,3,2,1,0:T(8,128)(2,1)S(1)}, u32[]{:S(2)}, u32[]{:S(2)}) collective-permute-start(bf16[1,1,1,24,128]{4,3,2,1,0:T(8,128)(2,1)S(1)} %fusion.79), channel_id=1, source_target_pairs={{0,4},{2,6},{4,0},{6,2},{1,5},{3,7},{5,1},{7,3},{8,12},{10,14},{12... | collective-permute-start | bytes 18440 | tf_op jit(solution)/shard_map/ppermute | solution.py:32
  20.4 5.3 %collective-permute-start.2 = (bf16[2,1,1,24,128]{4,3,2,1,0:T(8,128)(2,1)S(1)}, bf16[2,1,1,24,128]{4,3,2,1,0:T(8,128)(2,1)S(1)}, u32[]{:S(2)}, u32[]{:S(2)}) collective-permute-start(bf16[2,1,1,24,128]{4,3,2,1,0:T(8,128)(2,1)S(1)} %pad_maximum_fusion.14), channel_id=1, source_target_pairs={{0,128},{64,192},{128,0},{192,64},{1,129},{65,193},{129,1},{193,65... | collective-permute-start | bytes 36872 | tf_op jit(solution)/shard_map/ppermute | solution.py:32
  25.7 6.6 %collective-permute-start.3 = (bf16[2,2,1,24,128]{4,3,2,1,0:T(8,128)(2,1)S(1)}, bf16[2,2,1,24,128]{4,3,2,1,0:T(8,128)(2,1)S(1)}, u32[]{:S(2)}, u32[]{:S(2)}) collective-permute-start(bf16[2,2,1,24,128]{4,3,2,1,0:T(8,128)(2,1)S(1)} %pad_maximum_fusion.13), channel_id=1, source_target_pairs={{0,32},{16,48},{32,0},{48,16},{1,33},{17,49},{33,1},{49,17},{2,34}... | collective-permute-start | bytes 73736 | tf_op jit(solution)/shard_map/ppermute | solution.py:32
  38.1 43.2 %copy-start.7 = (bf16[128,16]{0,1:T(8,128)(2,1)S(1)}, bf16[128,16]{0,1:T(8,128)(2,1)}, u32[]{:S(2)}) copy-start(bf16[128,16]{0,1:T(8,128)(2,1)} %param.24) | copy-start | bytes 12292
  38.1 55.7 %all-to-all-start.1 = ((bf16[128,2,2304]{2,1,0:T(2,128)(2,1)}), bf16[128,2,2304]{2,1,0:T(2,128)(2,1)S(1)}, u32[]{:S(2)}, u32[]{:S(2)}) async-start(bf16[128,2,2304]{2,1,0:T(2,128)(2,1)} %reshape.279), calls=%async_computation.1 | async-start | bytes 2359296 | tf_op jit(solution)/shard_map/all_to_all | solution.py:27
  49.1 30.6 %collective-permute-start.4 = (bf16[1,384,128]{2,1,0:T(8,128)(2,1)S(1)}, bf16[1,384,128]{2,1,0:T(8,128)(2,1)S(1)}, u32[]{:S(2)}, u32[]{:S(2)}) collective-permute-start(bf16[1,384,128]{2,1,0:T(8,128)(2,1)S(1)} %bitcast.164), channel_id=1, source_target_pairs={{0,1},{1,0},{2,3},{3,2},{4,5},{5,4},{6,7},{7,6},{8,9},{9,8},{10,11... | collective-permute-start | bytes 294920 | tf_op jit(solution)/shard_map/ppermute | solution.py:32
  79.8 4.7 %collective-permute-start.7 = (bf16[2,2,1,2,1,2,1,1,24,128]{9,8,7,6,5,4,3,2,1,0:T(8,128)(2,1)S(1)}, bf16[2,2,1,2,1,2,1,1,24,128]{9,8,7,6,5,4,3,2,1,0:T(8,128)(2,1)S(1)}, u32[]{:S(2)}, u32[]{:S(2)}) collective-permute-start(bf16[2,2,1,2,1,2,1,1,24,128]{9,8,7,6,5,4,3,2,1,0:T(8,128)(2,1)S(1)} %bitcast.162), channel_id=1, source_target_pairs={{0,2},{2,0},{4,6},{6,4},{1,3},{3,1},{5,7},{7,5},{8,10},{10,8},{12,... | collective-permute-start | bytes 294920 | tf_op jit(solution)/shard_map/ppermute | solution.py:32
  81.4 5.0 %collective-permute-start.5 = (bf16[2,1,1,192,128]{4,3,2,1,0:T(8,128)(2,1)S(1)}, bf16[2,1,1,192,128]{4,3,2,1,0:T(8,128)(2,1)S(1)}, u32[]{:S(2)}, u32[]{:S(2)}) collective-permute-start(bf16[2,1,1,192,128]{4,3,2,1,0:T(8,128)(2,1)S(1)} %get-tuple-element.29), channel_id=1, source_target_pairs={{0,2},{2,0},{4,6},{6,4},{1,3},{3,1},{5,7},{7,5},{8,10},{10,8},{12,... | collective-permute-start | bytes 294920 | tf_op jit(solution)/shard_map/ppermute | solution.py:32
  84.6 5.8 %collective-permute-start.8 = (bf16[2,2,2,2,1,2,1,1,24,128]{9,8,7,6,5,4,3,2,1,0:T(8,128)(2,1)S(1)}, bf16[2,2,2,2,1,2,1,1,24,128]{9,8,7,6,5,4,3,2,1,0:T(8,128)(2,1)S(1)}, u32[]{:S(2)}, u32[]{:S(2)}) collective-permute-start(bf16[2,2,2,2,1,2,1,1,24,128]{9,8,7,6,5,4,3,2,1,0:T(8,128)(2,1)S(1)} %pad_maximum_fusion.10), channel_id=1, source_target_pairs={{0,64},{64,0},{128,192},{192,128},{1,65},{65,1},{129,193},{193,129... | collective-permute-start | bytes 589832 | tf_op jit(solution)/shard_map/ppermute | solution.py:32
  86.5 7.3 %collective-permute-start.6 = (bf16[2,1,2,192,128]{4,3,2,1,0:T(8,128)(2,1)S(1)}, bf16[2,1,2,192,128]{4,3,2,1,0:T(8,128)(2,1)S(1)}, u32[]{:S(2)}, u32[]{:S(2)}) collective-permute-start(bf16[2,1,2,192,128]{4,3,2,1,0:T(8,128)(2,1)S(1)} %pad_maximum_fusion.9), channel_id=1, source_target_pairs={{0,4},{2,6},{4,0},{6,2},{1,5},{3,7},{5,1},{7,3},{8,12},{10,14},{12... | collective-permute-start | bytes 589832 | tf_op jit(solution)/shard_map/ppermute | solution.py:32
  91.1 8.1 %collective-permute-start.9 = (bf16[2,2,2,2,2,2,1,1,24,128]{9,8,7,6,5,4,3,2,1,0:T(8,128)(2,1)}, bf16[2,2,2,2,2,2,1,1,24,128]{9,8,7,6,5,4,3,2,1,0:T(8,128)(2,1)}, u32[]{:S(2)}, u32[]{:S(2)}) collective-permute-start(bf16[2,2,2,2,2,2,1,1,24,128]{9,8,7,6,5,4,3,2,1,0:T(8,128)(2,1)} %pad_maximum_fusion.8), channel_id=1, source_target_pairs={{0,16},{16,0},{32,48},{48,32},{1,17},{17,1},{33,49},{49,33},{2,18}... | collective-permute-start | bytes 1179656 | tf_op jit(solution)/shard_map/ppermute | solution.py:32
  94.8 6.5 %collective-permute-start = (bf16[16,24,768]{2,1,0:T(8,128)(2,1)S(1)}, bf16[16,24,768]{2,1,0:T(8,128)(2,1)S(1)}, u32[]{:S(2)}, u32[]{:S(2)}) collective-permute-start(bf16[16,24,768]{2,1,0:T(8,128)(2,1)S(1)} %pad_maximum_fusion.4), channel_id=1, source_target_pairs={{0,8},{8,0},{1,9},{9,1},{2,10},{10,2},{3,11},{11,3},{4,12},{12,4},... | collective-permute-start | bytes 1769480 | tf_op jit(solution)/shard_map/ppermute | solution.py:126
  101.3 15.9 %collective-permute-start.10 = (bf16[2,2,2,2,2,2,2,1,24,128]{9,8,7,6,5,4,3,2,1,0:T(8,128)(2,1)}, bf16[2,2,2,2,2,2,2,1,24,128]{9,8,7,6,5,4,3,2,1,0:T(8,128)(2,1)}, u32[]{:S(2)}, u32[]{:S(2)}) collective-permute-start(bf16[2,2,2,2,2,2,2,1,24,128]{9,8,7,6,5,4,3,2,1,0:T(8,128)(2,1)} %pad_maximum_fusion.3), channel_id=1, source_target_pairs={{0,8},{8,0},{1,9},{9,1},{2,10},{10,2},{3,11},{11,3},{4,12},{12,4},... | collective-permute-start | bytes 2359304 | tf_op jit(solution)/shard_map/ppermute | solution.py:32
  104.4 11.2 %copy-start.12 = (bf16[128,128]{1,0:T(8,128)(2,1)S(1)}, bf16[128,128]{1,0:T(8,128)(2,1)}, u32[]{:S(2)}) copy-start(bf16[128,128]{1,0:T(8,128)(2,1)} %param.20) | copy-start | bytes 98308
  104.4 33.4 %all-to-all-start.2 = ((bf16[128,2,1152]{2,1,0:T(2,128)(2,1)}), bf16[128,2,1152]{2,1,0:T(2,128)(2,1)S(1)}, u32[]{:S(2)}, u32[]{:S(2)}) async-start(bf16[128,2,1152]{2,1,0:T(2,128)(2,1)} %reshape.286), calls=%async_computation.2 | async-start | bytes 1179648 | tf_op jit(solution)/shard_map/all_to_all | solution.py:27
  138.3 1.0 copy-start.5
  138.3 1.0 copy-start.9
  139.2 1.3 copy-start.1
  140.5 0.7 copy-start.14

commit v7 on v6

--- a/solution.py
+++ b/solution.py
@@ -11,7 +11,8 @@
 LANES = 128
 ROW = ("x", "zl", "core")
 CHAN = ("y", "zh")
-OWN = ("x", "zl", "y", "zh")
+SWAP = ("zh", "y")
+OWN = ("x", "zl", "zh", "y")
 BF = jnp.bfloat16
 F32 = jnp.float32
 
@@ -73,7 +74,7 @@
     part = rows // nq
     spots = part * width
     r = lax.axis_index(ROW)
-    q = lax.axis_index(CHAN)
+    q = lax.axis_index(SWAP)
     core = lax.axis_index("core")
     live = token_mask.astype(F32)
 
@@ -108,9 +109,21 @@
     rest = doubled(rest[:, None, None], "y", 0, 2)
     rest = doubled(rest, "y", 1, 1).reshape(nq, -1, LANES)
 
+    def by_place(values, axis):
+        shape = values.shape
+        values = values.reshape(shape[:axis] + (nq // 2, 2, -1) + shape[axis + 1 :])
+        return values.swapaxes(axis, axis + 1).reshape(shape)
+
+    pair_gain = by_place(pair_gain, 0)
+    w_ab = by_place(w_ab, 0)
+    bias_gain = by_place(bias_gain, 0)
+    w_out_gate = by_place(by_place(w_out_gate, 0), 1)
+    w_tri_out = by_place(w_tri_out, 1)
+    w_bias = by_place(by_place(w_bias, 0), 1)
+
     sent = jnp.concatenate([pair[:, nq * t : nq * (t + 1)] for t in range(part)], axis=2)
     sent = sent.transpose(1, 0, 2)
-    full = swap(sent, CHAN).reshape(C, spots).astype(F32)
+    full = swap(sent, SWAP).reshape(C, spots).astype(F32)
     normed = layer_norm(full, pair_gain[:, None], 0).astype(BF)
     live_rows = lax.dynamic_slice_in_dim(live, r * rows, rows, 0).reshape(part, nq)
     live_rows = lax.dynamic_index_in_dim(live_rows, q, 1, keepdims=False)
@@ -152,8 +165,7 @@
     update = jnp.einsum("cp,cd->dp", product_normed, w_tri_out, preferred_element_type=F32)
     renewed = (full + out_gate * update).astype(BF)
     bias_input = layer_norm(renewed.astype(F32), bias_gain[:, None], 0).astype(BF)
-    by_head = w_bias.reshape(C, nq // 2, 2, -1).transpose(0, 2, 1, 3).reshape(w_bias.shape)
-    bias = jnp.einsum("cp,ch->hp", bias_input, by_head, preferred_element_type=F32)
+    bias = jnp.einsum("cp,ch->hp", bias_input, w_bias, preferred_element_type=F32)
 
     heads = H // nq
     head_size = D // H
@@ -175,11 +187,12 @@
     mixed = jnp.where(is_head, mixed.reshape(nq, heads, part, local), 0).sum(axis=1)
     heads_out = (mixed * gate_mine).astype(BF).transpose(1, 0, 2).reshape(part, D)
     mix = rest[:, 2 * rows :].reshape(nq, D // LANES, local, LANES).transpose(0, 2, 1, 3)
-    summed = jnp.dot(heads_out, mix.reshape(D, D), preferred_element_type=F32).astype(BF)
+    mix = by_place(mix.reshape(D, D), 1)
+    summed = jnp.dot(heads_out, mix, preferred_element_type=F32).astype(BF)
     summed = summed.reshape(part, nq, local).transpose(1, 0, 2)
     summed = jnp.pad(summed, ((0, 0), (0, chans - part), (0, LANES - local)))
     sent = jnp.concatenate([renewed.reshape(nq, chans, spots), summed], axis=2)
-    both = swap(sent, CHAN)
+    both = swap(sent, SWAP)
     pair_out = both[:, :, :spots].transpose(1, 0, 2).reshape(chans * nq, spots)
     pair_out = rows_in_order(pair_out, part, nq)
     attended = both[:, :part, spots : spots + local].transpose(1, 0, 2).reshape(rows, local)

time: 170 us -> 171 us (level)
  waiting for transfers between devices: 64.1 us -> 58.6 us
  local copies, waits for them, and re-layouts: 7.85 us -> 12.7 us
    all_to_all x3, waiting for transfers between devices: 21.1 us -> 13.4 us  [swap(): return lax.all_to_all(shard, axes, 0, 0, tiled=True)]
    ppermute x10, waiting for transfers between devices: 42.9 us -> 45.2 us  [doubled(): there = lax.ppermute(block, axis, [(i, i ^ 1 << bit) for i in range(size)])]
    transpose x0 -> x7, local copies, waits for them, and re-layouts: none -> 1.91 us  [by_place(): return values.swapaxes(axis, axis + 1).reshape(shape)]
  transfers between devices with their start and end apart: 14 -> 14, of which waited for: 11 -> 9; matrix products, arithmetic and copies ran while one was open for 7% -> 11% of each run, Pallas kernels for 0% -> 0%
where the time goes in v7:
time: 171 us; the launch traced here: 170 us
  waiting for transfers between devices  58.6 us (34%)
  starting transfers between devices  53.1 us (31%)
  blocking collectives  24.7 us (14%)
  local copies, waits for them, and re-layouts  12.7 us (7%)
  other arithmetic  11.6 us (7%)
  matrix products  7.71 us (5%)
    ppermute x10, waiting for transfers between devices, doubled(): there = lax.ppermute(block, axis, [(i, i ^ 1 << bit) for i in range(size)])  45.2 us
    all_to_all x3, starting transfers between devices, swap(): return lax.all_to_all(shard, axes, 0, 0, tiled=True)  32.7 us
    all_to_all x1, blocking collectives, swap(): return lax.all_to_all(shard, axes, 0, 0, tiled=True)  24.7 us
    ppermute x10, starting transfers between devices, doubled(): there = lax.ppermute(block, axis, [(i, i ^ 1 << bit) for i in range(size)])  20.1 us
    all_to_all x3, waiting for transfers between devices, swap(): return lax.all_to_all(shard, axes, 0, 0, tiled=True)  13.4 us
    select_n x10, other arithmetic, doubled(): jnp.where(low, block, there)  3.5 us
  transfers between devices with their start and end apart: 14, of which 9 were waited for; matrix products, arithmetic and copies ran while one was open for 11% of the time, Pallas kernels for 0%

profile of v7, /device:TPU:32, one launch (start us, length us, event | category | flops | bytes accessed | tf_op | source)
XLA Modules:
  0.0 169.8 jit_solution(13914174729316023929)
XLA Ops:
  0.6 1.2 fusion.85
  2.0 0.9 maximum_bitcast_fusion
  2.9 10.3 %all-to-all-start = ((bf16[8,16,2304]{2,1,0:T(8,128)(2,1)}), bf16[8,16,2304]{2,1,0:T(8,128)(2,1)S(1)}, u32[]{:S(2)}, u32[]{:S(2)}) async-start(bf16[8,16,2304]{2,1,0:T(8,128)(2,1)} %maximum_bitcast_fusion), calls=%async_computation | async-start | bytes 1179648 | tf_op jit(solution)/shard_map/all_to_all | solution.py:28
  13.3 0.2 fusion.61
  13.5 0.2 convolution_convert_fusion.5
  13.7 0.2 convolution_convert_fusion.4
  14.0 3.6 %collective-permute-start.1 = (bf16[1,1,1,24,128]{4,3,2,1,0:T(8,128)(2,1)S(1)}, bf16[1,1,1,24,128]{4,3,2,1,0:T(8,128)(2,1)S(1)}, u32[]{:S(2)}, u32[]{:S(2)}) collective-permute-start(bf16[1,1,1,24,128]{4,3,2,1,0:T(8,128)(2,1)S(1)} %fusion.76), channel_id=1, source_target_pairs={{0,4},{2,6},{4,0},{6,2},{1,5},{3,7},{5,1},{7,3},{8,12},{10,14},{12... | collective-permute-start | bytes 18440 | tf_op jit(solution)/shard_map/ppermute | solution.py:33
  17.6 0.2 fusion.69
  17.8 2.5 %collective-permute-done.1 = bf16[1,1,1,24,128]{4,3,2,1,0:T(8,128)(2,1)S(1)} collective-permute-done((bf16[1,1,1,24,128]{4,3,2,1,0:T(8,128)(2,1)S(1)}, bf16[1,1,1,24,128]{4,3,2,1,0:T(8,128)(2,1)S(1)}, u32[]{:S(2)}, u32[]{:S(2)}) %collective-permute-start.1) | collective-permute-done | bytes 6176 | tf_op jit(solution)/shard_map/ppermute | solution.py:33
  20.4 3.1 %collective-permute-start.2 = (bf16[2,1,1,24,128]{4,3,2,1,0:T(8,128)(2,1)S(1)}, bf16[2,1,1,24,128]{4,3,2,1,0:T(8,128)(2,1)S(1)}, u32[]{:S(2)}, u32[]{:S(2)}) collective-permute-start(bf16[2,1,1,24,128]{4,3,2,1,0:T(8,128)(2,1)S(1)} %pad_maximum_fusion.14), channel_id=1, source_target_pairs={{0,128},{64,192},{128,0},{192,64},{1,129},{65,193},{129,1},{193,65... | collective-permute-start | bytes 36872 | tf_op jit(solution)/shard_map/ppermute | solution.py:33
  23.5 0.2 convolution_convert_fusion.3
  23.9 0.2 dynamic-slice_reduce_fusion
  24.1 1.6 collective-permute-done.2
  25.7 1.6 collective-permute-start.3
  27.5 4.8 %collective-permute-done.3 = bf16[2,2,1,24,128]{4,3,2,1,0:T(8,128)(2,1)S(1)} collective-permute-done((bf16[2,2,1,24,128]{4,3,2,1,0:T(8,128)(2,1)S(1)}, bf16[2,2,1,24,128]{4,3,2,1,0:T(8,128)(2,1)S(1)}, u32[]{:S(2)}, u32[]{:S(2)}) %collective-permute-start.3) | collective-permute-done | bytes 24608 | tf_op jit(solution)/shard_map/ppermute | solution.py:33
  32.5 1.1 all-to-all-done
  33.9 0.2 multiply_convert_fusion
  34.1 0.5 fusion.8
  34.6 0.5 fusion.11
  35.1 0.4 fusion.17
  35.5 0.4 fusion.18
  36.1 1.2 reshape.333
  37.3 12.4 %all-to-all-start.1 = ((bf16[128,2,2304]{2,1,0:T(2,128)(2,1)}), bf16[128,2,2304]{2,1,0:T(2,128)(2,1)S(1)}, u32[]{:S(2)}, u32[]{:S(2)}) async-start(bf16[128,2,2304]{2,1,0:T(2,128)(2,1)} %reshape.333), calls=%async_computation.1 | async-start | bytes 2359296 | tf_op jit(solution)/shard_map/all_to_all | solution.py:28
  49.8 4.6 %collective-permute-start.4 = (bf16[1,384,128]{2,1,0:T(8,128)(2,1)S(1)}, bf16[1,384,128]{2,1,0:T(8,128)(2,1)S(1)}, u32[]{:S(2)}, u32[]{:S(2)}) collective-permute-start(bf16[1,384,128]{2,1,0:T(8,128)(2,1)S(1)} %bitcast.192), channel_id=1, source_target_pairs={{0,1},{1,0},{2,3},{3,2},{4,5},{5,4},{6,7},{7,6},{8,9},{9,8},{10,11... | collective-permute-start | bytes 294920 | tf_op jit(solution)/shard_map/ppermute | solution.py:33
  54.4 26.5 %collective-permute-done.4 = bf16[1,384,128]{2,1,0:T(8,128)(2,1)S(1)} collective-permute-done((bf16[1,384,128]{2,1,0:T(8,128)(2,1)S(1)}, bf16[1,384,128]{2,1,0:T(8,128)(2,1)S(1)}, u32[]{:S(2)}, u32[]{:S(2)}) %collective-permute-start.4) | collective-permute-done | bytes 98336 | tf_op jit(solution)/shard_map/ppermute | solution.py:33
  81.0 1.6 collective-permute-start.7
  82.5 0.2 reshape_reshape.9
  83.5 2.9 %collective-permute-done.7 = bf16[2,2,1,2,1,2,1,1,24,128]{9,8,7,6,5,4,3,2,1,0:T(8,128)(2,1)S(1)} collective-permute-done((bf16[2,2,1,2,1,2,1,1,24,128]{9,8,7,6,5,4,3,2,1,0:T(8,128)(2,1)S(1)}, bf16[2,2,1,2,1,2,1,1,24,128]{9,8,7,6,5,4,3,2,1,0:T(8,128)(2,1)S(1)}, u32[]{:S(2)}, u32[]{:S(2)}) %collective-permute-start.7) | collective-permute-done | bytes 98336 | tf_op jit(solution)/shard_map/ppermute | solution.py:33
  86.5 1.6 collective-permute-start.8
  88.1 0.8 collective-permute-start.5
  88.9 3.3 %collective-permute-done.8 = bf16[2,2,2,2,1,2,1,1,24,128]{9,8,7,6,5,4,3,2,1,0:T(8,128)(2,1)S(1)} collective-permute-done((bf16[2,2,2,2,1,2,1,1,24,128]{9,8,7,6,5,4,3,2,1,0:T(8,128)(2,1)S(1)}, bf16[2,2,2,2,1,2,1,1,24,128]{9,8,7,6,5,4,3,2,1,0:T(8,128)(2,1)S(1)}, u32[]{:S(2)}, u32[]{:S(2)}) %collective-permute-start.8) | collective-permute-done | bytes 196640 | tf_op jit(solution)/shard_map/ppermute | solution.py:33
  92.2 0.8 pad_maximum_fusion.8
  93.1 0.8 fusion.82
  94.1 0.3 collective-permute-start
  94.5 3.2 %collective-permute-start.6 = (bf16[2,1,2,192,128]{4,3,2,1,0:T(8,128)(2,1)S(1)}, bf16[2,1,2,192,128]{4,3,2,1,0:T(8,128)(2,1)}, u32[]{:S(2)}, u32[]{:S(2)}) collective-permute-start(bf16[2,1,2,192,128]{4,3,2,1,0:T(8,128)(2,1)S(1)} %pad_maximum_fusion.9), channel_id=1, source_target_pairs={{0,4},{2,6},{4,0},{6,2},{1,5},{3,7},{5,1},{7,3},{8,12},{10,14},{12... | collective-permute-start | bytes 589832 | tf_op jit(solution)/shard_map/ppermute | solution.py:33
  97.7 3.4 %collective-permute-done.9 = bf16[2,2,2,2,2,2,1,1,24,128]{9,8,7,6,5,4,3,2,1,0:T(8,128)(2,1)} collective-permute-done((bf16[2,2,2,2,2,2,1,1,24,128]{9,8,7,6,5,4,3,2,1,0:T(8,128)(2,1)}, bf16[2,2,2,2,2,2,1,1,24,128]{9,8,7,6,5,4,3,2,1,0:T(8,128)(2,1)}, u32[]{:S(2)}, u32[]{:S(2)}) %collective-permute-start.9) | collective-permute-done | bytes 393248 | tf_op jit(solution)/shard_map/ppermute | solution.py:33
  101.1 1.1 broadcast_select_fusion.3
  102.2 1.0 pad_maximum_fusion.3
  103.2 0.3 select_bitcast_fusion.1
  103.7 0.5 convolution_convert_fusion.2
  104.2 0.5 convolution_convert_fusion.1
  104.8 0.5 convolution_convert_fusion
  105.4 0.9 reshape.340
  106.3 10.0 %all-to-all-start.2 = ((bf16[128,2,1152]{2,1,0:T(2,128)(2,1)}), bf16[128,2,1152]{2,1,0:T(2,128)(2,1)S(1)}, u32[]{:S(2)}, u32[]{:S(2)}) async-start(bf16[128,2,1152]{2,1,0:T(2,128)(2,1)} %reshape.340), calls=%async_computation.2 | async-start | bytes 1179648 | tf_op jit(solution)/shard_map/all_to_all | solution.py:28
  116.3 1.0 broadcast_select_fusion.7
  117.3 0.7 slice.178
  118.1 1.4 copy.141
  119.5 1.3 reshape_reshape.11
  120.8 1.7 %copy.142 = bf16[384,2,4,48]{0,3,2,1:T(8,128)(2,1)} copy(bf16[384,2,4,48]{0,3,1,2:T(8,128)(2,1)} %bitcast.183) | data formatting | bytes 589824 | tf_op jit(solution)/shard_map/transpose | solution.py:115
  122.5 1.5 fusion.5
  124.0 1.3 broadcast_select_fusion.1
  125.4 12.2 %all-to-all-done.2 = bf16[128,2,1152]{2,1,0:T(2,128)(2,1)S(1)} async-done(((bf16[128,2,1152]{2,1,0:T(2,128)(2,1)}), bf16[128,2,1152]{2,1,0:T(2,128)(2,1)S(1)}, u32[]{:S(2)}, u32[]{:S(2)}) %all-to-all-start.2) | async-done | bytes 589856 | tf_op jit(solution)/shard_map/all_to_all | solution.py:28
  137.7 0.5 convert_reduce_fusion.1
  138.2 0.8 fusion.28
  139.1 0.8 fusion.30
  139.9 0.4 copy-done.1
  140.3 0.4 convert_reduce_fusion
  140.9 0.3 convolution_bitcast_fusion
  141.2 0.5 fusion.41
  141.8 0.2 fusion.86
  142.0 0.7 fusion.19
  143.3 24.7 %all_to_all.20 = bf16[8,16,2432]{2,1,0:T(8,128)(2,1)S(1)} all-to-all(bf16[8,16,2432]{2,1,0:T(8,128)(2,1)S(1)} %fusion.48), channel_id=1, replica_groups=mesh['x'=4,'zl'=4,'core'=2,'y'=4,'zh'=2] {'zh','y'}, dimensions={0} | all-to-all | bytes 1245184 | tf_op jit(solution)/shard_map/all_to_all | solution.py:28
  168.3 0.6 copy.173
  168.9 0.9 pad_maximum_fusion.6
  (127 shorter events, 4.2 us)
Async XLA Ops:
  0.6 12.9 %copy-start = (bf16[384,48]{0,1:T(8,128)(2,1)S(1)}, bf16[384,48]{0,1:T(8,128)(2,1)}, u32[]{:S(2)}) copy-start(bf16[384,48]{0,1:T(8,128)(2,1)} %param.27) | copy-start | bytes 110596
  1.9 11.2 %copy-start.4 = (bf16[24,384]{1,0:T(8,128)(2,1)S(1)}, bf16[24,384]{1,0:T(8,128)(2,1)}, u32[]{:S(2)}) copy-start(bf16[24,384]{1,0:T(8,128)(2,1)} %param.16) | copy-start | bytes 55300
  2.0 11.6 %copy-start.15 = (f32[384]{0:T(512)S(1)}, f32[384]{0:T(512)}, u32[]{:S(2)}) copy-start(f32[384]{0:T(512)} %param.25) | copy-start | bytes 4612
  2.0 11.8 %copy-start.13 = (bf16[384,2,48]{0,2,1:T(8,128)(2,1)S(1)}, bf16[384,2,48]{0,2,1:T(8,128)(2,1)}, u32[]{:S(2)}) copy-start(bf16[384,2,48]{0,2,1:T(8,128)(2,1)} %param.28) | copy-start | bytes 221188
  2.0 21.6 %copy-start.14 = (bf16[384,48]{0,1:T(8,128)(2,1)S(1)}, bf16[384,48]{0,1:T(8,128)(2,1)}, u32[]{:S(2)}) copy-start(bf16[384,48]{0,1:T(8,128)(2,1)} %param.26) | copy-start | bytes 110596
  2.8 20.9 %copy-start.8 = (s32[768]{0:T(1024)S(1)}, s32[768]{0:T(1024)}, u32[]{:S(2)}) copy-start(s32[768]{0:T(1024)} %param.17) | copy-start | bytes 9220
  2.8 24.5 %copy-start.11 = (f32[128]{0:T(128)S(1)}, f32[128]{0:T(128)}, u32[]{:S(2)}) copy-start(f32[128]{0:T(128)} %param.18) | copy-start | bytes 1540
  2.9 24.6 %copy-start.3 = (bf16[128,4,128]{2,1,0:T(4,128)(2,1)S(1)}, bf16[128,4,128]{2,1,0:T(4,128)(2,1)}, u32[]{:S(2)}) copy-start(bf16[128,4,128]{2,1,0:T(4,128)(2,1)} %param.19) | copy-start | bytes 393220
  2.9 30.7 %all-to-all-start = ((bf16[8,16,2304]{2,1,0:T(8,128)(2,1)}), bf16[8,16,2304]{2,1,0:T(8,128)(2,1)S(1)}, u32[]{:S(2)}, u32[]{:S(2)}) async-start(bf16[8,16,2304]{2,1,0:T(8,128)(2,1)} %maximum_bitcast_fusion), calls=%async_computation | async-start | bytes 1179648 | tf_op jit(solution)/shard_map/all_to_all | solution.py:28
  14.0 6.3 %collective-permute-start.1 = (bf16[1,1,1,24,128]{4,3,2,1,0:T(8,128)(2,1)S(1)}, bf16[1,1,1,24,128]{4,3,2,1,0:T(8,128)(2,1)S(1)}, u32[]{:S(2)}, u32[]{:S(2)}) collective-permute-start(bf16[1,1,1,24,128]{4,3,2,1,0:T(8,128)(2,1)S(1)} %fusion.76), channel_id=1, source_target_pairs={{0,4},{2,6},{4,0},{6,2},{1,5},{3,7},{5,1},{7,3},{8,12},{10,14},{12... | collective-permute-start | bytes 18440 | tf_op jit(solution)/shard_map/ppermute | solution.py:33
  20.4 5.3 %collective-permute-start.2 = (bf16[2,1,1,24,128]{4,3,2,1,0:T(8,128)(2,1)S(1)}, bf16[2,1,1,24,128]{4,3,2,1,0:T(8,128)(2,1)S(1)}, u32[]{:S(2)}, u32[]{:S(2)}) collective-permute-start(bf16[2,1,1,24,128]{4,3,2,1,0:T(8,128)(2,1)S(1)} %pad_maximum_fusion.14), channel_id=1, source_target_pairs={{0,128},{64,192},{128,0},{192,64},{1,129},{65,193},{129,1},{193,65... | collective-permute-start | bytes 36872 | tf_op jit(solution)/shard_map/ppermute | solution.py:33
  25.7 6.6 %collective-permute-start.3 = (bf16[2,2,1,24,128]{4,3,2,1,0:T(8,128)(2,1)S(1)}, bf16[2,2,1,24,128]{4,3,2,1,0:T(8,128)(2,1)S(1)}, u32[]{:S(2)}, u32[]{:S(2)}) collective-permute-start(bf16[2,2,1,24,128]{4,3,2,1,0:T(8,128)(2,1)S(1)} %pad_maximum_fusion.13), channel_id=1, source_target_pairs={{0,32},{16,48},{32,0},{48,16},{1,33},{17,49},{33,1},{49,17},{2,34}... | collective-permute-start | bytes 73736 | tf_op jit(solution)/shard_map/ppermute | solution.py:33
  37.3 12.5 %copy-start.5 = (bf16[48,384]{1,0:T(8,128)(2,1)S(1)}, bf16[48,384]{1,0:T(8,128)(2,1)}, u32[]{:S(2)}) copy-start(bf16[48,384]{1,0:T(8,128)(2,1)} %param.29) | copy-start | bytes 110596
  37.3 45.2 %copy-start.6 = (bf16[128,128]{1,0:T(8,128)(2,1)S(1)}, bf16[128,128]{1,0:T(8,128)(2,1)}, u32[]{:S(2)}) copy-start(bf16[128,128]{1,0:T(8,128)(2,1)} %param.20) | copy-start | bytes 98308
  37.3 55.9 %all-to-all-start.1 = ((bf16[128,2,2304]{2,1,0:T(2,128)(2,1)}), bf16[128,2,2304]{2,1,0:T(2,128)(2,1)S(1)}, u32[]{:S(2)}, u32[]{:S(2)}) async-start(bf16[128,2,2304]{2,1,0:T(2,128)(2,1)} %reshape.333), calls=%async_computation.1 | async-start | bytes 2359296 | tf_op jit(solution)/shard_map/all_to_all | solution.py:28
  49.7 33.2 %copy-start.7 = (bf16[128,128]{1,0:T(8,128)(2,1)S(1)}, bf16[128,128]{1,0:T(8,128)(2,1)}, u32[]{:S(2)}) copy-start(bf16[128,128]{1,0:T(8,128)(2,1)} %param.22) | copy-start | bytes 98308
  49.7 33.3 %copy-start.9 = (bf16[128,16]{0,1:T(8,128)(2,1)S(1)}, bf16[128,16]{0,1:T(8,128)(2,1)}, u32[]{:S(2)}) copy-start(bf16[128,16]{0,1:T(8,128)(2,1)} %param.24) | copy-start | bytes 12292
  49.7 33.5 %copy-start.12 = (f32[128]{0:T(128)S(1)}, f32[128]{0:T(128)}, u32[]{:S(2)}) copy-start(f32[128]{0:T(128)} %param.23) | copy-start | bytes 1540
  49.8 31.1 %collective-permute-start.4 = (bf16[1,384,128]{2,1,0:T(8,128)(2,1)S(1)}, bf16[1,384,128]{2,1,0:T(8,128)(2,1)S(1)}, u32[]{:S(2)}, u32[]{:S(2)}) collective-permute-start(bf16[1,384,128]{2,1,0:T(8,128)(2,1)S(1)} %bitcast.192), channel_id=1, source_target_pairs={{0,1},{1,0},{2,3},{3,2},{4,5},{5,4},{6,7},{7,6},{8,9},{9,8},{10,11... | collective-permute-start | bytes 294920 | tf_op jit(solution)/shard_map/ppermute | solution.py:33
  81.0 5.5 %collective-permute-start.7 = (bf16[2,2,1,2,1,2,1,1,24,128]{9,8,7,6,5,4,3,2,1,0:T(8,128)(2,1)S(1)}, bf16[2,2,1,2,1,2,1,1,24,128]{9,8,7,6,5,4,3,2,1,0:T(8,128)(2,1)S(1)}, u32[]{:S(2)}, u32[]{:S(2)}) collective-permute-start(bf16[2,2,1,2,1,2,1,1,24,128]{9,8,7,6,5,4,3,2,1,0:T(8,128)(2,1)S(1)} %bitcast.186), channel_id=1, source_target_pairs={{0,2},{2,0},{4,6},{6,4},{1,3},{3,1},{5,7},{7,5},{8,10},{10,8},{12,... | collective-permute-start | bytes 294920 | tf_op jit(solution)/shard_map/ppermute | solution.py:33
  86.5 5.8 %collective-permute-start.8 = (bf16[2,2,2,2,1,2,1,1,24,128]{9,8,7,6,5,4,3,2,1,0:T(8,128)(2,1)S(1)}, bf16[2,2,2,2,1,2,1,1,24,128]{9,8,7,6,5,4,3,2,1,0:T(8,128)(2,1)S(1)}, u32[]{:S(2)}, u32[]{:S(2)}) collective-permute-start(bf16[2,2,2,2,1,2,1,1,24,128]{9,8,7,6,5,4,3,2,1,0:T(8,128)(2,1)S(1)} %pad_maximum_fusion.10), channel_id=1, source_target_pairs={{0,64},{64,0},{128,192},{192,128},{1,65},{65,1},{129,193},{193,129... | collective-permute-start | bytes 589832 | tf_op jit(solution)/shard_map/ppermute | solution.py:33
  88.1 6.3 %collective-permute-start.5 = (bf16[2,1,1,192,128]{4,3,2,1,0:T(8,128)(2,1)S(1)}, bf16[2,1,1,192,128]{4,3,2,1,0:T(8,128)(2,1)S(1)}, u32[]{:S(2)}, u32[]{:S(2)}) collective-permute-start(bf16[2,1,1,192,128]{4,3,2,1,0:T(8,128)(2,1)S(1)} %get-tuple-element.29), channel_id=1, source_target_pairs={{0,2},{2,0},{4,6},{6,4},{1,3},{3,1},{5,7},{7,5},{8,10},{10,8},{12,... | collective-permute-start | bytes 294920 | tf_op jit(solution)/shard_map/ppermute | solution.py:33
  93.0 8.1 %collective-permute-start.9 = (bf16[2,2,2,2,2,2,1,1,24,128]{9,8,7,6,5,4,3,2,1,0:T(8,128)(2,1)}, bf16[2,2,2,2,2,2,1,1,24,128]{9,8,7,6,5,4,3,2,1,0:T(8,128)(2,1)}, u32[]{:S(2)}, u32[]{:S(2)}) collective-permute-start(bf16[2,2,2,2,2,2,1,1,24,128]{9,8,7,6,5,4,3,2,1,0:T(8,128)(2,1)} %pad_maximum_fusion.8), channel_id=1, source_target_pairs={{0,16},{16,0},{32,48},{48,32},{1,17},{17,1},{33,49},{49,33},{2,18}... | collective-permute-start | bytes 1179656 | tf_op jit(solution)/shard_map/ppermute | solution.py:33
  94.1 9.1 %collective-permute-start = (bf16[16,24,768]{2,1,0:T(8,128)(2,1)S(1)}, bf16[16,24,768]{2,1,0:T(8,128)(2,1)S(1)}, u32[]{:S(2)}, u32[]{:S(2)}) collective-permute-start(bf16[16,24,768]{2,1,0:T(8,128)(2,1)S(1)} %pad_maximum_fusion.4), channel_id=1, source_target_pairs={{0,8},{8,0},{1,9},{9,1},{2,10},{10,2},{3,11},{11,3},{4,12},{12,4},... | collective-permute-start | bytes 1769480 | tf_op jit(solution)/shard_map/ppermute | solution.py:139
  94.5 21.8 %collective-permute-start.6 = (bf16[2,1,2,192,128]{4,3,2,1,0:T(8,128)(2,1)S(1)}, bf16[2,1,2,192,128]{4,3,2,1,0:T(8,128)(2,1)}, u32[]{:S(2)}, u32[]{:S(2)}) collective-permute-start(bf16[2,1,2,192,128]{4,3,2,1,0:T(8,128)(2,1)S(1)} %pad_maximum_fusion.9), channel_id=1, source_target_pairs={{0,4},{2,6},{4,0},{6,2},{1,5},{3,7},{5,1},{7,3},{8,12},{10,14},{12... | collective-permute-start | bytes 589832 | tf_op jit(solution)/shard_map/ppermute | solution.py:33
  103.2 20.8 %collective-permute-start.10 = (bf16[2,2,2,2,2,2,2,1,24,128]{9,8,7,6,5,4,3,2,1,0:T(8,128)(2,1)}, bf16[2,2,2,2,2,2,2,1,24,128]{9,8,7,6,5,4,3,2,1,0:T(8,128)(2,1)}, u32[]{:S(2)}, u32[]{:S(2)}) collective-permute-start(bf16[2,2,2,2,2,2,2,1,24,128]{9,8,7,6,5,4,3,2,1,0:T(8,128)(2,1)} %pad_maximum_fusion.3), channel_id=1, source_target_pairs={{0,8},{8,0},{1,9},{9,1},{2,10},{10,2},{3,11},{11,3},{4,12},{12,4},... | collective-permute-start | bytes 2359304 | tf_op jit(solution)/shard_map/ppermute | solution.py:33
  106.3 31.4 %all-to-all-start.2 = ((bf16[128,2,1152]{2,1,0:T(2,128)(2,1)}), bf16[128,2,1152]{2,1,0:T(2,128)(2,1)S(1)}, u32[]{:S(2)}, u32[]{:S(2)}) async-start(bf16[128,2,1152]{2,1,0:T(2,128)(2,1)} %reshape.340), calls=%async_computation.2 | async-start | bytes 1179648 | tf_op jit(solution)/shard_map/all_to_all | solution.py:28
  125.4 13.6 %copy-start.10 = (f32[128]{0:T(128)S(1)}, f32[128]{0:T(128)}, u32[]{:S(2)}) copy-start(f32[128]{0:T(128)} %param.21) | copy-start | bytes 1540
  139.1 1.3 copy-start.1
  142.0 1.0 copy-start.2

commit v8 on v6

--- a/solution.py
+++ b/solution.py
@@ -125,6 +125,8 @@
     right_here = rows_in_order(edges[:, :, :half].reshape(C, spots), part, nq)
     right_there = lax.ppermute(right_here, "core", [(0, 1), (1, 0)])
     left_owned = edges[:, :, half:].reshape(C, spots)
+    left_owned = [left_owned[:, width * t : width * (t + 1)] for t in range(part)]
+    left_owned = jnp.concatenate(left_owned, axis=0)
     first = core == 0
     right_owned = jnp.stack(
         [
@@ -133,17 +135,13 @@
         ],
         axis=1,
     ).reshape(2 * C * part, width)
-    owned = [
-        lax.dot_general(
-            left_owned[:, width * t : width * (t + 1)],
-            right_owned,
-            (((1,), (1,)), ((), ())),
-            preferred_element_type=F32,
-        ).astype(BF)
-        for t in range(part)
-    ]
-    owned = jnp.concatenate(owned, axis=1).reshape(C, 2, half)
+    owned = lax.dot_general(
+        left_owned, right_owned, (((1,), (1,)), ((), ())), preferred_element_type=F32
+    ).astype(BF)
+    owned = jnp.concatenate([owned[C * t : C * (t + 1)] for t in range(part)], axis=1)
+    owned = owned.reshape(C, 2, half)
     product = swap(owned, OWN).reshape(C, spots)
+    product = lax.optimization_barrier(product)
 
     product_normed = layer_norm(product.astype(F32), x_gain[:, None], 0).astype(BF)
     out_gate = jax.nn.sigmoid(

time: 170 us -> 154 us (0.906)
  waiting for transfers between devices: 64.1 us -> 50.1 us
    ppermute x10, waiting for transfers between devices: 42.9 us -> 20.8 us  [doubled(): there = lax.ppermute(block, axis, [(i, i ^ 1 << bit) for i in range(size)])]
    all_to_all x3, waiting for transfers between devices: 21.1 us -> 29.3 us  [swap(): return lax.all_to_all(shard, axes, 0, 0, tiled=True)]
  transfers between devices with their start and end apart: 14 -> 14, of which waited for: 11 -> 8; matrix products, arithmetic and copies ran while one was open for 7% -> 10% of each run, Pallas kernels for 0% -> 0%
where the time goes in v8:
time: 154 us; the launch traced here: 153 us
  starting transfers between devices  53.6 us (35%)
  waiting for transfers between devices  50.1 us (33%)
  blocking collectives  24.6 us (16%)
  other arithmetic  8.96 us (6%)
  local copies, waits for them, and re-layouts  7.62 us (5%)
  matrix products  6.85 us (4%)
    all_to_all x3, starting transfers between devices, swap(): return lax.all_to_all(shard, axes, 0, 0, tiled=True)  31.8 us
    all_to_all x3, waiting for transfers between devices, swap(): return lax.all_to_all(shard, axes, 0, 0, tiled=True)  29.3 us
    all_to_all x1, blocking collectives, swap(): return lax.all_to_all(shard, axes, 0, 0, tiled=True)  24.6 us
    ppermute x10, starting transfers between devices, doubled(): there = lax.ppermute(block, axis, [(i, i ^ 1 << bit) for i in range(size)])  21.8 us
    ppermute x10, waiting for transfers between devices, doubled(): there = lax.ppermute(block, axis, [(i, i ^ 1 << bit) for i in range(size)])  20.8 us
  transfers between devices with their start and end apart: 14, of which 8 were waited for; matrix products, arithmetic and copies ran while one was open for 10% of the time, Pallas kernels for 0%

profile of v8, /device:TPU:32, one launch (start us, length us, event | category | flops | bytes accessed | tf_op | source)
XLA Modules:
  0.0 153.1 jit_solution(9176228964363790847)
XLA Ops:
  0.6 1.2 fusion.99
  2.0 0.9 maximum_bitcast_fusion
  2.9 10.3 %all-to-all-start = ((bf16[8,16,2304]{2,1,0:T(8,128)(2,1)}), bf16[8,16,2304]{2,1,0:T(8,128)(2,1)S(1)}, u32[]{:S(2)}, u32[]{:S(2)}) async-start(bf16[8,16,2304]{2,1,0:T(8,128)(2,1)} %maximum_bitcast_fusion), calls=%async_computation | async-start | bytes 1179648 | tf_op jit(solution)/shard_map/all_to_all | solution.py:27
  13.2 0.1 convert_reduce_fusion.3
  13.3 0.2 fusion.72
  13.5 0.2 convolution_convert_fusion.3
  13.7 0.2 convolution_convert_fusion.2
  14.0 3.6 %collective-permute-start.1 = (bf16[1,1,1,24,128]{4,3,2,1,0:T(8,128)(2,1)S(1)}, bf16[1,1,1,24,128]{4,3,2,1,0:T(8,128)(2,1)S(1)}, u32[]{:S(2)}, u32[]{:S(2)}) collective-permute-start(bf16[1,1,1,24,128]{4,3,2,1,0:T(8,128)(2,1)S(1)} %fusion.87), channel_id=1, source_target_pairs={{0,4},{2,6},{4,0},{6,2},{1,5},{3,7},{5,1},{7,3},{8,12},{10,14},{12... | collective-permute-start | bytes 18440 | tf_op jit(solution)/shard_map/ppermute | solution.py:32
  17.6 0.2 fusion.80
  17.8 0.2 fusion.100
  18.0 0.2 convolution_convert_fusion.1
  18.4 0.2 dynamic-slice_reduce_fusion
  18.6 1.8 %collective-permute-done.1 = bf16[1,1,1,24,128]{4,3,2,1,0:T(8,128)(2,1)S(1)} collective-permute-done((bf16[1,1,1,24,128]{4,3,2,1,0:T(8,128)(2,1)S(1)}, bf16[1,1,1,24,128]{4,3,2,1,0:T(8,128)(2,1)S(1)}, u32[]{:S(2)}, u32[]{:S(2)}) %collective-permute-start.1) | collective-permute-done | bytes 6176 | tf_op jit(solution)/shard_map/ppermute | solution.py:32
  20.4 3.1 %collective-permute-start.2 = (bf16[2,1,1,24,128]{4,3,2,1,0:T(8,128)(2,1)S(1)}, bf16[2,1,1,24,128]{4,3,2,1,0:T(8,128)(2,1)S(1)}, u32[]{:S(2)}, u32[]{:S(2)}) collective-permute-start(bf16[2,1,1,24,128]{4,3,2,1,0:T(8,128)(2,1)S(1)} %pad_maximum_fusion.14), channel_id=1, source_target_pairs={{0,128},{64,192},{128,0},{192,64},{1,129},{65,193},{129,1},{193,65... | collective-permute-start | bytes 36872 | tf_op jit(solution)/shard_map/ppermute | solution.py:32
  23.6 2.1 %collective-permute-done.2 = bf16[2,1,1,24,128]{4,3,2,1,0:T(8,128)(2,1)S(1)} collective-permute-done((bf16[2,1,1,24,128]{4,3,2,1,0:T(8,128)(2,1)S(1)}, bf16[2,1,1,24,128]{4,3,2,1,0:T(8,128)(2,1)S(1)}, u32[]{:S(2)}, u32[]{:S(2)}) %collective-permute-start.2) | collective-permute-done | bytes 12320 | tf_op jit(solution)/shard_map/ppermute | solution.py:32
  25.7 1.6 %collective-permute-start.3 = (bf16[2,2,1,24,128]{4,3,2,1,0:T(8,128)(2,1)S(1)}, bf16[2,2,1,24,128]{4,3,2,1,0:T(8,128)(2,1)S(1)}, u32[]{:S(2)}, u32[]{:S(2)}) collective-permute-start(bf16[2,2,1,24,128]{4,3,2,1,0:T(8,128)(2,1)S(1)} %pad_maximum_fusion.13), channel_id=1, source_target_pairs={{0,32},{16,48},{32,0},{48,16},{1,33},{17,49},{33,1},{49,17},{2,34}... | collective-permute-start | bytes 73736 | tf_op jit(solution)/shard_map/ppermute | solution.py:32
  27.4 5.0 %collective-permute-done.3 = bf16[2,2,1,24,128]{4,3,2,1,0:T(8,128)(2,1)S(1)} collective-permute-done((bf16[2,2,1,24,128]{4,3,2,1,0:T(8,128)(2,1)S(1)}, bf16[2,2,1,24,128]{4,3,2,1,0:T(8,128)(2,1)S(1)}, u32[]{:S(2)}, u32[]{:S(2)}) %collective-permute-start.3) | collective-permute-done | bytes 24608 | tf_op jit(solution)/shard_map/ppermute | solution.py:32
  32.5 4.9 %collective-permute-start.4 = (bf16[1,384,128]{2,1,0:T(8,128)(2,1)S(1)}, bf16[1,384,128]{2,1,0:T(8,128)(2,1)S(1)}, u32[]{:S(2)}, u32[]{:S(2)}) collective-permute-start(bf16[1,384,128]{2,1,0:T(8,128)(2,1)S(1)} %bitcast.159), channel_id=1, source_target_pairs={{0,1},{1,0},{2,3},{3,2},{4,5},{5,4},{6,7},{7,6},{8,9},{9,8},{10,11... | collective-permute-start | bytes 294920 | tf_op jit(solution)/shard_map/ppermute | solution.py:32
  37.6 0.2 multiply_reduce_fusion
  37.8 0.2 multiply_convert_fusion
  38.0 0.5 fusion.5
  38.5 0.5 fusion.8
  39.0 0.4 fusion.17
  39.4 0.4 fusion.18
  40.0 1.2 reshape.259
  41.2 10.4 %all-to-all-start.1 = ((bf16[128,2,2304]{2,1,0:T(2,128)(2,1)}), bf16[128,2,2304]{2,1,0:T(2,128)(2,1)S(1)}, u32[]{:S(2)}, u32[]{:S(2)}) async-start(bf16[128,2,2304]{2,1,0:T(2,128)(2,1)} %reshape.259), calls=%async_computation.1 | async-start | bytes 2359296 | tf_op jit(solution)/shard_map/all_to_all | solution.py:27
  51.7 1.6 %collective-permute-start.5 = (bf16[2,1,1,192,128]{4,3,2,1,0:T(8,128)(2,1)S(1)}, bf16[2,1,1,192,128]{4,3,2,1,0:T(8,128)(2,1)S(1)}, u32[]{:S(2)}, u32[]{:S(2)}) collective-permute-start(bf16[2,1,1,192,128]{4,3,2,1,0:T(8,128)(2,1)S(1)} %get-tuple-element.35), channel_id=1, source_target_pairs={{0,2},{2,0},{4,6},{6,4},{1,3},{3,1},{5,7},{7,5},{8,10},{10,8},{12,... | collective-permute-start | bytes 294920 | tf_op jit(solution)/shard_map/ppermute | solution.py:32
  53.3 0.6 collective-permute-start.7
  54.0 5.6 %collective-permute-done.5 = bf16[2,1,1,192,128]{4,3,2,1,0:T(8,128)(2,1)S(1)} collective-permute-done((bf16[2,1,1,192,128]{4,3,2,1,0:T(8,128)(2,1)S(1)}, bf16[2,1,1,192,128]{4,3,2,1,0:T(8,128)(2,1)S(1)}, u32[]{:S(2)}, u32[]{:S(2)}) %collective-permute-start.5) | collective-permute-done | bytes 98336 | tf_op jit(solution)/shard_map/ppermute | solution.py:32
  59.6 3.1 %collective-permute-start.6 = (bf16[2,1,2,192,128]{4,3,2,1,0:T(8,128)(2,1)S(1)}, bf16[2,1,2,192,128]{4,3,2,1,0:T(8,128)(2,1)S(1)}, u32[]{:S(2)}, u32[]{:S(2)}) collective-permute-start(bf16[2,1,2,192,128]{4,3,2,1,0:T(8,128)(2,1)S(1)} %pad_maximum_fusion.9), channel_id=1, source_target_pairs={{0,4},{2,6},{4,0},{6,2},{1,5},{3,7},{5,1},{7,3},{8,12},{10,14},{12... | collective-permute-start | bytes 589832 | tf_op jit(solution)/shard_map/ppermute | solution.py:32
  62.7 0.9 collective-permute-start.8
  63.6 5.1 %collective-permute-done.6 = bf16[2,1,2,192,128]{4,3,2,1,0:T(8,128)(2,1)S(1)} collective-permute-done((bf16[2,1,2,192,128]{4,3,2,1,0:T(8,128)(2,1)S(1)}, bf16[2,1,2,192,128]{4,3,2,1,0:T(8,128)(2,1)S(1)}, u32[]{:S(2)}, u32[]{:S(2)}) %collective-permute-start.6) | collective-permute-done | bytes 196640 | tf_op jit(solution)/shard_map/ppermute | solution.py:32
  68.9 1.3 collective-permute-done.8
  70.2 0.8 pad_maximum_fusion.8
  71.0 1.9 %collective-permute-start.9 = (bf16[2,2,2,2,2,2,1,1,24,128]{9,8,7,6,5,4,3,2,1,0:T(8,128)(2,1)}, bf16[2,2,2,2,2,2,1,1,24,128]{9,8,7,6,5,4,3,2,1,0:T(8,128)(2,1)}, u32[]{:S(2)}, u32[]{:S(2)}) collective-permute-start(bf16[2,2,2,2,2,2,1,1,24,128]{9,8,7,6,5,4,3,2,1,0:T(8,128)(2,1)} %pad_maximum_fusion.8), channel_id=1, source_target_pairs={{0,16},{16,0},{32,48},{48,32},{1,17},{17,1},{33,49},{49,33},{2,18}... | collective-permute-start | bytes 1179656 | tf_op jit(solution)/shard_map/ppermute | solution.py:32
  73.0 0.2 copy.118
  73.1 10.1 %all-to-all-done.1 = bf16[128,2,2304]{2,1,0:T(2,128)(2,1)S(1)} async-done(((bf16[128,2,2304]{2,1,0:T(2,128)(2,1)}), bf16[128,2,2304]{2,1,0:T(2,128)(2,1)S(1)}, u32[]{:S(2)}, u32[]{:S(2)}) %all-to-all-start.1) | async-done | bytes 1179680 | tf_op jit(solution)/shard_map/all_to_all | solution.py:27
  83.3 0.8 fusion.94
  84.4 1.1 broadcast_select_fusion.3
  85.4 1.0 pad_maximum_fusion.3
  86.4 0.5 collective-permute-start.10
  87.0 0.3 select_bitcast_fusion.1
  87.4 0.1 pad_maximum_fusion.2
  87.5 0.7 convolution_convert_fusion
  88.2 0.9 reshape.266
  89.2 11.0 %all-to-all-start.2 = ((bf16[128,2,1152]{2,1,0:T(2,128)(2,1)}), bf16[128,2,1152]{2,1,0:T(2,128)(2,1)S(1)}, u32[]{:S(2)}, u32[]{:S(2)}) async-start(bf16[128,2,1152]{2,1,0:T(2,128)(2,1)} %reshape.266), calls=%async_computation.2 | async-start | bytes 1179648 | tf_op jit(solution)/shard_map/all_to_all | solution.py:27
  100.2 0.2 fusion.36
  100.4 1.5 %fusion.11 = f32[2304,128]{0,1:T(8,128)} fusion(bf16[128,2304]{1,0:T(8,128)(2,1)S(1)} %fusion.36, bf16[128,128]{1,0:T(8,128)(2,1)S(1)} %copy-done.12), kind=kOutput, calls=%fused_computation.17 | convolution fusion | flops 76382208 | bytes 1802240 | tf_op jit(solution)/shard_map/cp,cd->dp/dot_general | solution.py:148
  102.0 1.3 broadcast_select_fusion.1
  103.2 0.1 pad_maximum_fusion
  103.4 19.2 %all-to-all-done.2 = bf16[128,2,1152]{2,1,0:T(2,128)(2,1)S(1)} async-done(((bf16[128,2,1152]{2,1,0:T(2,128)(2,1)}), bf16[128,2,1152]{2,1,0:T(2,128)(2,1)S(1)}, u32[]{:S(2)}, u32[]{:S(2)}) %all-to-all-start.2) | async-done | bytes 589856 | tf_op jit(solution)/shard_map/all_to_all | solution.py:27
  122.7 0.2 fusion.31
  122.9 0.9 copy-done.1
  123.8 0.4 convert_reduce_fusion
  124.3 0.2 fusion.28
  124.5 0.3 convolution_bitcast_fusion
  124.8 0.5 fusion.44
  125.3 0.2 fusion.101
  125.6 0.7 fusion.19
  126.4 0.2 convolution_convert_fusion.4
  126.8 24.6 %all_to_all.20 = bf16[8,16,2432]{2,1,0:T(8,128)(2,1)S(1)} all-to-all(bf16[8,16,2432]{2,1,0:T(8,128)(2,1)S(1)} %fusion.51), channel_id=1, replica_groups=mesh['x'=4,'zl'=4,'core'=2,'y'=4,'zh'=2] {'y','zh'}, dimensions={0} | all-to-all | bytes 1245184 | tf_op jit(solution)/shard_map/all_to_all | solution.py:27
  151.4 0.2 copy.159
  151.6 0.6 copy.162
  152.2 0.9 pad_maximum_fusion.6
  (110 shorter events, 2.6 us)
Async XLA Ops:
  0.6 12.9 %copy-start = (bf16[384,48]{0,1:T(8,128)(2,1)S(1)}, bf16[384,48]{0,1:T(8,128)(2,1)}, u32[]{:S(2)}) copy-start(bf16[384,48]{0,1:T(8,128)(2,1)} %param.27) | copy-start | bytes 110596
  1.9 11.3 %copy-start.3 = (bf16[24,384]{1,0:T(8,128)(2,1)S(1)}, bf16[24,384]{1,0:T(8,128)(2,1)}, u32[]{:S(2)}) copy-start(bf16[24,384]{1,0:T(8,128)(2,1)} %param.16) | copy-start | bytes 55300
  2.0 11.6 %copy-start.13 = (f32[384]{0:T(512)S(1)}, f32[384]{0:T(512)}, u32[]{:S(2)}) copy-start(f32[384]{0:T(512)} %param.25) | copy-start | bytes 4612
  2.0 11.8 %copy-start.10 = (bf16[384,2,48]{0,2,1:T(8,128)(2,1)S(1)}, bf16[384,2,48]{0,2,1:T(8,128)(2,1)}, u32[]{:S(2)}) copy-start(bf16[384,2,48]{0,2,1:T(8,128)(2,1)} %param.28) | copy-start | bytes 221188
  2.0 15.8 %copy-start.2 = (bf16[128,4,128]{2,1,0:T(4,128)(2,1)S(1)}, bf16[128,4,128]{2,1,0:T(4,128)(2,1)}, u32[]{:S(2)}) copy-start(bf16[128,4,128]{2,1,0:T(4,128)(2,1)} %param.19) | copy-start | bytes 393220
  2.8 15.2 %copy-start.11 = (bf16[384,48]{0,1:T(8,128)(2,1)S(1)}, bf16[384,48]{0,1:T(8,128)(2,1)}, u32[]{:S(2)}) copy-start(bf16[384,48]{0,1:T(8,128)(2,1)} %param.26) | copy-start | bytes 110596
  2.8 15.4 %copy-start.6 = (s32[768]{0:T(1024)S(1)}, s32[768]{0:T(1024)}, u32[]{:S(2)}) copy-start(s32[768]{0:T(1024)} %param.17) | copy-start | bytes 9220
  2.9 24.5 %copy-start.8 = (f32[128]{0:T(128)S(1)}, f32[128]{0:T(128)}, u32[]{:S(2)}) copy-start(f32[128]{0:T(128)} %param.18) | copy-start | bytes 1540
  2.9 29.6 %copy-start.4 = (bf16[48,384]{1,0:T(8,128)(2,1)S(1)}, bf16[48,384]{1,0:T(8,128)(2,1)}, u32[]{:S(2)}) copy-start(bf16[48,384]{1,0:T(8,128)(2,1)} %param.29) | copy-start | bytes 110596
  2.9 34.6 %all-to-all-start = ((bf16[8,16,2304]{2,1,0:T(8,128)(2,1)}), bf16[8,16,2304]{2,1,0:T(8,128)(2,1)S(1)}, u32[]{:S(2)}, u32[]{:S(2)}) async-start(bf16[8,16,2304]{2,1,0:T(8,128)(2,1)} %maximum_bitcast_fusion), calls=%async_computation | async-start | bytes 1179648 | tf_op jit(solution)/shard_map/all_to_all | solution.py:27
  14.0 6.3 %collective-permute-start.1 = (bf16[1,1,1,24,128]{4,3,2,1,0:T(8,128)(2,1)S(1)}, bf16[1,1,1,24,128]{4,3,2,1,0:T(8,128)(2,1)S(1)}, u32[]{:S(2)}, u32[]{:S(2)}) collective-permute-start(bf16[1,1,1,24,128]{4,3,2,1,0:T(8,128)(2,1)S(1)} %fusion.87), channel_id=1, source_target_pairs={{0,4},{2,6},{4,0},{6,2},{1,5},{3,7},{5,1},{7,3},{8,12},{10,14},{12... | collective-permute-start | bytes 18440 | tf_op jit(solution)/shard_map/ppermute | solution.py:32
  20.4 5.3 %collective-permute-start.2 = (bf16[2,1,1,24,128]{4,3,2,1,0:T(8,128)(2,1)S(1)}, bf16[2,1,1,24,128]{4,3,2,1,0:T(8,128)(2,1)S(1)}, u32[]{:S(2)}, u32[]{:S(2)}) collective-permute-start(bf16[2,1,1,24,128]{4,3,2,1,0:T(8,128)(2,1)S(1)} %pad_maximum_fusion.14), channel_id=1, source_target_pairs={{0,128},{64,192},{128,0},{192,64},{1,129},{65,193},{129,1},{193,65... | collective-permute-start | bytes 36872 | tf_op jit(solution)/shard_map/ppermute | solution.py:32
  25.7 6.6 %collective-permute-start.3 = (bf16[2,2,1,24,128]{4,3,2,1,0:T(8,128)(2,1)S(1)}, bf16[2,2,1,24,128]{4,3,2,1,0:T(8,128)(2,1)S(1)}, u32[]{:S(2)}, u32[]{:S(2)}) collective-permute-start(bf16[2,2,1,24,128]{4,3,2,1,0:T(8,128)(2,1)S(1)} %pad_maximum_fusion.13), channel_id=1, source_target_pairs={{0,32},{16,48},{32,0},{48,16},{1,33},{17,49},{33,1},{49,17},{2,34}... | collective-permute-start | bytes 73736 | tf_op jit(solution)/shard_map/ppermute | solution.py:32
  32.5 19.1 %collective-permute-start.4 = (bf16[1,384,128]{2,1,0:T(8,128)(2,1)S(1)}, bf16[1,384,128]{2,1,0:T(8,128)(2,1)S(1)}, u32[]{:S(2)}, u32[]{:S(2)}) collective-permute-start(bf16[1,384,128]{2,1,0:T(8,128)(2,1)S(1)} %bitcast.159), channel_id=1, source_target_pairs={{0,1},{1,0},{2,3},{3,2},{4,5},{5,4},{6,7},{7,6},{8,9},{9,8},{10,11... | collective-permute-start | bytes 294920 | tf_op jit(solution)/shard_map/ppermute | solution.py:32
  41.2 12.1 %copy-start.7 = (bf16[128,16]{0,1:T(8,128)(2,1)S(1)}, bf16[128,16]{0,1:T(8,128)(2,1)}, u32[]{:S(2)}) copy-start(bf16[128,16]{0,1:T(8,128)(2,1)} %param.24) | copy-start | bytes 12292
  41.2 42.1 %all-to-all-start.1 = ((bf16[128,2,2304]{2,1,0:T(2,128)(2,1)}), bf16[128,2,2304]{2,1,0:T(2,128)(2,1)S(1)}, u32[]{:S(2)}, u32[]{:S(2)}) async-start(bf16[128,2,2304]{2,1,0:T(2,128)(2,1)} %reshape.259), calls=%async_computation.1 | async-start | bytes 2359296 | tf_op jit(solution)/shard_map/all_to_all | solution.py:27
  51.7 7.8 %collective-permute-start.5 = (bf16[2,1,1,192,128]{4,3,2,1,0:T(8,128)(2,1)S(1)}, bf16[2,1,1,192,128]{4,3,2,1,0:T(8,128)(2,1)S(1)}, u32[]{:S(2)}, u32[]{:S(2)}) collective-permute-start(bf16[2,1,1,192,128]{4,3,2,1,0:T(8,128)(2,1)S(1)} %get-tuple-element.35), channel_id=1, source_target_pairs={{0,2},{2,0},{4,6},{6,4},{1,3},{3,1},{5,7},{7,5},{8,10},{10,8},{12,... | collective-permute-start | bytes 294920 | tf_op jit(solution)/shard_map/ppermute | solution.py:32
  53.3 9.4 %collective-permute-start.7 = (bf16[2,2,1,2,1,2,1,1,24,128]{9,8,7,6,5,4,3,2,1,0:T(8,128)(2,1)S(1)}, bf16[2,2,1,2,1,2,1,1,24,128]{9,8,7,6,5,4,3,2,1,0:T(8,128)(2,1)S(1)}, u32[]{:S(2)}, u32[]{:S(2)}) collective-permute-start(bf16[2,2,1,2,1,2,1,1,24,128]{9,8,7,6,5,4,3,2,1,0:T(8,128)(2,1)S(1)} %bitcast.157), channel_id=1, source_target_pairs={{0,2},{2,0},{4,6},{6,4},{1,3},{3,1},{5,7},{7,5},{8,10},{10,8},{12,... | collective-permute-start | bytes 294920 | tf_op jit(solution)/shard_map/ppermute | solution.py:32
  59.6 9.1 %collective-permute-start.6 = (bf16[2,1,2,192,128]{4,3,2,1,0:T(8,128)(2,1)S(1)}, bf16[2,1,2,192,128]{4,3,2,1,0:T(8,128)(2,1)S(1)}, u32[]{:S(2)}, u32[]{:S(2)}) collective-permute-start(bf16[2,1,2,192,128]{4,3,2,1,0:T(8,128)(2,1)S(1)} %pad_maximum_fusion.9), channel_id=1, source_target_pairs={{0,4},{2,6},{4,0},{6,2},{1,5},{3,7},{5,1},{7,3},{8,12},{10,14},{12... | collective-permute-start | bytes 589832 | tf_op jit(solution)/shard_map/ppermute | solution.py:32
  62.7 7.5 %collective-permute-start.8 = (bf16[2,2,2,2,1,2,1,1,24,128]{9,8,7,6,5,4,3,2,1,0:T(8,128)(2,1)S(1)}, bf16[2,2,2,2,1,2,1,1,24,128]{9,8,7,6,5,4,3,2,1,0:T(8,128)(2,1)S(1)}, u32[]{:S(2)}, u32[]{:S(2)}) collective-permute-start(bf16[2,2,2,2,1,2,1,1,24,128]{9,8,7,6,5,4,3,2,1,0:T(8,128)(2,1)S(1)} %pad_maximum_fusion.10), channel_id=1, source_target_pairs={{0,64},{64,0},{128,192},{192,128},{1,65},{65,1},{129,193},{193,129... | collective-permute-start | bytes 589832 | tf_op jit(solution)/shard_map/ppermute | solution.py:32
  71.0 13.3 %collective-permute-start.9 = (bf16[2,2,2,2,2,2,1,1,24,128]{9,8,7,6,5,4,3,2,1,0:T(8,128)(2,1)}, bf16[2,2,2,2,2,2,1,1,24,128]{9,8,7,6,5,4,3,2,1,0:T(8,128)(2,1)}, u32[]{:S(2)}, u32[]{:S(2)}) collective-permute-start(bf16[2,2,2,2,2,2,1,1,24,128]{9,8,7,6,5,4,3,2,1,0:T(8,128)(2,1)} %pad_maximum_fusion.8), channel_id=1, source_target_pairs={{0,16},{16,0},{32,48},{48,32},{1,17},{17,1},{33,49},{49,33},{2,18}... | collective-permute-start | bytes 1179656 | tf_op jit(solution)/shard_map/ppermute | solution.py:32
  84.2 2.8 %collective-permute-start = (bf16[16,24,768]{2,1,0:T(8,128)(2,1)S(1)}, bf16[16,24,768]{2,1,0:T(8,128)(2,1)S(1)}, u32[]{:S(2)}, u32[]{:S(2)}) collective-permute-start(bf16[16,24,768]{2,1,0:T(8,128)(2,1)S(1)} %pad_maximum_fusion.4), channel_id=1, source_target_pairs={{0,8},{8,0},{1,9},{9,1},{2,10},{10,2},{3,11},{11,3},{4,12},{12,4},... | collective-permute-start | bytes 1769480 | tf_op jit(solution)/shard_map/ppermute | solution.py:126
  86.4 15.6 %collective-permute-start.10 = (bf16[2,2,2,2,2,2,2,1,24,128]{9,8,7,6,5,4,3,2,1,0:T(8,128)(2,1)}, bf16[2,2,2,2,2,2,2,1,24,128]{9,8,7,6,5,4,3,2,1,0:T(8,128)(2,1)}, u32[]{:S(2)}, u32[]{:S(2)}) collective-permute-start(bf16[2,2,2,2,2,2,2,1,24,128]{9,8,7,6,5,4,3,2,1,0:T(8,128)(2,1)} %pad_maximum_fusion.3), channel_id=1, source_target_pairs={{0,8},{8,0},{1,9},{9,1},{2,10},{10,2},{3,11},{11,3},{4,12},{12,4},... | collective-permute-start | bytes 2359304 | tf_op jit(solution)/shard_map/ppermute | solution.py:32
  89.2 11.2 %copy-start.12 = (bf16[128,128]{1,0:T(8,128)(2,1)S(1)}, bf16[128,128]{1,0:T(8,128)(2,1)}, u32[]{:S(2)}) copy-start(bf16[128,128]{1,0:T(8,128)(2,1)} %param.20) | copy-start | bytes 98308
  89.2 33.4 %all-to-all-start.2 = ((bf16[128,2,1152]{2,1,0:T(2,128)(2,1)}), bf16[128,2,1152]{2,1,0:T(2,128)(2,1)S(1)}, u32[]{:S(2)}, u32[]{:S(2)}) async-start(bf16[128,2,1152]{2,1,0:T(2,128)(2,1)} %reshape.266), calls=%async_computation.2 | async-start | bytes 1179648 | tf_op jit(solution)/shard_map/all_to_all | solution.py:27
  122.5 1.3 copy-start.1
  122.5 1.3 copy-start.5
  122.5 1.3 copy-start.9
  123.8 0.7 copy-start.14
